TPU v7x, 32 devices: a whole 2x2x4 slice. The times are simulated.
32 devices in a mesh: groups: 1, ep: 32 (over z, y, x, core).
Axes of the slice: x: 2, y: 2, z: 4, core: 2. Of those that a mesh axis runs over, the one named last changes fastest.
Arguments:
- tokens: bfloat16 [2048, 2880], P(('groups', 'ep')), may hold values from -6 to 6
- routes: int32 [2048, 4], P(('groups', 'ep')), may hold values from 0 to 7, all different within a row; in each aligned block of 64 rows (0 to 63, 64 to 127, ...) at most 36 rows name the same one
- norm_gain: bfloat16 [2880], replicated, may hold values from 0.25 to 1.75
- router_weight: bfloat16 [2880, 8], replicated, may hold values from -0.02734375 to 0.02734375
- gate_up_weight: bfloat16 [32, 2880, 720], P('ep'), may hold values from -0.109375 to 0.109375
- down_weight: bfloat16 [32, 360, 2880], P('ep'), may hold values from -0.15625 to 0.15625
Outputs:
- mixed: bfloat16 [2048, 2880], P(('groups', 'ep'))
Inputs may be any that keep to these rules, and one draw needn't show every extreme that they name: `routes`: in each aligned block of 64 rows (the rows of one device), no expert is named by more than 36 rows; in some blocks one expert is named by exactly 36 rows. A row names 4 different experts.
All inputs are finite; a program needn't handle non-finite values.
Results may differ from a plain program's by a relative error of at most 0.005.
Values may be sent and summed in bfloat16 or wider, within the bound.
No kernel may reach another device: no remote copies, remote signals or barrier semaphores. Data moves between devices by JAX's collectives and lax.ppermute only.
A program may use at most 128 MiB of HBM per device.

v0:
```python
import jax
import jax.numpy as jnp
from jax import lax
from jax.sharding import PartitionSpec as P


def shards(tokens, routes, norm_gain, router_weight, gate_up_weight, down_weight):
    tok_rows = tokens.shape[0]
    model_width = tokens.shape[1]
    top_count = routes.shape[1]
    experts = router_weight.shape[1]
    devices = lax.axis_size("ep")
    shard_count = devices // experts
    ff_dev = down_weight.shape[1]
    capacity = min(
        tok_rows, shard_count * (17 * tok_rows * top_count // (16 * experts * shard_count) + 1)
    )
    stream = tokens.astype(jnp.float32)
    mean_square = jnp.mean(stream * stream, axis=-1, keepdims=True)
    normed = (stream * lax.rsqrt(mean_square + 1e-05) * norm_gain.astype(jnp.float32)).astype(
        jnp.bfloat16
    )
    logits = jnp.dot(normed, router_weight, preferred_element_type=jnp.float32)
    expert_ids = lax.broadcasted_iota(jnp.int32, (1, 1, experts), 2)
    onehot = routes[:, :, None] == expert_ids
    chosen = jnp.sum(jnp.where(onehot, logits[:, None, :], jnp.float32(0.0)), axis=-1)
    expo = jnp.exp(chosen)
    route_prob = expo / jnp.sum(expo, axis=-1, keepdims=True)
    flat_hits = onehot.astype(jnp.int32).reshape(tok_rows * top_count, experts)
    rank_before = jnp.cumsum(flat_hits, axis=0) - flat_hits
    slot_index = jnp.sum(flat_hits * rank_before, axis=1)
    position = routes.reshape(-1) * capacity + slot_index
    slot_iota = lax.broadcasted_iota(jnp.int32, (1, experts * capacity), 1)
    placement = position[:, None] == slot_iota
    selector = (
        placement.astype(jnp.bfloat16).reshape(tok_rows, top_count, experts * capacity).sum(axis=1)
    )
    combine_weight = jnp.where(placement, route_prob.reshape(-1)[:, None], jnp.float32(0.0))
    combine_weight = combine_weight.reshape(tok_rows, top_count, experts * capacity).sum(axis=1)
    buffer = jnp.einsum("te,td->ed", selector, normed, preferred_element_type=jnp.float32).astype(
        jnp.bfloat16
    )
    buffer = buffer.reshape(experts, capacity, model_width)
    outgoing = jnp.broadcast_to(buffer[:, None], (experts, shard_count, capacity, model_width))
    outgoing = outgoing.reshape(devices, capacity, model_width)
    received = lax.all_to_all(outgoing, "ep", split_axis=0, concat_axis=0, tiled=True)
    rows_in = received.reshape(devices * capacity, model_width)
    hidden = jnp.dot(rows_in, gate_up_weight[0], preferred_element_type=jnp.float32)
    gate_part = hidden[:, :ff_dev]
    up_part = hidden[:, ff_dev:]
    activated = ((up_part + 1.0) * gate_part * jax.nn.sigmoid(1.702 * gate_part)).astype(
        jnp.bfloat16
    )
    partial_value = jnp.dot(activated, down_weight[0], preferred_element_type=jnp.float32).astype(
        jnp.bfloat16
    )
    partial_value = partial_value.reshape(devices, capacity, model_width)
    returned = lax.all_to_all(partial_value, "ep", split_axis=0, concat_axis=0, tiled=True)
    expert_sum = (
        returned.astype(jnp.float32)
        .reshape(experts, shard_count, capacity, model_width)
        .sum(axis=1)
    )
    expert_sum = expert_sum.reshape(experts * capacity, model_width)
    mixture = jnp.dot(
        combine_weight,
        expert_sum,
        precision=lax.Precision.HIGHEST,
        preferred_element_type=jnp.float32,
    )
    return (stream + mixture).astype(jnp.bfloat16)


def solution(mesh):
    in_specs = (
        P(("groups", "ep"), None),
        P(("groups", "ep"), None),
        P(),
        P(),
        P("ep", None, None),
        P("ep", None, None),
    )
    out_specs = P(("groups", "ep"), None)
    return jax.shard_map(shards, mesh=mesh, in_specs=in_specs, out_specs=out_specs, check_vma=False)
```

profile of v0, /device:TPU:13, one launch (start us, length us, event | category | flops | bytes accessed | tf_op | source)
XLA Modules:
  0.0 410.6 jit_solution(18121460770090798714)
XLA Ops:
  0.0 0.0 copy-start
  0.0 0.9 copy.23
  0.9 0.1 eq.51
  1.0 0.1 eq.47
  1.1 1.2 fusion.10
  2.3 0.7 convert_element_type.39
  3.0 0.6 reduce-window.6
  3.6 0.2 slice_reduce_fusion
  3.9 0.1 fusion.19
  4.0 0.1 reduce_sum.69
  4.1 0.1 copy.25
  4.1 0.7 multiply_add_fusion
  4.8 0.1 fusion.14
  5.0 2.8 convolution_convert_fusion.1
  7.8 2.6 broadcast_in_dim.41
  10.4 2.0 broadcast_in_dim.42
  12.5 170.9 %all_to_all.10 = bf16[32,36,2880]{2,1,0:T(8,128)(2,1)} all-to-all(bf16[32,36,2880]{2,1,0:T(8,128)(2,1)S(1)} %bitcast.23), channel_id=1, replica_groups=mesh['groups'=1,'ep'=32] {'ep'}, dimensions={0} | all-to-all | bytes 13271040 | tf_op jit(solution)/shard_map/all_to_all | solution.py:46
  183.4 9.3 %reshape.92 = bf16[1152,2880]{1,0:T(8,128)(2,1)} reshape(bf16[32,36,2880]{2,1,0:T(8,128)(2,1)} %all_to_all.10) | data formatting | bytes 13271040 | tf_op jit(solution)/shard_map/reshape | solution.py:47
  192.7 9.7 %fusion = f32[1152,720]{0,1:T(8,128)S(1)} fusion(bf16[1152,2880]{1,0:T(8,128)(2,1)} %reshape.92, bf16[1,2880,720]{1,2,0:T(8,128)(2,1)} %param.10), kind=kOutput, calls=%fused_computation.2 | convolution fusion | flops 4777574400 | bytes 14100480 | tf_op jit(solution)/shard_map/dot_general | solution.py:48
  202.4 0.0 copy-done
  202.4 6.3 %convolution_convert_fusion = bf16[1152,2880]{0,1:T(8,128)(2,1)} fusion(bf16[1,360,2880]{2,1,0:T(8,128)(2,1)S(1)} %copy-done, f32[1152,720]{0,1:T(8,128)S(1)} %fusion), kind=kOutput, calls=%fused_computation.1 | convolution fusion | flops 2395422720 | bytes 12026880 | tf_op jit(solution)/shard_map/dot_general | solution.py:54
  208.7 10.1 %copy.26 = bf16[1152,2880]{1,0:T(8,128)(2,1)} copy(bf16[1152,2880]{0,1:T(8,128)(2,1)} %convolution_convert_fusion) | data formatting | bytes 13271040 | tf_op jit(solution)/shard_map/convert_element_type | solution.py:54
  218.8 8.7 %reshape.93 = bf16[32,36,2880]{2,1,0:T(8,128)(2,1)} reshape(bf16[1152,2880]{1,0:T(8,128)(2,1)} %copy.26) | data formatting | bytes 13271040 | tf_op jit(solution)/shard_map/reshape | solution.py:57
  227.5 0.0 copy-start.2
  227.5 0.0 copy-start.4
  227.5 0.0 copy-start.3
  227.5 5.7 %all-to-all-start.1 = ((bf16[32,36,2880]{2,1,0:T(8,128)(2,1)}), bf16[32,36,2880]{2,1,0:T(8,128)(2,1)}, u32[]{:S(2)}, u32[]{:S(2)}) async-start(bf16[32,36,2880]{2,1,0:T(8,128)(2,1)} %reshape.93), calls=%async_computation.1 | async-start | bytes 15073280 | tf_op jit(solution)/shard_map/all_to_all | solution.py:58
  233.2 0.0 copy-done.2
  233.2 0.0 copy-done.4
  233.2 0.3 fusion.16
  233.5 0.0 copy-done.3
  233.6 0.1 select_reduce_fusion
  233.7 161.6 %all-to-all-done.1 = bf16[32,36,2880]{2,1,0:T(8,128)(2,1)} async-done(((bf16[32,36,2880]{2,1,0:T(8,128)(2,1)}), bf16[32,36,2880]{2,1,0:T(8,128)(2,1)}, u32[]{:S(2)}, u32[]{:S(2)}) %all-to-all-start.1) | async-done | bytes 6635552 | tf_op jit(solution)/shard_map/all_to_all | solution.py:58
  395.3 6.7 %convert_reduce_fusion = f32[8,36,2880]{2,1,0:T(8,128)} fusion(bf16[32,36,2880]{2,1,0:T(8,128)(2,1)} %all-to-all-done.1), kind=kLoop, calls=%fused_computation | loop fusion | flops 5806080 | bytes 9953280 | tf_op jit(solution)/shard_map/reduce_sum | solution.py:62
  402.0 0.0 copy-start.1
  402.0 3.6 reshape.96
  405.6 5.0 %fusion.2 = bf16[64,2880]{1,0:T(8,128)(2,1)} fusion(f32[64,288]{1,0:T(8,128)S(1)} %select_reduce_fusion, f32[288,2880]{1,0:T(8,128)} %reshape.96, bf16[64,2880]{1,0:T(8,128)(2,1)S(1)} %copy-done.2), kind=kOutput, calls=%fused_computation.6 | convolution fusion | flops 637562880 | bytes 4128768 | tf_op jit(solution)/shard_map/dot_general | solution.py:65
  410.6 0.0 copy-done.1
  (7 shorter events, 0.1 us)
Async XLA Ops:
  0.0 202.4 %copy-start = (bf16[1,360,2880]{2,1,0:T(8,128)(2,1)S(1)}, bf16[1,360,2880]{2,1,0:T(8,128)(2,1)}, u32[]{:S(2)}) copy-start(bf16[1,360,2880]{2,1,0:T(8,128)(2,1)} %param.11) | copy-start | bytes 6220804
  227.5 5.7 %copy-start.2 = (bf16[64,2880]{1,0:T(8,128)(2,1)S(1)}, bf16[64,2880]{1,0:T(8,128)(2,1)}, u32[]{:S(2)}) copy-start(bf16[64,2880]{1,0:T(8,128)(2,1)} %param.6) | copy-start | bytes 1105924
  227.5 5.7 %copy-start.4 = (bf16[2880,8]{0,1:T(8,128)(2,1)S(1)}, bf16[2880,8]{0,1:T(8,128)(2,1)}, u32[]{:S(2)}) copy-start(bf16[2880,8]{0,1:T(8,128)(2,1)} %param.9) | copy-start | bytes 138244
  227.5 6.0 %copy-start.3 = (s32[64,4]{0,1:T(4,128)S(1)}, s32[64,4]{0,1:T(4,128)}, u32[]{:S(2)}) copy-start(s32[64,4]{0,1:T(4,128)} %param.7) | copy-start | bytes 3076
  227.5 167.9 %all-to-all-start.1 = ((bf16[32,36,2880]{2,1,0:T(8,128)(2,1)}), bf16[32,36,2880]{2,1,0:T(8,128)(2,1)}, u32[]{:S(2)}, u32[]{:S(2)}) async-start(bf16[32,36,2880]{2,1,0:T(8,128)(2,1)} %reshape.93), calls=%async_computation.1 | async-start | bytes 15073280 | tf_op jit(solution)/shard_map/all_to_all | solution.py:58
  402.0 8.6 %copy-start.1 = (bf16[1,360,2880]{2,1,0:T(8,128)(2,1)S(1)}, bf16[1,360,2880]{2,1,0:T(8,128)(2,1)}, u32[]{:S(2)}) copy-start(bf16[1,360,2880]{2,1,0:T(8,128)(2,1)} %param.11) | copy-start | bytes 6220804
where the time goes:
time: 418 us; the launch traced here: 411 us
  blocking collectives  171 us (41%)
  waiting for transfers between devices  162 us (39%)
  local copies, waits for them, and re-layouts  37.9 us (9%)
  matrix products  24.1 us (6%)
  other arithmetic  10.2 us (2%)
  starting transfers between devices  5.72 us (1%)
    all_to_all x1, blocking collectives, shards(): lax.all_to_all(outgoing, 'ep', split_axis=0, concat_axis=0, tiled=True)  171 us
    all_to_all x1, waiting for transfers between devices, shards(): lax.all_to_all(partial_value, 'ep', split_axis=0, concat_axis=0, tiled=True)  162 us
    convert_element_type x1, local copies, waits for them, and re-layouts, shards(): jnp.dot(activated, down_weight[0], preferred_element_type=jnp.float32)  10.1 us
    dot_general x1, matrix products, shards(): jnp.dot(rows_in, gate_up_weight[0], preferred_element_type=jnp.float32)  9.7 us
    reshape x1, local copies, waits for them, and re-layouts, shards(): rows_in = received.reshape(devices * capacity, model_width)  9.31 us
    reshape x1, local copies, waits for them, and re-layouts, shards(): partial_value = partial_value.reshape(devices, capacity, model_width)  8.71 us
  transfers between devices with their start and end apart: 1, of which 1 were waited for; matrix products, arithmetic and copies ran while one was open for 0% of the time, Pallas kernels for 0%

commit v1 on v0

v1 whole, which is shorter than its diff:
```python
import functools

import jax
import jax.numpy as jnp
from jax import lax
from jax.experimental import pallas as pl
from jax.experimental.pallas import tpu as pltpu
from jax.sharding import PartitionSpec as P

CORES = 2
VMEM_BYTES = 48 * 1024 * 1024


def dot32(a, b, dims=((1,), (0,))):
    return lax.dot_general(a, b, (dims, ((), ())), preferred_element_type=jnp.float32)


def hits_of(routes, experts):
    ids = lax.broadcasted_iota(jnp.int32, (routes.shape[0], experts), 1)
    hits = (routes[:, 0:1] == ids).astype(jnp.float32)
    for k in range(1, routes.shape[1]):
        hits = hits + (routes[:, k : k + 1] == ids).astype(jnp.float32)
    return hits


def normed_of(tokens, gain):
    stream = tokens.astype(jnp.float32)
    mean_square = jnp.mean(stream * stream, axis=-1, keepdims=True)
    return (stream * lax.rsqrt(mean_square + 1e-05) * gain).astype(jnp.bfloat16)


def select_kernel(ids, own, other, routes_own, routes_other, gain, normed, *blocks, experts, cap):
    rows = own.shape[0]
    scale = gain[...].astype(jnp.float32)
    own_core = ids[len(blocks)]
    normed[0:rows, :] = normed_of(own[...], scale)
    normed[rows:, :] = normed_of(other[...], scale)
    before = (
        lax.broadcasted_iota(jnp.int32, (rows, rows), 0)
        < lax.broadcasted_iota(jnp.int32, (rows, rows), 1)
    ).astype(jnp.bfloat16)
    same = (
        lax.broadcasted_iota(jnp.int32, (rows, rows), 0)
        == lax.broadcasted_iota(jnp.int32, (rows, rows), 1)
    ).astype(jnp.bfloat16)
    parts = []
    for which, routes in enumerate((routes_own, routes_other)):
        hits = hits_of(routes[...], experts).astype(jnp.bfloat16)
        slot = dot32(hits, before, ((0,), (0,))).astype(jnp.int32)
        hit = dot32(hits, same, ((0,), (0,)))
        core = own_core if which == 0 else 1 - own_core
        parts.append((slot + core * cap, hit))
    place = jnp.concatenate([p[0] for p in parts], axis=1)
    hit = jnp.concatenate([p[1] for p in parts], axis=1)
    expert_row = lax.broadcasted_iota(jnp.int32, place.shape, 0)
    values = normed[...]
    slots = lax.broadcasted_iota(jnp.int32, (CORES * cap, CORES * rows), 0)
    for m, block in enumerate(blocks):
        mine = expert_row == ids[m]
        at = jnp.sum(jnp.where(mine & (hit > 0.5), place + 1, 0), axis=0, keepdims=True) - 1
        pick = (slots == at).astype(jnp.bfloat16)
        block[...] = dot32(pick, values).astype(jnp.bfloat16)


def weight_kernel(ids, normed, router, routes_own, routes_other, high, low, *, experts, cap):
    rows = routes_own.shape[0]
    count = high.shape[1] // (CORES * cap)
    own_core = ids[count]
    logits = dot32(normed[...], router[...])
    before = (
        lax.broadcasted_iota(jnp.int32, (rows, rows), 1)
        < lax.broadcasted_iota(jnp.int32, (rows, rows), 0)
    ).astype(jnp.bfloat16)
    for which, routes in enumerate((routes_own, routes_other)):
        hits = hits_of(routes[...], experts)
        slot = dot32(before, hits.astype(jnp.bfloat16)).astype(jnp.int32)
        core = own_core if which == 0 else 1 - own_core
        part = logits[which * rows : (which + 1) * rows, :]
        expo = jnp.where(hits > 0.5, jnp.exp(part), 0.0)
        prob = expo / jnp.sum(expo, axis=1, keepdims=True)
        column = lax.broadcasted_iota(jnp.int32, (rows, experts), 1)
        at_lane = lax.broadcasted_iota(jnp.int32, (rows, high.shape[1]), 1)
        total = jnp.zeros((rows, high.shape[1]), jnp.float32)
        for m in range(count):
            mine = column == ids[m]
            weight = jnp.sum(jnp.where(mine, prob, 0.0), axis=1, keepdims=True)
            at = jnp.sum(jnp.where(mine, slot, 0), axis=1, keepdims=True)
            at = at + core * cap + m * CORES * cap
            total = total + jnp.where(at_lane == at, weight, 0.0)
        first = total.astype(jnp.bfloat16)
        high[which * rows : (which + 1) * rows, :] = first
        low[which * rows : (which + 1) * rows, :] = (total - first.astype(jnp.float32)).astype(
            jnp.bfloat16
        )


def expert_kernel(a, b, c, d, gate_up, down, mine_a, mine_b, send, *, ff):
    rows = a.shape[0]
    values = jnp.concatenate([a[...], b[...], c[...], d[...]], axis=0)
    hidden = dot32(values, gate_up[...])
    gate = hidden[:, :ff]
    up = hidden[:, ff:]
    activated = ((up + 1.0) * gate * jax.nn.sigmoid(1.702 * gate)).astype(jnp.bfloat16)
    partial_value = dot32(activated, down[...]).astype(jnp.bfloat16)
    mine_a[...] = partial_value[0:rows]
    mine_b[...] = partial_value[rows : 2 * rows]
    send[...] = partial_value[2 * rows :]


def combine_kernel(high, low, *refs):
    mixed_own, mixed_other = refs[-2], refs[-1]
    values = jnp.concatenate([r[...] for r in refs[:-2]], axis=0)
    mixture = dot32(high[...], values) + dot32(low[...], values)
    rows = mixed_own.shape[0]
    mixed_own[...] = mixture[:rows]
    mixed_other[...] = mixture[rows:].astype(jnp.bfloat16)


def vmem_call(kernel, out_shape, name, scalars=0, count=0):
    specs = [pl.BlockSpec(memory_space=pltpu.SMEM)] * scalars
    specs = specs + [pl.BlockSpec(memory_space=pltpu.VMEM)] * (count - scalars)
    return pl.pallas_call(
        kernel,
        out_shape=out_shape,
        in_specs=specs,
        out_specs=jax.tree.map(lambda _: pl.BlockSpec(memory_space=pltpu.VMEM), out_shape),
        compiler_params=pltpu.CompilerParams(vmem_limit_bytes=VMEM_BYTES),
        name=name,
    )


def shards(tokens, routes, norm_gain, router_weight, gate_up_weight, down_weight):
    rows, width = tokens.shape
    top = routes.shape[1]
    experts = router_weight.shape[1]
    devices = lax.axis_size("ep")
    shard_count = devices // experts
    if shard_count != 2 * CORES or experts % CORES:
        raise ValueError("unsupported mesh")
    ff = down_weight.shape[1]
    cap = min(rows, shard_count * (17 * rows * top // (16 * experts * shard_count) + 1))
    chunks = experts // CORES
    pair = CORES * cap

    index = lax.axis_index("ep")
    core = index % CORES
    expert_high = index // (CORES * shard_count)
    ids = jnp.stack(
        [(expert_high ^ m) * CORES + core for m in range(chunks)] + [core]
    ).astype(jnp.int32)

    def split(i):
        e, s = divmod(i, shard_count)
        return e // CORES, e % CORES, s // CORES, s % CORES

    def join(high, e_low, x, c):
        return ((high * CORES + e_low) * 2 + x) * CORES + c

    far = []
    for m in range(chunks):
        pairs = []
        for i in range(devices):
            high, e_low, x, c = split(i)
            pairs.append((i, join(high ^ m, c, x, e_low)))
        far.append(pairs)
    to_core = [(i, i ^ 1) for i in range(devices)]
    to_x = [(i, i ^ CORES) for i in range(devices)]
    move = functools.partial(lax.ppermute, axis_name="ep")

    other = move(tokens, perm=to_core)
    routes_other = move(routes, perm=to_core)
    block = jax.ShapeDtypeStruct((pair, width), jnp.bfloat16)
    gain = norm_gain.reshape(1, width)
    normed, *blocks = vmem_call(
        functools.partial(select_kernel, experts=experts, cap=cap),
        [jax.ShapeDtypeStruct((CORES * rows, width), jnp.bfloat16)] + [block] * chunks,
        "select",
        1,
        6,
    )(ids, tokens, other, routes, routes_other, gain)

    near = [move(blocks[m], perm=far[m]) for m in range(chunks)]
    weights = jax.ShapeDtypeStruct((CORES * rows, chunks * pair), jnp.bfloat16)
    high, low = vmem_call(
        functools.partial(weight_kernel, experts=experts, cap=cap),
        [weights, weights],
        "weights",
        1,
        5,
    )(ids, normed, router_weight, routes, routes_other)

    gate_up = gate_up_weight[0]
    down = down_weight[0]
    back = []
    for m in range(chunks):
        side = move(near[m], perm=to_x)
        near_other = move(near[m], perm=to_core)
        side_other = move(side, perm=to_core)
        mine, mine_side, send = vmem_call(
            functools.partial(expert_kernel, ff=ff),
            [block, block, jax.ShapeDtypeStruct((2 * pair, width), jnp.bfloat16)],
            f"expert{m}",
            0,
            6,
        )(near[m], side, near_other, side_other, gate_up, down)
        got = move(send, perm=to_core)
        got_mine, got_side = got[:pair], got[pair:]
        out_side = (mine_side.astype(jnp.float32) + got_side.astype(jnp.float32)).astype(
            jnp.bfloat16
        )
        in_side = move(out_side, perm=to_x)
        total = (
            mine.astype(jnp.float32) + got_mine.astype(jnp.float32) + in_side.astype(jnp.float32)
        ).astype(jnp.bfloat16)
        back.append(move(total, perm=far[m]))

    mixed_own, mixed_other = vmem_call(
        combine_kernel,
        [
            jax.ShapeDtypeStruct((rows, width), jnp.float32),
            jax.ShapeDtypeStruct((rows, width), jnp.bfloat16),
        ],
        "combine",
        0,
        2 + chunks,
    )(high, low, *back)
    from_other = move(mixed_other, perm=to_core)
    return (tokens.astype(jnp.float32) + mixed_own + from_other.astype(jnp.float32)).astype(
        jnp.bfloat16
    )


def solution(mesh):
    in_specs = (
        P(("groups", "ep"), None),
        P(("groups", "ep"), None),
        P(),
        P(),
        P("ep", None, None),
        P("ep", None, None),
    )
    out_specs = P(("groups", "ep"), None)
    return jax.shard_map(shards, mesh=mesh, in_specs=in_specs, out_specs=out_specs, check_vma=False)
```

time: 418 us -> 169 us (0.40); the launches traced: 411 us -> 169 us
  blocking collectives: 171 us -> 0 us
  waiting for transfers between devices: 162 us -> 65.9 us
  starting transfers between devices: 5.72 us -> 58.4 us
  Pallas kernels: 0 us -> 29.6 us
  local copies, waits for them, and re-layouts: 37.9 us -> 9.46 us
  matrix products: 24.1 us -> 0 us
  other arithmetic: 10.2 us -> 5.01 us
    all_to_all x1 -> x0, blocking collectives: 171 us -> none  [shards(): lax.all_to_all(outgoing, 'ep', split_axis=0, concat_axis=0, tiled=True)]
    all_to_all x1 -> x0, waiting for transfers between devices: 162 us -> none  [shards(): lax.all_to_all(partial_value, 'ep', split_axis=0, concat_axis=0, tiled=True)]
    ppermute x0 -> x31, waiting for transfers between devices: none -> 65.9 us  [the longest x4 31.1 us: shards(): back.append(move(total, perm=far[m]))]
    ppermute x0 -> x31, starting transfers between devices: none -> 58.4 us  [the longest x4 24.9 us: shards(): near_other = move(near[m], perm=to_core)]
    pallas_call x0 -> x7, Pallas kernels: none -> 29.6 us  [the longest x4 24 us: shards(): vmem_call(functools.partial(expert_kernel, ff=ff), [block, block, jax.Sha...]
    dot_general x5 -> x0, matrix products: 24.1 us -> none  [the longest x1 9.7 us: shards(): jnp.dot(rows_in, gate_up_weight[0], preferred_element_type=jnp.float32)]
    reshape x3 -> x1, local copies, waits for them, and re-layouts: 21.6 us -> 0.7 us  [shards(): gain = norm_gain.reshape(1, width)]
    convert_element_type x1 -> x0, local copies, waits for them, and re-layouts: 10.1 us -> none  [shards(): jnp.dot(activated, down_weight[0], preferred_element_type=jnp.float32)]
  transfers between devices with their start and end apart: 1 -> 31, of which waited for: 1 -> 10; matrix products, arithmetic and copies ran while one was open for 0% -> 7% of each run, Pallas kernels for 0% -> 15%
where the time goes in v1:
time: 169 us
  waiting for transfers between devices  65.9 us (39%)
  starting transfers between devices  58.4 us (35%)
  Pallas kernels  29.6 us (18%)
  local copies, waits for them, and re-layouts  9.46 us (6%)
  other arithmetic  5.01 us (3%)
    ppermute x4, waiting for transfers between devices, shards(): back.append(move(total, perm=far[m]))  31.1 us
    ppermute x4, starting transfers between devices, shards(): near_other = move(near[m], perm=to_core)  24.9 us
    pallas_call x4, Pallas kernels, shards(): vmem_call(functools.partial(expert_kernel, ff=ff), [block, block, jax.Sha...  24 us
    ppermute x4, waiting for transfers between devices, shards(): in_side = move(out_side, perm=to_x)  22.9 us
    ppermute x4, starting transfers between devices, shards(): side_other = move(side, perm=to_core)  10.6 us
    ppermute x4, waiting for transfers between devices, shards(): side = move(near[m], perm=to_x)  10.2 us
    ppermute x4, starting transfers between devices, shards(): back.append(move(total, perm=far[m]))  9.62 us
    unnamed x11, local copies, waits for them, and re-layouts  8.67 us
  transfers between devices with their start and end apart: 31, of which 10 were waited for; matrix products, arithmetic and copies ran while one was open for 7% of the time, Pallas kernels for 15%

profile of v1, /device:TPU:13, one launch (start us, length us, event | category | flops | bytes accessed | tf_op | source)
XLA Modules:
  0.0 168.5 jit_solution(7060325648272338729)
XLA Ops:
  0.0 0.7 collective-permute-start
  0.7 0.8 copy.8.routes_own
  1.4 0.0 collective-permute-start.1
  1.5 0.7 reshape.3.gain
  2.2 0.1 stack.23.ids
  2.3 0.4 collective-permute-done.1.routes_other
  2.7 1.0 copy-done.1
  3.7 2.4 %select.7 = (bf16[128,2880]{1,0:T(8,128)(2,1)S(1)}, bf16[72,2880]{1,0:T(8,128)(2,1)S(1)}, bf16[72,2880]{1,0:T(8,128)(2,1)S(1)}, bf16[72,2880]{1,0:T(8,128)(2,1)S(1)}, bf16[72,2880]{1,0:T(8,128)(2,1)}) custom-call(s32[5]{0:T(128)S(1)} %stack.23.ids, bf16[64,2880]{1,0:T(8,128)(2,1)S(1)} %copy-done.1, bf16[64,2880]{1,0:T(8,128)(2,1)S(1)} %collective-permute-done.other, ...), custom_call_target="tpu_custom_call" | custom-call | tf_op jit(solution)/shard_map/select/pallas_call | solution.py:174
  6.1 1.4 collective-permute-start.2
  7.5 0.2 collective-permute-start.9
  7.6 1.2 collective-permute-start.3
  8.8 2.3 %collective-permute-start.16 = (bf16[72,2880]{1,0:T(8,128)(2,1)S(1)}, bf16[72,2880]{1,0:T(8,128)(2,1)}, u32[]{:S(2)}, u32[]{:S(2)}) collective-permute-start(bf16[72,2880]{1,0:T(8,128)(2,1)S(1)} %get-tuple-element.37), channel_id=1, source_target_pairs={{0,16},{1,20},{2,18},{3,22},{4,17},{5,21},{6,19},{7,23},{8,24},{9,... | collective-permute-start | bytes 1244168 | tf_op jit(solution)/shard_map/ppermute | solution.py:182
  11.2 0.2 collective-permute-start.23
  11.3 9.7 %collective-permute-start.4 = (bf16[72,2880]{1,0:T(8,128)(2,1)}, bf16[72,2880]{1,0:T(8,128)(2,1)}, u32[]{:S(2)}, u32[]{:S(2)}) collective-permute-start(bf16[72,2880]{1,0:T(8,128)(2,1)} %collective-permute-done.2.a), channel_id=1, source_target_pairs={{0,1},{1,0},{2,3},{3,2},{4,5},{5,4},{6,7},{7,6},{8,9},{9,8},{10,11... | collective-permute-start | bytes 1244168 | tf_op jit(solution)/shard_map/ppermute | solution.py:197
  21.0 0.5 collective-permute-start.10
  21.5 8.6 %collective-permute-start.5 = (bf16[72,2880]{1,0:T(8,128)(2,1)}, bf16[72,2880]{1,0:T(8,128)(2,1)}, u32[]{:S(2)}, u32[]{:S(2)}) collective-permute-start(bf16[72,2880]{1,0:T(8,128)(2,1)} %collective-permute-done.3.b), channel_id=1, source_target_pairs={{0,1},{1,0},{2,3},{3,2},{4,5},{5,4},{6,7},{7,6},{8,9},{9,8},{10,11... | collective-permute-start | bytes 1244168 | tf_op jit(solution)/shard_map/ppermute | solution.py:198
  30.1 13.8 %collective-permute-start.11 = (bf16[72,2880]{1,0:T(8,128)(2,1)}, bf16[72,2880]{1,0:T(8,128)(2,1)}, u32[]{:S(2)}, u32[]{:S(2)}) collective-permute-start(bf16[72,2880]{1,0:T(8,128)(2,1)} %collective-permute-done.9.a), channel_id=1, source_target_pairs={{0,1},{1,0},{2,3},{3,2},{4,5},{5,4},{6,7},{7,6},{8,9},{9,8},{10,11... | collective-permute-start | bytes 1244168 | tf_op jit(solution)/shard_map/ppermute | solution.py:197
  43.9 6.5 %copy.11 = bf16[1,2880,720]{2,1,0:T(8,128)(2,1)} copy(bf16[1,2880,720]{1,2,0:T(8,128)(2,1)} %param.10) | data formatting | bytes 8294400 | tf_op args[4]
  50.4 0.3 collective-permute-start.17
  50.7 1.2 collective-permute-start.24
  51.9 0.6 collective-permute-start.12
  52.5 6.2 %expert0.1 = (bf16[72,2880]{1,0:T(8,128)(2,1)S(1)}, bf16[72,2880]{1,0:T(8,128)(2,1)S(1)}, bf16[144,2880]{1,0:T(8,128)(2,1)S(1)}) custom-call(bf16[72,2880]{1,0:T(8,128)(2,1)} %collective-permute-done.2.a, bf16[72,2880]{1,0:T(8,128)(2,1)} %collective-permute-done.3.b, bf16[72,2880]{1,0:T(8,128)(2,1)} %collective-permute-done.4.c, ...), custom_call_target="tpu_custom_call" | custom-call | tf_op jit(solution)/shard_map/expert0/pallas_call | solution.py:199
  58.8 0.1 collective-permute-start.6
  58.9 0.5 collective-permute-start.18
  59.3 2.5 %collective-permute-done.17.b = bf16[72,2880]{1,0:T(8,128)(2,1)S(1)} collective-permute-done((bf16[72,2880]{1,0:T(8,128)(2,1)}, bf16[72,2880]{1,0:T(8,128)(2,1)S(1)}, u32[]{:S(2)}, u32[]{:S(2)}) %collective-permute-start.17) | collective-permute-done | bytes 414752 | tf_op jit(solution)/shard_map/ppermute | solution.py:196
  61.9 1.4 collective-permute-start.19
  63.3 7.6 %collective-permute-done.24.b = bf16[72,2880]{1,0:T(8,128)(2,1)S(1)} collective-permute-done((bf16[72,2880]{1,0:T(8,128)(2,1)S(1)}, bf16[72,2880]{1,0:T(8,128)(2,1)S(1)}, u32[]{:S(2)}, u32[]{:S(2)}) %collective-permute-start.24) | collective-permute-done | bytes 414752 | tf_op jit(solution)/shard_map/ppermute | solution.py:196
  71.0 0.9 collective-permute-start.25
  71.9 0.0 collective-permute-start.26
  71.9 6.1 %expert1.1 = (bf16[72,2880]{1,0:T(8,128)(2,1)S(1)}, bf16[72,2880]{1,0:T(8,128)(2,1)S(1)}, bf16[144,2880]{1,0:T(8,128)(2,1)S(1)}) custom-call(bf16[72,2880]{1,0:T(8,128)(2,1)} %collective-permute-done.9.a, bf16[72,2880]{1,0:T(8,128)(2,1)} %collective-permute-done.10.b, bf16[72,2880]{1,0:T(8,128)(2,1)} %collective-permute-done.11.c, ...), custom_call_target="tpu_custom_call" | custom-call | tf_op jit(solution)/shard_map/expert1/pallas_call | solution.py:199
  78.0 0.6 collective-permute-start.13
  78.6 5.9 %expert2.1 = (bf16[72,2880]{1,0:T(8,128)(2,1)S(1)}, bf16[72,2880]{1,0:T(8,128)(2,1)S(1)}, bf16[144,2880]{1,0:T(8,128)(2,1)S(1)}) custom-call(bf16[72,2880]{1,0:T(8,128)(2,1)} %collective-permute-done.16.a, bf16[72,2880]{1,0:T(8,128)(2,1)S(1)} %collective-permute-done.17.b, bf16[72,2880]{1,0:T(8,128)(2,1)S(1)} %collective-permute-done.18.c, ...), custom_call_target="tpu_custom_call" | custom-call | tf_op jit(solution)/shard_map/expert2/pallas_call | solution.py:199
  84.5 0.1 collective-permute-start.20
  84.6 5.7 %expert3.1 = (bf16[72,2880]{1,0:T(8,128)(2,1)S(1)}, bf16[72,2880]{1,0:T(8,128)(2,1)S(1)}, bf16[144,2880]{1,0:T(8,128)(2,1)S(1)}) custom-call(bf16[72,2880]{1,0:T(8,128)(2,1)S(1)} %collective-permute-done.23.a, bf16[72,2880]{1,0:T(8,128)(2,1)S(1)} %collective-permute-done.24.b, bf16[72,2880]{1,0:T(8,128)(2,1)S(1)} %collective-permute-done.25.c, ...), custom_call_target="tpu_custom_call" | custom-call | tf_op jit(solution)/shard_map/expert3/pallas_call | solution.py:199
  90.4 0.5 collective-permute-start.27
  90.9 0.1 add_convert_fusion.7
  91.0 0.3 collective-permute-start.7
  91.3 0.1 add_convert_fusion.5
  91.4 1.3 collective-permute-start.14
  92.7 0.1 add_convert_fusion.3
  92.8 0.0 copy-start.3
  92.8 0.3 collective-permute-start.21
  93.2 0.1 add_convert_fusion.1
  93.3 1.3 collective-permute-start.28
  94.5 7.8 %collective-permute-done.7 = bf16[72,2880]{1,0:T(8,128)(2,1)S(1)} collective-permute-done((bf16[72,2880]{1,0:T(8,128)(2,1)S(1)}, bf16[72,2880]{1,0:T(8,128)(2,1)S(1)}, u32[]{:S(2)}, u32[]{:S(2)}) %collective-permute-start.7) | collective-permute-done | bytes 414752 | tf_op jit(solution)/shard_map/ppermute | solution.py:211
  102.4 0.9 add_convert_fusion.6
  103.3 1.8 %collective-permute-start.8 = (bf16[72,2880]{1,0:T(8,128)(2,1)}, bf16[72,2880]{1,0:T(8,128)(2,1)S(1)}, u32[]{:S(2)}, u32[]{:S(2)}) collective-permute-start(bf16[72,2880]{1,0:T(8,128)(2,1)} %add_convert_fusion.6), channel_id=1, source_target_pairs={{0,0},{1,4},{2,2},{3,6},{4,1},{5,5},{6,3},{7,7},{8,8},{9,12},{10,1... | collective-permute-start | bytes 1244168 | tf_op jit(solution)/shard_map/ppermute | solution.py:215
  105.1 6.4 %collective-permute-done.14 = bf16[72,2880]{1,0:T(8,128)(2,1)S(1)} collective-permute-done((bf16[72,2880]{1,0:T(8,128)(2,1)S(1)}, bf16[72,2880]{1,0:T(8,128)(2,1)S(1)}, u32[]{:S(2)}, u32[]{:S(2)}) %collective-permute-start.14) | collective-permute-done | bytes 414752 | tf_op jit(solution)/shard_map/ppermute | solution.py:211
  111.5 0.9 add_convert_fusion.4
  112.4 3.3 %collective-permute-start.15 = (bf16[72,2880]{1,0:T(8,128)(2,1)}, bf16[72,2880]{1,0:T(8,128)(2,1)S(1)}, u32[]{:S(2)}, u32[]{:S(2)}) collective-permute-start(bf16[72,2880]{1,0:T(8,128)(2,1)} %add_convert_fusion.4), channel_id=1, source_target_pairs={{0,8},{1,12},{2,10},{3,14},{4,9},{5,13},{6,11},{7,15},{8,0},{9,4},... | collective-permute-start | bytes 1244168 | tf_op jit(solution)/shard_map/ppermute | solution.py:215
  115.7 4.8 %collective-permute-done.21 = bf16[72,2880]{1,0:T(8,128)(2,1)S(1)} collective-permute-done((bf16[72,2880]{1,0:T(8,128)(2,1)S(1)}, bf16[72,2880]{1,0:T(8,128)(2,1)S(1)}, u32[]{:S(2)}, u32[]{:S(2)}) %collective-permute-start.21) | collective-permute-done | bytes 414752 | tf_op jit(solution)/shard_map/ppermute | solution.py:211
  120.5 0.9 add_convert_fusion.2
  121.5 4.3 %collective-permute-start.22 = (bf16[72,2880]{1,0:T(8,128)(2,1)}, bf16[72,2880]{1,0:T(8,128)(2,1)S(1)}, u32[]{:S(2)}, u32[]{:S(2)}) collective-permute-start(bf16[72,2880]{1,0:T(8,128)(2,1)} %add_convert_fusion.2), channel_id=1, source_target_pairs={{0,16},{1,20},{2,18},{3,22},{4,17},{5,21},{6,19},{7,23},{8,24},{9,... | collective-permute-start | bytes 1244168 | tf_op jit(solution)/shard_map/ppermute | solution.py:215
  125.8 3.8 %collective-permute-done.28 = bf16[72,2880]{1,0:T(8,128)(2,1)S(1)} collective-permute-done((bf16[72,2880]{1,0:T(8,128)(2,1)S(1)}, bf16[72,2880]{1,0:T(8,128)(2,1)S(1)}, u32[]{:S(2)}, u32[]{:S(2)}) %collective-permute-start.28) | collective-permute-done | bytes 414752 | tf_op jit(solution)/shard_map/ppermute | solution.py:211
  129.6 1.0 add_convert_fusion
  130.6 0.2 collective-permute-start.29
  130.8 0.4 copy.9.router
  131.2 1.3 weights.1
  132.4 20.2 %collective-permute-done.22.refs_2_ = bf16[72,2880]{1,0:T(8,128)(2,1)S(1)} collective-permute-done((bf16[72,2880]{1,0:T(8,128)(2,1)}, bf16[72,2880]{1,0:T(8,128)(2,1)S(1)}, u32[]{:S(2)}, u32[]{:S(2)}) %collective-permute-start.22) | collective-permute-done | bytes 414752 | tf_op jit(solution)/shard_map/ppermute | solution.py:215
  152.6 10.9 %collective-permute-done.29.refs_3_ = bf16[72,2880]{1,0:T(8,128)(2,1)} collective-permute-done((bf16[72,2880]{1,0:T(8,128)(2,1)}, bf16[72,2880]{1,0:T(8,128)(2,1)}, u32[]{:S(2)}, u32[]{:S(2)}) %collective-permute-start.29) | collective-permute-done | bytes 414752 | tf_op jit(solution)/shard_map/ppermute | solution.py:215
  163.5 2.0 %combine.1 = (f32[64,2880]{1,0:T(8,128)S(1)}, bf16[64,2880]{1,0:T(8,128)(2,1)S(1)}) custom-call(bf16[128,288]{1,0:T(8,128)(2,1)S(1)} %get-tuple-element.27.high, bf16[128,288]{1,0:T(8,128)(2,1)S(1)} %get-tuple-element.28.low, bf16[72,2880]{1,0:T(8,128)(2,1)S(1)} %collective-permute-done.8.refs_0_, bf16[72,2880]{1,0:T(8,128)(2,1)S(1)} %collective-permute-done.15.refs_1_, ...), custom_call_target="tpu_custom_call" | custom-call | tf_op jit(solution)/shard_map/combine/pallas_call | solution.py:217
  165.5 0.8 collective-permute-start.30
  166.3 1.3 collective-permute-done.30
  167.6 0.9 add_convert_fusion.8
  (27 shorter events, 0.1 us)
Async XLA Ops:
  0.0 2.7 %collective-permute-start = (bf16[64,2880]{1,0:T(8,128)(2,1)}, bf16[64,2880]{1,0:T(8,128)(2,1)S(1)}, u32[]{:S(2)}, u32[]{:S(2)}) collective-permute-start(bf16[64,2880]{1,0:T(8,128)(2,1)} %own.1), channel_id=1, source_target_pairs={{0,1},{1,0},{2,3},{3,2},{4,5},{5,4},{6,7},{7,6},{8,9},{9,8},{10,11... | collective-permute-start | bytes 1105928 | tf_op jit(solution)/shard_map/ppermute | solution.py:170
  1.4 1.2 collective-permute-start.1
  2.7 1.0 copy-start.1
  6.1 1.6 collective-permute-start.2
  7.5 13.5 %collective-permute-start.9 = (bf16[72,2880]{1,0:T(8,128)(2,1)S(1)}, bf16[72,2880]{1,0:T(8,128)(2,1)}, u32[]{:S(2)}, u32[]{:S(2)}) collective-permute-start(bf16[72,2880]{1,0:T(8,128)(2,1)S(1)} %get-tuple-element.33), channel_id=1, source_target_pairs={{0,8},{1,12},{2,10},{3,14},{4,9},{5,13},{6,11},{7,15},{8,0},{9,4},... | collective-permute-start | bytes 1244168 | tf_op jit(solution)/shard_map/ppermute | solution.py:182
  7.6 13.9 %collective-permute-start.3 = (bf16[72,2880]{1,0:T(8,128)(2,1)}, bf16[72,2880]{1,0:T(8,128)(2,1)}, u32[]{:S(2)}, u32[]{:S(2)}) collective-permute-start(bf16[72,2880]{1,0:T(8,128)(2,1)} %collective-permute-done.2.a), channel_id=1, source_target_pairs={{0,2},{1,3},{2,0},{3,1},{4,6},{5,7},{6,4},{7,5},{8,10},{9,11},{10,... | collective-permute-start | bytes 1244168 | tf_op jit(solution)/shard_map/ppermute | solution.py:196
  8.8 21.2 %collective-permute-start.16 = (bf16[72,2880]{1,0:T(8,128)(2,1)S(1)}, bf16[72,2880]{1,0:T(8,128)(2,1)}, u32[]{:S(2)}, u32[]{:S(2)}) collective-permute-start(bf16[72,2880]{1,0:T(8,128)(2,1)S(1)} %get-tuple-element.37), channel_id=1, source_target_pairs={{0,16},{1,20},{2,18},{3,22},{4,17},{5,21},{6,19},{7,23},{8,24},{9,... | collective-permute-start | bytes 1244168 | tf_op jit(solution)/shard_map/ppermute | solution.py:182
  11.2 41.4 %copy-start = (bf16[1,360,2880]{2,1,0:T(8,128)(2,1)S(1)}, bf16[1,360,2880]{2,1,0:T(8,128)(2,1)}, u32[]{:S(2)}) copy-start(bf16[1,360,2880]{2,1,0:T(8,128)(2,1)} %param.11) | copy-start | bytes 6220804
  11.2 39.3 %collective-permute-start.23 = (bf16[72,2880]{1,0:T(8,128)(2,1)}, bf16[72,2880]{1,0:T(8,128)(2,1)S(1)}, u32[]{:S(2)}, u32[]{:S(2)}) collective-permute-start(bf16[72,2880]{1,0:T(8,128)(2,1)} %get-tuple-element.41), channel_id=1, source_target_pairs={{0,24},{1,28},{2,26},{3,30},{4,25},{5,29},{6,27},{7,31},{8,16},{9,... | collective-permute-start | bytes 1244168 | tf_op jit(solution)/shard_map/ppermute | solution.py:182
  11.3 39.3 %collective-permute-start.4 = (bf16[72,2880]{1,0:T(8,128)(2,1)}, bf16[72,2880]{1,0:T(8,128)(2,1)}, u32[]{:S(2)}, u32[]{:S(2)}) collective-permute-start(bf16[72,2880]{1,0:T(8,128)(2,1)} %collective-permute-done.2.a), channel_id=1, source_target_pairs={{0,1},{1,0},{2,3},{3,2},{4,5},{5,4},{6,7},{7,6},{8,9},{9,8},{10,11... | collective-permute-start | bytes 1244168 | tf_op jit(solution)/shard_map/ppermute | solution.py:197
  21.0 30.9 %collective-permute-start.10 = (bf16[72,2880]{1,0:T(8,128)(2,1)}, bf16[72,2880]{1,0:T(8,128)(2,1)}, u32[]{:S(2)}, u32[]{:S(2)}) collective-permute-start(bf16[72,2880]{1,0:T(8,128)(2,1)} %collective-permute-done.9.a), channel_id=1, source_target_pairs={{0,2},{1,3},{2,0},{3,1},{4,6},{5,7},{6,4},{7,5},{8,10},{9,11},{10,... | collective-permute-start | bytes 1244168 | tf_op jit(solution)/shard_map/ppermute | solution.py:196
  21.5 31.0 %collective-permute-start.5 = (bf16[72,2880]{1,0:T(8,128)(2,1)}, bf16[72,2880]{1,0:T(8,128)(2,1)}, u32[]{:S(2)}, u32[]{:S(2)}) collective-permute-start(bf16[72,2880]{1,0:T(8,128)(2,1)} %collective-permute-done.3.b), channel_id=1, source_target_pairs={{0,1},{1,0},{2,3},{3,2},{4,5},{5,4},{6,7},{7,6},{8,9},{9,8},{10,11... | collective-permute-start | bytes 1244168 | tf_op jit(solution)/shard_map/ppermute | solution.py:198
  30.1 28.8 %collective-permute-start.11 = (bf16[72,2880]{1,0:T(8,128)(2,1)}, bf16[72,2880]{1,0:T(8,128)(2,1)}, u32[]{:S(2)}, u32[]{:S(2)}) collective-permute-start(bf16[72,2880]{1,0:T(8,128)(2,1)} %collective-permute-done.9.a), channel_id=1, source_target_pairs={{0,1},{1,0},{2,3},{3,2},{4,5},{5,4},{6,7},{7,6},{8,9},{9,8},{10,11... | collective-permute-start | bytes 1244168 | tf_op jit(solution)/shard_map/ppermute | solution.py:197
  50.4 11.5 %collective-permute-start.17 = (bf16[72,2880]{1,0:T(8,128)(2,1)}, bf16[72,2880]{1,0:T(8,128)(2,1)S(1)}, u32[]{:S(2)}, u32[]{:S(2)}) collective-permute-start(bf16[72,2880]{1,0:T(8,128)(2,1)} %collective-permute-done.16.a), channel_id=1, source_target_pairs={{0,2},{1,3},{2,0},{3,1},{4,6},{5,7},{6,4},{7,5},{8,10},{9,11},{10,... | collective-permute-start | bytes 1244168 | tf_op jit(solution)/shard_map/ppermute | solution.py:196
  50.7 20.3 %collective-permute-start.24 = (bf16[72,2880]{1,0:T(8,128)(2,1)S(1)}, bf16[72,2880]{1,0:T(8,128)(2,1)S(1)}, u32[]{:S(2)}, u32[]{:S(2)}) collective-permute-start(bf16[72,2880]{1,0:T(8,128)(2,1)S(1)} %collective-permute-done.23.a), channel_id=1, source_target_pairs={{0,2},{1,3},{2,0},{3,1},{4,6},{5,7},{6,4},{7,5},{8,10},{9,11},{10,... | collective-permute-start | bytes 1244168 | tf_op jit(solution)/shard_map/ppermute | solution.py:196
  51.9 20.0 %collective-permute-start.12 = (bf16[72,2880]{1,0:T(8,128)(2,1)}, bf16[72,2880]{1,0:T(8,128)(2,1)S(1)}, u32[]{:S(2)}, u32[]{:S(2)}) collective-permute-start(bf16[72,2880]{1,0:T(8,128)(2,1)} %collective-permute-done.10.b), channel_id=1, source_target_pairs={{0,1},{1,0},{2,3},{3,2},{4,5},{5,4},{6,7},{7,6},{8,9},{9,8},{10,11... | collective-permute-start | bytes 1244168 | tf_op jit(solution)/shard_map/ppermute | solution.py:198
  58.8 32.1 %collective-permute-start.6 = (bf16[144,2880]{1,0:T(8,128)(2,1)S(1)}, bf16[144,2880]{1,0:T(8,128)(2,1)S(1)}, u32[]{:S(2)}, u32[]{:S(2)}) collective-permute-start(bf16[144,2880]{1,0:T(8,128)(2,1)S(1)} %get-tuple-element.31), channel_id=1, source_target_pairs={{0,1},{1,0},{2,3},{3,2},{4,5},{5,4},{6,7},{7,6},{8,9},{9,8},{10,11... | collective-permute-start | bytes 2488328 | tf_op jit(solution)/shard_map/ppermute | solution.py:206
  58.9 19.2 %collective-permute-start.18 = (bf16[72,2880]{1,0:T(8,128)(2,1)}, bf16[72,2880]{1,0:T(8,128)(2,1)S(1)}, u32[]{:S(2)}, u32[]{:S(2)}) collective-permute-start(bf16[72,2880]{1,0:T(8,128)(2,1)} %collective-permute-done.16.a), channel_id=1, source_target_pairs={{0,1},{1,0},{2,3},{3,2},{4,5},{5,4},{6,7},{7,6},{8,9},{9,8},{10,11... | collective-permute-start | bytes 1244168 | tf_op jit(solution)/shard_map/ppermute | solution.py:197
  61.9 16.7 %collective-permute-start.19 = (bf16[72,2880]{1,0:T(8,128)(2,1)S(1)}, bf16[72,2880]{1,0:T(8,128)(2,1)S(1)}, u32[]{:S(2)}, u32[]{:S(2)}) collective-permute-start(bf16[72,2880]{1,0:T(8,128)(2,1)S(1)} %collective-permute-done.17.b), channel_id=1, source_target_pairs={{0,1},{1,0},{2,3},{3,2},{4,5},{5,4},{6,7},{7,6},{8,9},{9,8},{10,11... | collective-permute-start | bytes 1244168 | tf_op jit(solution)/shard_map/ppermute | solution.py:198
  71.0 13.6 %collective-permute-start.25 = (bf16[72,2880]{1,0:T(8,128)(2,1)S(1)}, bf16[72,2880]{1,0:T(8,128)(2,1)S(1)}, u32[]{:S(2)}, u32[]{:S(2)}) collective-permute-start(bf16[72,2880]{1,0:T(8,128)(2,1)S(1)} %collective-permute-done.23.a), channel_id=1, source_target_pairs={{0,1},{1,0},{2,3},{3,2},{4,5},{5,4},{6,7},{7,6},{8,9},{9,8},{10,11... | collective-permute-start | bytes 1244168 | tf_op jit(solution)/shard_map/ppermute | solution.py:197
  71.9 12.7 %collective-permute-start.26 = (bf16[72,2880]{1,0:T(8,128)(2,1)S(1)}, bf16[72,2880]{1,0:T(8,128)(2,1)S(1)}, u32[]{:S(2)}, u32[]{:S(2)}) collective-permute-start(bf16[72,2880]{1,0:T(8,128)(2,1)S(1)} %collective-permute-done.24.b), channel_id=1, source_target_pairs={{0,1},{1,0},{2,3},{3,2},{4,5},{5,4},{6,7},{7,6},{8,9},{9,8},{10,11... | collective-permute-start | bytes 1244168 | tf_op jit(solution)/shard_map/ppermute | solution.py:198
  78.0 13.3 %collective-permute-start.13 = (bf16[144,2880]{1,0:T(8,128)(2,1)S(1)}, bf16[144,2880]{1,0:T(8,128)(2,1)S(1)}, u32[]{:S(2)}, u32[]{:S(2)}) collective-permute-start(bf16[144,2880]{1,0:T(8,128)(2,1)S(1)} %get-tuple-element.35), channel_id=1, source_target_pairs={{0,1},{1,0},{2,3},{3,2},{4,5},{5,4},{6,7},{7,6},{8,9},{9,8},{10,11... | collective-permute-start | bytes 2488328 | tf_op jit(solution)/shard_map/ppermute | solution.py:206
  84.5 8.2 %collective-permute-start.20 = (bf16[144,2880]{1,0:T(8,128)(2,1)S(1)}, bf16[144,2880]{1,0:T(8,128)(2,1)S(1)}, u32[]{:S(2)}, u32[]{:S(2)}) collective-permute-start(bf16[144,2880]{1,0:T(8,128)(2,1)S(1)} %get-tuple-element.39), channel_id=1, source_target_pairs={{0,1},{1,0},{2,3},{3,2},{4,5},{5,4},{6,7},{7,6},{8,9},{9,8},{10,11... | collective-permute-start | bytes 2488328 | tf_op jit(solution)/shard_map/ppermute | solution.py:206
  90.4 2.8 %collective-permute-start.27 = (bf16[144,2880]{1,0:T(8,128)(2,1)S(1)}, bf16[144,2880]{1,0:T(8,128)(2,1)S(1)}, u32[]{:S(2)}, u32[]{:S(2)}) collective-permute-start(bf16[144,2880]{1,0:T(8,128)(2,1)S(1)} %get-tuple-element.43), channel_id=1, source_target_pairs={{0,1},{1,0},{2,3},{3,2},{4,5},{5,4},{6,7},{7,6},{8,9},{9,8},{10,11... | collective-permute-start | bytes 2488328 | tf_op jit(solution)/shard_map/ppermute | solution.py:206
  91.0 11.4 %collective-permute-start.7 = (bf16[72,2880]{1,0:T(8,128)(2,1)S(1)}, bf16[72,2880]{1,0:T(8,128)(2,1)S(1)}, u32[]{:S(2)}, u32[]{:S(2)}) collective-permute-start(bf16[72,2880]{1,0:T(8,128)(2,1)S(1)} %add_convert_fusion.7), channel_id=1, source_target_pairs={{0,2},{1,3},{2,0},{3,1},{4,6},{5,7},{6,4},{7,5},{8,10},{9,11},{10,... | collective-permute-start | bytes 1244168 | tf_op jit(solution)/shard_map/ppermute | solution.py:211
  91.4 20.0 %collective-permute-start.14 = (bf16[72,2880]{1,0:T(8,128)(2,1)S(1)}, bf16[72,2880]{1,0:T(8,128)(2,1)S(1)}, u32[]{:S(2)}, u32[]{:S(2)}) collective-permute-start(bf16[72,2880]{1,0:T(8,128)(2,1)S(1)} %add_convert_fusion.5), channel_id=1, source_target_pairs={{0,2},{1,3},{2,0},{3,1},{4,6},{5,7},{6,4},{7,5},{8,10},{9,11},{10,... | collective-permute-start | bytes 1244168 | tf_op jit(solution)/shard_map/ppermute | solution.py:211
  92.8 37.9 %copy-start.3 = (bf16[2880,8]{0,1:T(8,128)(2,1)S(1)}, bf16[2880,8]{0,1:T(8,128)(2,1)}, u32[]{:S(2)}) copy-start(bf16[2880,8]{0,1:T(8,128)(2,1)} %param.9) | copy-start | bytes 138244
  92.8 27.7 %collective-permute-start.21 = (bf16[72,2880]{1,0:T(8,128)(2,1)S(1)}, bf16[72,2880]{1,0:T(8,128)(2,1)S(1)}, u32[]{:S(2)}, u32[]{:S(2)}) collective-permute-start(bf16[72,2880]{1,0:T(8,128)(2,1)S(1)} %add_convert_fusion.3), channel_id=1, source_target_pairs={{0,2},{1,3},{2,0},{3,1},{4,6},{5,7},{6,4},{7,5},{8,10},{9,11},{10,... | collective-permute-start | bytes 1244168 | tf_op jit(solution)/shard_map/ppermute | solution.py:211
  93.3 36.4 %collective-permute-start.28 = (bf16[72,2880]{1,0:T(8,128)(2,1)S(1)}, bf16[72,2880]{1,0:T(8,128)(2,1)S(1)}, u32[]{:S(2)}, u32[]{:S(2)}) collective-permute-start(bf16[72,2880]{1,0:T(8,128)(2,1)S(1)} %add_convert_fusion.1), channel_id=1, source_target_pairs={{0,2},{1,3},{2,0},{3,1},{4,6},{5,7},{6,4},{7,5},{8,10},{9,11},{10,... | collective-permute-start | bytes 1244168 | tf_op jit(solution)/shard_map/ppermute | solution.py:211
  103.3 29.1 %collective-permute-start.8 = (bf16[72,2880]{1,0:T(8,128)(2,1)}, bf16[72,2880]{1,0:T(8,128)(2,1)S(1)}, u32[]{:S(2)}, u32[]{:S(2)}) collective-permute-start(bf16[72,2880]{1,0:T(8,128)(2,1)} %add_convert_fusion.6), channel_id=1, source_target_pairs={{0,0},{1,4},{2,2},{3,6},{4,1},{5,5},{6,3},{7,7},{8,8},{9,12},{10,1... | collective-permute-start | bytes 1244168 | tf_op jit(solution)/shard_map/ppermute | solution.py:215
  112.4 55.2 %copy-start.2 = (bf16[64,2880]{1,0:T(8,128)(2,1)S(1)}, bf16[64,2880]{1,0:T(8,128)(2,1)}, u32[]{:S(2)}) copy-start(bf16[64,2880]{1,0:T(8,128)(2,1)} %own.1) | copy-start | bytes 1105924
  112.4 20.0 %collective-permute-start.15 = (bf16[72,2880]{1,0:T(8,128)(2,1)}, bf16[72,2880]{1,0:T(8,128)(2,1)S(1)}, u32[]{:S(2)}, u32[]{:S(2)}) collective-permute-start(bf16[72,2880]{1,0:T(8,128)(2,1)} %add_convert_fusion.4), channel_id=1, source_target_pairs={{0,8},{1,12},{2,10},{3,14},{4,9},{5,13},{6,11},{7,15},{8,0},{9,4},... | collective-permute-start | bytes 1244168 | tf_op jit(solution)/shard_map/ppermute | solution.py:215
  121.5 31.2 %collective-permute-start.22 = (bf16[72,2880]{1,0:T(8,128)(2,1)}, bf16[72,2880]{1,0:T(8,128)(2,1)S(1)}, u32[]{:S(2)}, u32[]{:S(2)}) collective-permute-start(bf16[72,2880]{1,0:T(8,128)(2,1)} %add_convert_fusion.2), channel_id=1, source_target_pairs={{0,16},{1,20},{2,18},{3,22},{4,17},{5,21},{6,19},{7,23},{8,24},{9,... | collective-permute-start | bytes 1244168 | tf_op jit(solution)/shard_map/ppermute | solution.py:215
  130.6 32.9 %collective-permute-start.29 = (bf16[72,2880]{1,0:T(8,128)(2,1)}, bf16[72,2880]{1,0:T(8,128)(2,1)}, u32[]{:S(2)}, u32[]{:S(2)}) collective-permute-start(bf16[72,2880]{1,0:T(8,128)(2,1)} %add_convert_fusion), channel_id=1, source_target_pairs={{0,24},{1,28},{2,26},{3,30},{4,25},{5,29},{6,27},{7,31},{8,16},{9,... | collective-permute-start | bytes 1244168 | tf_op jit(solution)/shard_map/ppermute | solution.py:215
  165.5 2.2 %collective-permute-start.30 = (bf16[64,2880]{1,0:T(8,128)(2,1)S(1)}, bf16[64,2880]{1,0:T(8,128)(2,1)S(1)}, u32[]{:S(2)}, u32[]{:S(2)}) collective-permute-start(bf16[64,2880]{1,0:T(8,128)(2,1)S(1)} %get-tuple-element.46), channel_id=1, source_target_pairs={{0,1},{1,0},{2,3},{3,2},{4,5},{5,4},{6,7},{7,6},{8,9},{9,8},{10,11... | collective-permute-start | bytes 1105928 | tf_op jit(solution)/shard_map/ppermute | solution.py:227

commit v2 on v1

v2 whole, which is shorter than its diff:
```python
import functools

import jax
import jax.numpy as jnp
from jax import lax
from jax.experimental import pallas as pl
from jax.experimental.pallas import tpu as pltpu
from jax.sharding import PartitionSpec as P


CORES = 2
SHARDS = 4
VMEM_BYTES = 48 * 1024 * 1024


def dot32(a, b, dims=((1,), (0,))):
    return lax.dot_general(a, b, (dims, ((), ())), preferred_element_type=jnp.float32)


def places_of(routes_own, routes_other, own_core, experts, cap):
    places, named = [], []
    for routes, core in ((routes_own, own_core), (routes_other, 1 - own_core)):
        rows = routes.shape[1]
        ids = lax.broadcasted_iota(jnp.int32, (experts, rows), 0)
        hits = (routes[0:1, :] == ids).astype(jnp.float32)
        for k in range(1, routes.shape[0]):
            hits = hits + (routes[k : k + 1, :] == ids).astype(jnp.float32)
        before = (
            lax.broadcasted_iota(jnp.int32, (rows, rows), 0)
            < lax.broadcasted_iota(jnp.int32, (rows, rows), 1)
        ).astype(jnp.bfloat16)
        slot = dot32(hits.astype(jnp.bfloat16), before).astype(jnp.int32)
        places.append(slot + core * cap)
        named.append(hits)
    return jnp.concatenate(places, axis=1), jnp.concatenate(named, axis=1) > 0.5


def at_rows(value, expert):
    mine = lax.broadcasted_iota(jnp.int32, value.shape, 0) == expert
    return jnp.sum(jnp.where(mine, value, jnp.zeros_like(value)), axis=0, keepdims=True)


def normed_of(tokens, gain):
    stream = tokens.astype(jnp.float32)
    mean_square = jnp.mean(stream * stream, axis=-1, keepdims=True)
    return (stream * lax.rsqrt(mean_square + 1e-05) * gain).astype(jnp.bfloat16)


def select_kernel(ids, own, other, routes_own, routes_other, gain, normed, *blocks, experts, cap):
    rows = own.shape[0]
    scale = gain[...].astype(jnp.float32)
    own_core = ids[len(blocks)]
    normed[0:rows, :] = normed_of(own[...], scale)
    normed[rows:, :] = normed_of(other[...], scale)
    place, named = places_of(routes_own[...], routes_other[...], own_core, experts, cap)
    place = jnp.where(named, place + 1, 0)
    values = normed[...]
    slots = lax.broadcasted_iota(jnp.int32, (CORES * cap, CORES * rows), 0) + 1
    for m, block in enumerate(blocks):
        pick = (slots == at_rows(place, ids[m])).astype(jnp.bfloat16)
        block[...] = dot32(pick, values).astype(jnp.bfloat16)


def weight_kernel(ids, normed, router, routes_own, routes_other, high, low, *, experts, cap):
    pair = CORES * cap
    count = high.shape[0] // pair
    logits = dot32(router[...], normed[...], ((1,), (1,)))
    place, named = places_of(routes_own[...], routes_other[...], ids[count], experts, cap)
    expo = jnp.where(named, jnp.exp(logits), 0.0)
    prob = expo / jnp.sum(expo, axis=0, keepdims=True)
    place = jnp.where(named, place + 1, 0)
    slots = lax.broadcasted_iota(jnp.int32, (pair, high.shape[1]), 0) + 1
    for m in range(count):
        here = slots == at_rows(place, ids[m])
        weight = jnp.where(here, at_rows(prob, ids[m]), 0.0)
        first = weight.astype(jnp.bfloat16)
        high[m * pair : (m + 1) * pair, :] = first
        low[m * pair : (m + 1) * pair, :] = (weight - first.astype(jnp.float32)).astype(
            jnp.bfloat16
        )


def expert_kernel(a, b, c, d, gate_up, down, mine_a, mine_b, send, *, ff):
    rows = a.shape[0]
    values = jnp.concatenate([a[...], b[...], c[...], d[...]], axis=0)
    hidden = dot32(values, gate_up[...], ((1,), (1,)))
    gate = hidden[:, :ff]
    up = hidden[:, ff:]
    activated = ((up + 1.0) * gate * jax.nn.sigmoid(1.702 * gate)).astype(jnp.bfloat16)
    partial_value = dot32(activated, down[...]).astype(jnp.bfloat16)
    mine_a[...] = partial_value[0:rows]
    mine_b[...] = partial_value[rows : 2 * rows]
    send[...] = partial_value[2 * rows :]


def combine_kernel(high, low, *refs):
    mixed_own, mixed_other = refs[-2], refs[-1]
    values = jnp.concatenate([r[...] for r in refs[:-2]], axis=0)
    mixture = dot32(high[...], values, ((0,), (0,))) + dot32(low[...], values, ((0,), (0,)))
    rows = mixed_own.shape[0]
    mixed_own[...] = mixture[:rows]
    mixed_other[...] = mixture[rows:].astype(jnp.bfloat16)


def vmem_call(kernel, out_shape, scalars=0, count=0):
    specs = [pl.BlockSpec(memory_space=pltpu.SMEM)] * scalars
    specs = specs + [pl.BlockSpec(memory_space=pltpu.VMEM)] * (count - scalars)
    return pl.pallas_call(
        kernel,
        out_shape=out_shape,
        in_specs=specs,
        out_specs=jax.tree.map(lambda _: pl.BlockSpec(memory_space=pltpu.VMEM), out_shape),
        compiler_params=pltpu.CompilerParams(vmem_limit_bytes=VMEM_BYTES),
    )


def shards(tokens, routes, norm_gain, router_weight, gate_up_weight, down_weight):
    rows, width = tokens.shape
    top = routes.shape[1]
    experts = router_weight.shape[1]
    devices = lax.axis_size("ep")
    shard_count = devices // experts
    if shard_count != SHARDS or experts % CORES:
        raise ValueError("unsupported mesh")
    ff = down_weight.shape[1]
    cap = min(rows, shard_count * (17 * rows * top // (16 * experts * shard_count) + 1))
    chunks = experts // CORES
    pair = CORES * cap

    index = lax.axis_index("ep")
    core = index % CORES
    expert_high = index // (CORES * shard_count)
    ids = jnp.stack(
        [(expert_high ^ m) * CORES + core for m in range(chunks)] + [core]
    ).astype(jnp.int32)

    def split(i):
        e, s = divmod(i, shard_count)
        return e // CORES, e % CORES, s // CORES, s % CORES

    def join(high, e_low, x, c):
        return ((high * CORES + e_low) * 2 + x) * CORES + c

    far = []
    for m in range(chunks):
        pairs = []
        for i in range(devices):
            high, e_low, x, c = split(i)
            pairs.append((i, join(high ^ m, c, x, e_low)))
        far.append(pairs)
    to_core = [(i, i ^ 1) for i in range(devices)]
    to_x = [(i, i ^ CORES) for i in range(devices)]

    def move(value, perm):
        return lax.ppermute(value, "ep", perm)

    other = move(tokens, to_core)
    routes = routes.T
    routes_other = move(routes, to_core)
    block = jax.ShapeDtypeStruct((pair, width), jnp.bfloat16)
    gain = norm_gain.reshape(1, width)
    normed, *blocks = vmem_call(
        functools.partial(select_kernel, experts=experts, cap=cap),
        [jax.ShapeDtypeStruct((CORES * rows, width), jnp.bfloat16)] + [block] * chunks,
        1,
        6,
    )(ids, tokens, other, routes, routes_other, gain)

    near = [move(blocks[m], far[m]) for m in range(chunks)]
    weights = jax.ShapeDtypeStruct((chunks * pair, CORES * rows), jnp.bfloat16)
    high, low = vmem_call(
        functools.partial(weight_kernel, experts=experts, cap=cap), [weights, weights], 1, 5
    )(ids, normed, router_weight.T, routes, routes_other)

    gate_up = gate_up_weight[0].T
    down = down_weight[0]
    back = []
    for m in range(chunks):
        side = move(near[m], to_x)
        near_other = move(near[m], to_core)
        side_other = move(side, to_core)
        mine, mine_side, send = vmem_call(
            functools.partial(expert_kernel, ff=ff),
            [block, block, jax.ShapeDtypeStruct((2 * pair, width), jnp.bfloat16)],
            0,
            6,
        )(near[m], side, near_other, side_other, gate_up, down)
        got = move(send, to_core)
        got_mine, got_side = got[:pair], got[pair:]
        out_side = (mine_side.astype(jnp.float32) + got_side.astype(jnp.float32)).astype(
            jnp.bfloat16
        )
        in_side = move(out_side, to_x)
        total = (
            mine.astype(jnp.float32) + got_mine.astype(jnp.float32) + in_side.astype(jnp.float32)
        ).astype(jnp.bfloat16)
        back.append(move(total, far[m]))

    mixed_own, mixed_other = vmem_call(
        combine_kernel,
        [
            jax.ShapeDtypeStruct((rows, width), jnp.float32),
            jax.ShapeDtypeStruct((rows, width), jnp.bfloat16),
        ],
        0,
        2 + chunks,
    )(high, low, *back)
    from_other = move(mixed_other, to_core)
    return (tokens.astype(jnp.float32) + mixed_own + from_other.astype(jnp.float32)).astype(
        jnp.bfloat16
    )


def solution(mesh):
    in_specs = (
        P(("groups", "ep"), None),
        P(("groups", "ep"), None),
        P(),
        P(),
        P("ep", None, None),
        P("ep", None, None),
    )
    out_specs = P(("groups", "ep"), None)
    return jax.shard_map(shards, mesh=mesh, in_specs=in_specs, out_specs=out_specs, check_vma=False)
```

time: 169 us -> 158 us (0.935)
  starting transfers between devices: 58.4 us -> 66 us
  waiting for transfers between devices: 65.9 us -> 59.2 us
  local copies, waits for them, and re-layouts: 9.46 us -> 4.08 us
  Pallas kernels: 29.6 us -> 26.5 us
  other arithmetic: 5.01 us -> 1.95 us
    ppermute x31, starting transfers between devices: 58.4 us -> 66 us  [move(): return lax.ppermute(value, 'ep', perm)]
    ppermute x31, waiting for transfers between devices: 65.9 us -> 59.2 us  [move(): return lax.ppermute(value, 'ep', perm)]
    unnamed x11 -> x14, local copies, waits for them, and re-layouts: 8.67 us -> 3.29 us
    convert_element_type x4, other arithmetic: 3.71 us -> 0.67 us  [shards(): total = (mine.astype(jnp.float32) + got_mine.astype(jnp.float32) + in_sid...]
  transfers between devices with their start and end apart: 31 -> 31, of which waited for: 10 -> 8; matrix products, arithmetic and copies ran while one was open for 7% -> 1% of each run, Pallas kernels for 15% -> 15%
where the time goes in v2:
time: 158 us
  starting transfers between devices  66 us (42%)
  waiting for transfers between devices  59.2 us (37%)
  Pallas kernels  26.5 us (17%)
  local copies, waits for them, and re-layouts  4.08 us (3%)
  other arithmetic  1.95 us (1%)
    ppermute x31, starting transfers between devices, move(): return lax.ppermute(value, 'ep', perm)  66 us
    ppermute x31, waiting for transfers between devices, move(): return lax.ppermute(value, 'ep', perm)  59.2 us
    pallas_call x4, Pallas kernels, shards(): vmem_call(functools.partial(expert_kernel, ff=ff), [block, block, jax.Sha...  23 us
    unnamed x14, local copies, waits for them, and re-layouts  3.29 us
  transfers between devices with their start and end apart: 31, of which 8 were waited for; matrix products, arithmetic and copies ran while one was open for 1% of the time, Pallas kernels for 15%

profile of v2, /device:TPU:13, one launch (start us, length us, event | category | flops | bytes accessed | tf_op | source)
XLA Modules:
  0.0 157.9 jit_solution(16951085073994655876)
XLA Ops:
  0.0 0.7 collective-permute-start
  0.7 0.7 reshape.3.gain
  1.4 0.1 stack.23.ids
  1.5 0.8 collective-permute-done.1.routes_other
  2.2 1.0 copy-done.2
  3.2 0.7 copy-done.5
  3.9 1.5 shard_map.64
  5.4 0.7 collective-permute-start.2
  6.1 0.2 collective-permute-start.9
  6.3 1.2 collective-permute-start.3
  7.5 2.3 %collective-permute-start.16 = (bf16[72,2880]{1,0:T(8,128)(2,1)S(1)}, bf16[72,2880]{1,0:T(8,128)(2,1)S(1)}, u32[]{:S(2)}, u32[]{:S(2)}) collective-permute-start(bf16[72,2880]{1,0:T(8,128)(2,1)S(1)} %get-tuple-element.37), channel_id=1, source_target_pairs={{0,16},{1,20},{2,18},{3,22},{4,17},{5,21},{6,19},{7,23},{8,24},{9,... | collective-permute-start | bytes 1244168 | tf_op jit(solution)/shard_map/ppermute | solution.py:155
  9.8 0.2 collective-permute-start.23
  10.0 10.0 %collective-permute-start.4 = (bf16[72,2880]{1,0:T(8,128)(2,1)S(1)}, bf16[72,2880]{1,0:T(8,128)(2,1)S(1)}, u32[]{:S(2)}, u32[]{:S(2)}) collective-permute-start(bf16[72,2880]{1,0:T(8,128)(2,1)S(1)} %collective-permute-done.2.a), channel_id=1, source_target_pairs={{0,1},{1,0},{2,3},{3,2},{4,5},{5,4},{6,7},{7,6},{8,9},{9,8},{10,11... | collective-permute-start | bytes 1244168 | tf_op jit(solution)/shard_map/ppermute | solution.py:155
  20.0 0.6 collective-permute-start.10
  20.6 0.0 collective-permute-done.3.b
  20.6 9.5 %collective-permute-start.5 = (bf16[72,2880]{1,0:T(8,128)(2,1)S(1)}, bf16[72,2880]{1,0:T(8,128)(2,1)S(1)}, u32[]{:S(2)}, u32[]{:S(2)}) collective-permute-start(bf16[72,2880]{1,0:T(8,128)(2,1)S(1)} %collective-permute-done.3.b), channel_id=1, source_target_pairs={{0,1},{1,0},{2,3},{3,2},{4,5},{5,4},{6,7},{7,6},{8,9},{9,8},{10,11... | collective-permute-start | bytes 1244168 | tf_op jit(solution)/shard_map/ppermute | solution.py:155
  30.1 12.5 %collective-permute-start.11 = (bf16[72,2880]{1,0:T(8,128)(2,1)S(1)}, bf16[72,2880]{1,0:T(8,128)(2,1)S(1)}, u32[]{:S(2)}, u32[]{:S(2)}) collective-permute-start(bf16[72,2880]{1,0:T(8,128)(2,1)S(1)} %collective-permute-done.9.a), channel_id=1, source_target_pairs={{0,1},{1,0},{2,3},{3,2},{4,5},{5,4},{6,7},{7,6},{8,9},{9,8},{10,11... | collective-permute-start | bytes 1244168 | tf_op jit(solution)/shard_map/ppermute | solution.py:155
  42.6 0.2 collective-permute-start.17
  42.8 1.2 collective-permute-start.24
  44.0 0.0 collective-permute-done.10.b
  44.0 7.3 %collective-permute-start.12 = (bf16[72,2880]{1,0:T(8,128)(2,1)S(1)}, bf16[72,2880]{1,0:T(8,128)(2,1)S(1)}, u32[]{:S(2)}, u32[]{:S(2)}) collective-permute-start(bf16[72,2880]{1,0:T(8,128)(2,1)S(1)} %collective-permute-done.10.b), channel_id=1, source_target_pairs={{0,1},{1,0},{2,3},{3,2},{4,5},{5,4},{6,7},{7,6},{8,9},{9,8},{10,11... | collective-permute-start | bytes 1244168 | tf_op jit(solution)/shard_map/ppermute | solution.py:155
  51.4 1.6 %copy-done = bf16[1,360,2880]{2,1,0:T(8,128)(2,1)S(1)} copy-done((bf16[1,360,2880]{2,1,0:T(8,128)(2,1)S(1)}, bf16[1,360,2880]{2,1,0:T(8,128)(2,1)}, u32[]{:S(2)}) %copy-start) | copy-done | bytes 2073624
  53.0 5.9 %shard_map.66 = (bf16[72,2880]{1,0:T(8,128)(2,1)S(1)}, bf16[72,2880]{1,0:T(8,128)(2,1)S(1)}, bf16[144,2880]{1,0:T(8,128)(2,1)S(1)}) custom-call(bf16[72,2880]{1,0:T(8,128)(2,1)S(1)} %collective-permute-done.2.a, bf16[72,2880]{1,0:T(8,128)(2,1)S(1)} %collective-permute-done.3.b, bf16[72,2880]{1,0:T(8,128)(2,1)S(1)} %collective-permute-done.4.c, ...), custom_call_target="tpu_custom_call" | custom-call | tf_op jit(solution)/shard_map/pallas_call | solution.py:182
  58.9 0.1 collective-permute-start.6
  58.9 0.5 collective-permute-start.18
  59.4 0.1 collective-permute-start.19
  59.5 4.3 %collective-permute-start.25 = (bf16[72,2880]{1,0:T(8,128)(2,1)S(1)}, bf16[72,2880]{1,0:T(8,128)(2,1)S(1)}, u32[]{:S(2)}, u32[]{:S(2)}) collective-permute-start(bf16[72,2880]{1,0:T(8,128)(2,1)S(1)} %collective-permute-done.23.a), channel_id=1, source_target_pairs={{0,1},{1,0},{2,3},{3,2},{4,5},{5,4},{6,7},{7,6},{8,9},{9,8},{10,11... | collective-permute-start | bytes 1244168 | tf_op jit(solution)/shard_map/ppermute | solution.py:155
  63.8 0.0 collective-permute-start.26
  63.9 5.7 %shard_map.67 = (bf16[72,2880]{1,0:T(8,128)(2,1)S(1)}, bf16[72,2880]{1,0:T(8,128)(2,1)S(1)}, bf16[144,2880]{1,0:T(8,128)(2,1)S(1)}) custom-call(bf16[72,2880]{1,0:T(8,128)(2,1)S(1)} %collective-permute-done.9.a, bf16[72,2880]{1,0:T(8,128)(2,1)S(1)} %collective-permute-done.10.b, bf16[72,2880]{1,0:T(8,128)(2,1)S(1)} %collective-permute-done.11.c, ...), custom_call_target="tpu_custom_call" | custom-call | tf_op jit(solution)/shard_map/pallas_call | solution.py:182
  69.6 0.6 collective-permute-start.13
  70.2 5.7 %shard_map.68 = (bf16[72,2880]{1,0:T(8,128)(2,1)S(1)}, bf16[72,2880]{1,0:T(8,128)(2,1)S(1)}, bf16[144,2880]{1,0:T(8,128)(2,1)S(1)}) custom-call(bf16[72,2880]{1,0:T(8,128)(2,1)S(1)} %collective-permute-done.16.a, bf16[72,2880]{1,0:T(8,128)(2,1)S(1)} %collective-permute-done.17.b, bf16[72,2880]{1,0:T(8,128)(2,1)S(1)} %collective-permute-done.18.c, ...), custom_call_target="tpu_custom_call" | custom-call | tf_op jit(solution)/shard_map/pallas_call | solution.py:182
  75.9 0.1 collective-permute-start.20
  76.0 5.7 %shard_map.69 = (bf16[72,2880]{1,0:T(8,128)(2,1)S(1)}, bf16[72,2880]{1,0:T(8,128)(2,1)S(1)}, bf16[144,2880]{1,0:T(8,128)(2,1)S(1)}) custom-call(bf16[72,2880]{1,0:T(8,128)(2,1)S(1)} %collective-permute-done.23.a, bf16[72,2880]{1,0:T(8,128)(2,1)S(1)} %collective-permute-done.24.b, bf16[72,2880]{1,0:T(8,128)(2,1)S(1)} %collective-permute-done.25.c, ...), custom_call_target="tpu_custom_call" | custom-call | tf_op jit(solution)/shard_map/pallas_call | solution.py:182
  81.7 0.5 collective-permute-start.27
  82.3 0.1 add_convert_fusion.7
  82.4 0.3 collective-permute-start.7
  82.7 0.1 add_convert_fusion.5
  82.8 1.3 collective-permute-start.14
  84.1 0.1 add_convert_fusion.3
  84.2 0.0 copy-start.4
  84.2 0.0 copy-start.6
  84.2 0.3 collective-permute-start.21
  84.5 0.1 add_convert_fusion.1
  84.7 1.3 collective-permute-start.28
  85.9 7.8 %collective-permute-done.7 = bf16[72,2880]{1,0:T(8,128)(2,1)S(1)} collective-permute-done((bf16[72,2880]{1,0:T(8,128)(2,1)S(1)}, bf16[72,2880]{1,0:T(8,128)(2,1)S(1)}, u32[]{:S(2)}, u32[]{:S(2)}) %collective-permute-start.7) | collective-permute-done | bytes 414752 | tf_op jit(solution)/shard_map/ppermute | solution.py:155
  93.7 0.2 add_convert_fusion.6
  93.9 0.0 copy-start.3
  93.9 0.8 collective-permute-start.8
  94.8 8.1 %collective-permute-done.14 = bf16[72,2880]{1,0:T(8,128)(2,1)S(1)} collective-permute-done((bf16[72,2880]{1,0:T(8,128)(2,1)S(1)}, bf16[72,2880]{1,0:T(8,128)(2,1)S(1)}, u32[]{:S(2)}, u32[]{:S(2)}) %collective-permute-start.14) | collective-permute-done | bytes 414752 | tf_op jit(solution)/shard_map/ppermute | solution.py:155
  102.8 0.2 add_convert_fusion.4
  103.0 3.5 %collective-permute-start.15 = (bf16[72,2880]{1,0:T(8,128)(2,1)S(1)}, bf16[72,2880]{1,0:T(8,128)(2,1)S(1)}, u32[]{:S(2)}, u32[]{:S(2)}) collective-permute-start(bf16[72,2880]{1,0:T(8,128)(2,1)S(1)} %add_convert_fusion.4), channel_id=1, source_target_pairs={{0,8},{1,12},{2,10},{3,14},{4,9},{5,13},{6,11},{7,15},{8,0},{9,4},... | collective-permute-start | bytes 1244168 | tf_op jit(solution)/shard_map/ppermute | solution.py:155
  106.5 5.4 %collective-permute-done.21 = bf16[72,2880]{1,0:T(8,128)(2,1)S(1)} collective-permute-done((bf16[72,2880]{1,0:T(8,128)(2,1)S(1)}, bf16[72,2880]{1,0:T(8,128)(2,1)S(1)}, u32[]{:S(2)}, u32[]{:S(2)}) %collective-permute-start.21) | collective-permute-done | bytes 414752 | tf_op jit(solution)/shard_map/ppermute | solution.py:155
  111.9 0.2 add_convert_fusion.2
  112.1 4.5 %collective-permute-start.22 = (bf16[72,2880]{1,0:T(8,128)(2,1)S(1)}, bf16[72,2880]{1,0:T(8,128)(2,1)S(1)}, u32[]{:S(2)}, u32[]{:S(2)}) collective-permute-start(bf16[72,2880]{1,0:T(8,128)(2,1)S(1)} %add_convert_fusion.2), channel_id=1, source_target_pairs={{0,16},{1,20},{2,18},{3,22},{4,17},{5,21},{6,19},{7,23},{8,24},{9,... | collective-permute-start | bytes 1244168 | tf_op jit(solution)/shard_map/ppermute | solution.py:155
  116.6 4.4 %collective-permute-done.28 = bf16[72,2880]{1,0:T(8,128)(2,1)S(1)} collective-permute-done((bf16[72,2880]{1,0:T(8,128)(2,1)S(1)}, bf16[72,2880]{1,0:T(8,128)(2,1)S(1)}, u32[]{:S(2)}, u32[]{:S(2)}) %collective-permute-start.28) | collective-permute-done | bytes 414752 | tf_op jit(solution)/shard_map/ppermute | solution.py:155
  121.0 0.2 add_convert_fusion
  121.2 0.2 collective-permute-start.29
  121.4 1.0 shard_map.65
  122.4 20.7 %collective-permute-done.22.refs_2_ = bf16[72,2880]{1,0:T(8,128)(2,1)S(1)} collective-permute-done((bf16[72,2880]{1,0:T(8,128)(2,1)S(1)}, bf16[72,2880]{1,0:T(8,128)(2,1)S(1)}, u32[]{:S(2)}, u32[]{:S(2)}) %collective-permute-start.22) | collective-permute-done | bytes 414752 | tf_op jit(solution)/shard_map/ppermute | solution.py:155
  143.1 10.7 %collective-permute-done.29.refs_3_ = bf16[72,2880]{1,0:T(8,128)(2,1)S(1)} collective-permute-done((bf16[72,2880]{1,0:T(8,128)(2,1)S(1)}, bf16[72,2880]{1,0:T(8,128)(2,1)S(1)}, u32[]{:S(2)}, u32[]{:S(2)}) %collective-permute-start.29) | collective-permute-done | bytes 414752 | tf_op jit(solution)/shard_map/ppermute | solution.py:155
  153.8 1.0 shard_map.70
  154.8 0.9 collective-permute-start.30
  155.7 1.3 collective-permute-done.30
  157.1 0.9 add_convert_fusion.8
  (30 shorter events, 0.1 us)
Async XLA Ops:
  0.0 2.2 %collective-permute-start = (bf16[64,2880]{1,0:T(8,128)(2,1)}, bf16[64,2880]{1,0:T(8,128)(2,1)S(1)}, u32[]{:S(2)}, u32[]{:S(2)}) collective-permute-start(bf16[64,2880]{1,0:T(8,128)(2,1)} %own.1), channel_id=1, source_target_pairs={{0,1},{1,0},{2,3},{3,2},{4,5},{5,4},{6,7},{7,6},{8,9},{9,8},{10,11... | collective-permute-start | bytes 1105928 | tf_op jit(solution)/shard_map/ppermute | solution.py:155
  0.7 1.5 collective-permute-start.1
  2.2 1.0 copy-start.2
  3.2 0.7 copy-start.5
  5.4 0.9 collective-permute-start.2
  6.1 13.9 %collective-permute-start.9 = (bf16[72,2880]{1,0:T(8,128)(2,1)S(1)}, bf16[72,2880]{1,0:T(8,128)(2,1)S(1)}, u32[]{:S(2)}, u32[]{:S(2)}) collective-permute-start(bf16[72,2880]{1,0:T(8,128)(2,1)S(1)} %get-tuple-element.33), channel_id=1, source_target_pairs={{0,8},{1,12},{2,10},{3,14},{4,9},{5,13},{6,11},{7,15},{8,0},{9,4},... | collective-permute-start | bytes 1244168 | tf_op jit(solution)/shard_map/ppermute | solution.py:155
  6.3 14.3 %collective-permute-start.3 = (bf16[72,2880]{1,0:T(8,128)(2,1)S(1)}, bf16[72,2880]{1,0:T(8,128)(2,1)S(1)}, u32[]{:S(2)}, u32[]{:S(2)}) collective-permute-start(bf16[72,2880]{1,0:T(8,128)(2,1)S(1)} %collective-permute-done.2.a), channel_id=1, source_target_pairs={{0,2},{1,3},{2,0},{3,1},{4,6},{5,7},{6,4},{7,5},{8,10},{9,11},{10,... | collective-permute-start | bytes 1244168 | tf_op jit(solution)/shard_map/ppermute | solution.py:155
  7.5 22.6 %collective-permute-start.16 = (bf16[72,2880]{1,0:T(8,128)(2,1)S(1)}, bf16[72,2880]{1,0:T(8,128)(2,1)S(1)}, u32[]{:S(2)}, u32[]{:S(2)}) collective-permute-start(bf16[72,2880]{1,0:T(8,128)(2,1)S(1)} %get-tuple-element.37), channel_id=1, source_target_pairs={{0,16},{1,20},{2,18},{3,22},{4,17},{5,21},{6,19},{7,23},{8,24},{9,... | collective-permute-start | bytes 1244168 | tf_op jit(solution)/shard_map/ppermute | solution.py:155
  9.8 32.7 %collective-permute-start.23 = (bf16[72,2880]{1,0:T(8,128)(2,1)S(1)}, bf16[72,2880]{1,0:T(8,128)(2,1)S(1)}, u32[]{:S(2)}, u32[]{:S(2)}) collective-permute-start(bf16[72,2880]{1,0:T(8,128)(2,1)S(1)} %get-tuple-element.41), channel_id=1, source_target_pairs={{0,24},{1,28},{2,26},{3,30},{4,25},{5,29},{6,27},{7,31},{8,16},{9,... | collective-permute-start | bytes 1244168 | tf_op jit(solution)/shard_map/ppermute | solution.py:155
  10.0 32.8 %collective-permute-start.4 = (bf16[72,2880]{1,0:T(8,128)(2,1)S(1)}, bf16[72,2880]{1,0:T(8,128)(2,1)S(1)}, u32[]{:S(2)}, u32[]{:S(2)}) collective-permute-start(bf16[72,2880]{1,0:T(8,128)(2,1)S(1)} %collective-permute-done.2.a), channel_id=1, source_target_pairs={{0,1},{1,0},{2,3},{3,2},{4,5},{5,4},{6,7},{7,6},{8,9},{9,8},{10,11... | collective-permute-start | bytes 1244168 | tf_op jit(solution)/shard_map/ppermute | solution.py:155
  20.0 24.1 %collective-permute-start.10 = (bf16[72,2880]{1,0:T(8,128)(2,1)S(1)}, bf16[72,2880]{1,0:T(8,128)(2,1)S(1)}, u32[]{:S(2)}, u32[]{:S(2)}) collective-permute-start(bf16[72,2880]{1,0:T(8,128)(2,1)S(1)} %collective-permute-done.9.a), channel_id=1, source_target_pairs={{0,2},{1,3},{2,0},{3,1},{4,6},{5,7},{6,4},{7,5},{8,10},{9,11},{10,... | collective-permute-start | bytes 1244168 | tf_op jit(solution)/shard_map/ppermute | solution.py:155
  20.6 30.8 %collective-permute-start.5 = (bf16[72,2880]{1,0:T(8,128)(2,1)S(1)}, bf16[72,2880]{1,0:T(8,128)(2,1)S(1)}, u32[]{:S(2)}, u32[]{:S(2)}) collective-permute-start(bf16[72,2880]{1,0:T(8,128)(2,1)S(1)} %collective-permute-done.3.b), channel_id=1, source_target_pairs={{0,1},{1,0},{2,3},{3,2},{4,5},{5,4},{6,7},{7,6},{8,9},{9,8},{10,11... | collective-permute-start | bytes 1244168 | tf_op jit(solution)/shard_map/ppermute | solution.py:155
  30.1 28.9 %collective-permute-start.11 = (bf16[72,2880]{1,0:T(8,128)(2,1)S(1)}, bf16[72,2880]{1,0:T(8,128)(2,1)S(1)}, u32[]{:S(2)}, u32[]{:S(2)}) collective-permute-start(bf16[72,2880]{1,0:T(8,128)(2,1)S(1)} %collective-permute-done.9.a), channel_id=1, source_target_pairs={{0,1},{1,0},{2,3},{3,2},{4,5},{5,4},{6,7},{7,6},{8,9},{9,8},{10,11... | collective-permute-start | bytes 1244168 | tf_op jit(solution)/shard_map/ppermute | solution.py:155
  42.6 16.9 %collective-permute-start.17 = (bf16[72,2880]{1,0:T(8,128)(2,1)S(1)}, bf16[72,2880]{1,0:T(8,128)(2,1)S(1)}, u32[]{:S(2)}, u32[]{:S(2)}) collective-permute-start(bf16[72,2880]{1,0:T(8,128)(2,1)S(1)} %collective-permute-done.16.a), channel_id=1, source_target_pairs={{0,2},{1,3},{2,0},{3,1},{4,6},{5,7},{6,4},{7,5},{8,10},{9,11},{10,... | collective-permute-start | bytes 1244168 | tf_op jit(solution)/shard_map/ppermute | solution.py:155
  42.8 16.7 %collective-permute-start.24 = (bf16[72,2880]{1,0:T(8,128)(2,1)S(1)}, bf16[72,2880]{1,0:T(8,128)(2,1)S(1)}, u32[]{:S(2)}, u32[]{:S(2)}) collective-permute-start(bf16[72,2880]{1,0:T(8,128)(2,1)S(1)} %collective-permute-done.23.a), channel_id=1, source_target_pairs={{0,2},{1,3},{2,0},{3,1},{4,6},{5,7},{6,4},{7,5},{8,10},{9,11},{10,... | collective-permute-start | bytes 1244168 | tf_op jit(solution)/shard_map/ppermute | solution.py:155
  44.0 19.8 %collective-permute-start.12 = (bf16[72,2880]{1,0:T(8,128)(2,1)S(1)}, bf16[72,2880]{1,0:T(8,128)(2,1)S(1)}, u32[]{:S(2)}, u32[]{:S(2)}) collective-permute-start(bf16[72,2880]{1,0:T(8,128)(2,1)S(1)} %collective-permute-done.10.b), channel_id=1, source_target_pairs={{0,1},{1,0},{2,3},{3,2},{4,5},{5,4},{6,7},{7,6},{8,9},{9,8},{10,11... | collective-permute-start | bytes 1244168 | tf_op jit(solution)/shard_map/ppermute | solution.py:155
  51.4 1.6 %copy-start = (bf16[1,360,2880]{2,1,0:T(8,128)(2,1)S(1)}, bf16[1,360,2880]{2,1,0:T(8,128)(2,1)}, u32[]{:S(2)}) copy-start(bf16[1,360,2880]{2,1,0:T(8,128)(2,1)} %param.11) | copy-start | bytes 6220804
  53.0 10.9 %copy-start.1 = (bf16[1,360,2880]{2,1,0:T(8,128)(2,1)S(1)}, bf16[1,360,2880]{2,1,0:T(8,128)(2,1)}, u32[]{:S(2)}) copy-start(bf16[1,360,2880]{2,1,0:T(8,128)(2,1)} %param.11) | copy-start | bytes 6220804
  58.9 23.4 %collective-permute-start.6 = (bf16[144,2880]{1,0:T(8,128)(2,1)S(1)}, bf16[144,2880]{1,0:T(8,128)(2,1)S(1)}, u32[]{:S(2)}, u32[]{:S(2)}) collective-permute-start(bf16[144,2880]{1,0:T(8,128)(2,1)S(1)} %get-tuple-element.31), channel_id=1, source_target_pairs={{0,1},{1,0},{2,3},{3,2},{4,5},{5,4},{6,7},{7,6},{8,9},{9,8},{10,11... | collective-permute-start | bytes 2488328 | tf_op jit(solution)/shard_map/ppermute | solution.py:155
  58.9 10.6 %collective-permute-start.18 = (bf16[72,2880]{1,0:T(8,128)(2,1)S(1)}, bf16[72,2880]{1,0:T(8,128)(2,1)S(1)}, u32[]{:S(2)}, u32[]{:S(2)}) collective-permute-start(bf16[72,2880]{1,0:T(8,128)(2,1)S(1)} %collective-permute-done.16.a), channel_id=1, source_target_pairs={{0,1},{1,0},{2,3},{3,2},{4,5},{5,4},{6,7},{7,6},{8,9},{9,8},{10,11... | collective-permute-start | bytes 1244168 | tf_op jit(solution)/shard_map/ppermute | solution.py:155
  59.4 10.7 %collective-permute-start.19 = (bf16[72,2880]{1,0:T(8,128)(2,1)S(1)}, bf16[72,2880]{1,0:T(8,128)(2,1)S(1)}, u32[]{:S(2)}, u32[]{:S(2)}) collective-permute-start(bf16[72,2880]{1,0:T(8,128)(2,1)S(1)} %collective-permute-done.17.b), channel_id=1, source_target_pairs={{0,1},{1,0},{2,3},{3,2},{4,5},{5,4},{6,7},{7,6},{8,9},{9,8},{10,11... | collective-permute-start | bytes 1244168 | tf_op jit(solution)/shard_map/ppermute | solution.py:155
  59.5 16.5 %collective-permute-start.25 = (bf16[72,2880]{1,0:T(8,128)(2,1)S(1)}, bf16[72,2880]{1,0:T(8,128)(2,1)S(1)}, u32[]{:S(2)}, u32[]{:S(2)}) collective-permute-start(bf16[72,2880]{1,0:T(8,128)(2,1)S(1)} %collective-permute-done.23.a), channel_id=1, source_target_pairs={{0,1},{1,0},{2,3},{3,2},{4,5},{5,4},{6,7},{7,6},{8,9},{9,8},{10,11... | collective-permute-start | bytes 1244168 | tf_op jit(solution)/shard_map/ppermute | solution.py:155
  63.8 12.1 %collective-permute-start.26 = (bf16[72,2880]{1,0:T(8,128)(2,1)S(1)}, bf16[72,2880]{1,0:T(8,128)(2,1)S(1)}, u32[]{:S(2)}, u32[]{:S(2)}) collective-permute-start(bf16[72,2880]{1,0:T(8,128)(2,1)S(1)} %collective-permute-done.24.b), channel_id=1, source_target_pairs={{0,1},{1,0},{2,3},{3,2},{4,5},{5,4},{6,7},{7,6},{8,9},{9,8},{10,11... | collective-permute-start | bytes 1244168 | tf_op jit(solution)/shard_map/ppermute | solution.py:155
  69.6 13.1 %collective-permute-start.13 = (bf16[144,2880]{1,0:T(8,128)(2,1)S(1)}, bf16[144,2880]{1,0:T(8,128)(2,1)S(1)}, u32[]{:S(2)}, u32[]{:S(2)}) collective-permute-start(bf16[144,2880]{1,0:T(8,128)(2,1)S(1)} %get-tuple-element.35), channel_id=1, source_target_pairs={{0,1},{1,0},{2,3},{3,2},{4,5},{5,4},{6,7},{7,6},{8,9},{9,8},{10,11... | collective-permute-start | bytes 2488328 | tf_op jit(solution)/shard_map/ppermute | solution.py:155
  75.9 8.2 %collective-permute-start.20 = (bf16[144,2880]{1,0:T(8,128)(2,1)S(1)}, bf16[144,2880]{1,0:T(8,128)(2,1)S(1)}, u32[]{:S(2)}, u32[]{:S(2)}) collective-permute-start(bf16[144,2880]{1,0:T(8,128)(2,1)S(1)} %get-tuple-element.39), channel_id=1, source_target_pairs={{0,1},{1,0},{2,3},{3,2},{4,5},{5,4},{6,7},{7,6},{8,9},{9,8},{10,11... | collective-permute-start | bytes 2488328 | tf_op jit(solution)/shard_map/ppermute | solution.py:155
  81.7 2.8 %collective-permute-start.27 = (bf16[144,2880]{1,0:T(8,128)(2,1)S(1)}, bf16[144,2880]{1,0:T(8,128)(2,1)S(1)}, u32[]{:S(2)}, u32[]{:S(2)}) collective-permute-start(bf16[144,2880]{1,0:T(8,128)(2,1)S(1)} %get-tuple-element.43), channel_id=1, source_target_pairs={{0,1},{1,0},{2,3},{3,2},{4,5},{5,4},{6,7},{7,6},{8,9},{9,8},{10,11... | collective-permute-start | bytes 2488328 | tf_op jit(solution)/shard_map/ppermute | solution.py:155
  82.4 11.4 %collective-permute-start.7 = (bf16[72,2880]{1,0:T(8,128)(2,1)S(1)}, bf16[72,2880]{1,0:T(8,128)(2,1)S(1)}, u32[]{:S(2)}, u32[]{:S(2)}) collective-permute-start(bf16[72,2880]{1,0:T(8,128)(2,1)S(1)} %add_convert_fusion.7), channel_id=1, source_target_pairs={{0,2},{1,3},{2,0},{3,1},{4,6},{5,7},{6,4},{7,5},{8,10},{9,11},{10,... | collective-permute-start | bytes 1244168 | tf_op jit(solution)/shard_map/ppermute | solution.py:155
  82.8 20.0 %collective-permute-start.14 = (bf16[72,2880]{1,0:T(8,128)(2,1)S(1)}, bf16[72,2880]{1,0:T(8,128)(2,1)S(1)}, u32[]{:S(2)}, u32[]{:S(2)}) collective-permute-start(bf16[72,2880]{1,0:T(8,128)(2,1)S(1)} %add_convert_fusion.5), channel_id=1, source_target_pairs={{0,2},{1,3},{2,0},{3,1},{4,6},{5,7},{6,4},{7,5},{8,10},{9,11},{10,... | collective-permute-start | bytes 1244168 | tf_op jit(solution)/shard_map/ppermute | solution.py:155
  84.2 37.2 %copy-start.4 = (bf16[2880,8]{0,1:T(8,128)(2,1)S(1)}, bf16[2880,8]{0,1:T(8,128)(2,1)}, u32[]{:S(2)}) copy-start(bf16[2880,8]{0,1:T(8,128)(2,1)} %param.9) | copy-start | bytes 138244
  84.2 37.2 %copy-start.6 = (s32[64,4]{0,1:T(4,128)S(1)}, s32[64,4]{0,1:T(4,128)}, u32[]{:S(2)}) copy-start(s32[64,4]{0,1:T(4,128)} %param.7) | copy-start | bytes 3076
  84.2 27.7 %collective-permute-start.21 = (bf16[72,2880]{1,0:T(8,128)(2,1)S(1)}, bf16[72,2880]{1,0:T(8,128)(2,1)S(1)}, u32[]{:S(2)}, u32[]{:S(2)}) collective-permute-start(bf16[72,2880]{1,0:T(8,128)(2,1)S(1)} %add_convert_fusion.3), channel_id=1, source_target_pairs={{0,2},{1,3},{2,0},{3,1},{4,6},{5,7},{6,4},{7,5},{8,10},{9,11},{10,... | collective-permute-start | bytes 1244168 | tf_op jit(solution)/shard_map/ppermute | solution.py:155
  84.7 36.3 %collective-permute-start.28 = (bf16[72,2880]{1,0:T(8,128)(2,1)S(1)}, bf16[72,2880]{1,0:T(8,128)(2,1)S(1)}, u32[]{:S(2)}, u32[]{:S(2)}) collective-permute-start(bf16[72,2880]{1,0:T(8,128)(2,1)S(1)} %add_convert_fusion.1), channel_id=1, source_target_pairs={{0,2},{1,3},{2,0},{3,1},{4,6},{5,7},{6,4},{7,5},{8,10},{9,11},{10,... | collective-permute-start | bytes 1244168 | tf_op jit(solution)/shard_map/ppermute | solution.py:155
  93.9 63.2 %copy-start.3 = (bf16[64,2880]{1,0:T(8,128)(2,1)S(1)}, bf16[64,2880]{1,0:T(8,128)(2,1)}, u32[]{:S(2)}) copy-start(bf16[64,2880]{1,0:T(8,128)(2,1)} %own.1) | copy-start | bytes 1105924
  93.9 28.5 %collective-permute-start.8 = (bf16[72,2880]{1,0:T(8,128)(2,1)S(1)}, bf16[72,2880]{1,0:T(8,128)(2,1)S(1)}, u32[]{:S(2)}, u32[]{:S(2)}) collective-permute-start(bf16[72,2880]{1,0:T(8,128)(2,1)S(1)} %add_convert_fusion.6), channel_id=1, source_target_pairs={{0,0},{1,4},{2,2},{3,6},{4,1},{5,5},{6,3},{7,7},{8,8},{9,12},{10,1... | collective-permute-start | bytes 1244168 | tf_op jit(solution)/shard_map/ppermute | solution.py:155
  103.0 19.4 %collective-permute-start.15 = (bf16[72,2880]{1,0:T(8,128)(2,1)S(1)}, bf16[72,2880]{1,0:T(8,128)(2,1)S(1)}, u32[]{:S(2)}, u32[]{:S(2)}) collective-permute-start(bf16[72,2880]{1,0:T(8,128)(2,1)S(1)} %add_convert_fusion.4), channel_id=1, source_target_pairs={{0,8},{1,12},{2,10},{3,14},{4,9},{5,13},{6,11},{7,15},{8,0},{9,4},... | collective-permute-start | bytes 1244168 | tf_op jit(solution)/shard_map/ppermute | solution.py:155
  112.1 31.0 %collective-permute-start.22 = (bf16[72,2880]{1,0:T(8,128)(2,1)S(1)}, bf16[72,2880]{1,0:T(8,128)(2,1)S(1)}, u32[]{:S(2)}, u32[]{:S(2)}) collective-permute-start(bf16[72,2880]{1,0:T(8,128)(2,1)S(1)} %add_convert_fusion.2), channel_id=1, source_target_pairs={{0,16},{1,20},{2,18},{3,22},{4,17},{5,21},{6,19},{7,23},{8,24},{9,... | collective-permute-start | bytes 1244168 | tf_op jit(solution)/shard_map/ppermute | solution.py:155
  121.2 32.6 %collective-permute-start.29 = (bf16[72,2880]{1,0:T(8,128)(2,1)S(1)}, bf16[72,2880]{1,0:T(8,128)(2,1)S(1)}, u32[]{:S(2)}, u32[]{:S(2)}) collective-permute-start(bf16[72,2880]{1,0:T(8,128)(2,1)S(1)} %add_convert_fusion), channel_id=1, source_target_pairs={{0,24},{1,28},{2,26},{3,30},{4,25},{5,29},{6,27},{7,31},{8,16},{9,... | collective-permute-start | bytes 1244168 | tf_op jit(solution)/shard_map/ppermute | solution.py:155
  154.8 2.3 %collective-permute-start.30 = (bf16[64,2880]{1,0:T(8,128)(2,1)S(1)}, bf16[64,2880]{1,0:T(8,128)(2,1)S(1)}, u32[]{:S(2)}, u32[]{:S(2)}) collective-permute-start(bf16[64,2880]{1,0:T(8,128)(2,1)S(1)} %get-tuple-element.46), channel_id=1, source_target_pairs={{0,1},{1,0},{2,3},{3,2},{4,5},{5,4},{6,7},{7,6},{8,9},{9,8},{10,11... | collective-permute-start | bytes 1105928 | tf_op jit(solution)/shard_map/ppermute | solution.py:155

commit v3 on v2

v3 whole, which is shorter than its diff:
```python
import functools

import jax
import jax.numpy as jnp
from jax import lax
from jax.experimental import pallas as pl
from jax.experimental.pallas import tpu as pltpu
from jax.sharding import PartitionSpec as P


CORES = 2
SHARDS = 4
NEAR = 2
VMEM_BYTES = 48 * 1024 * 1024


def dot32(a, b, dims=((1,), (0,))):
    return lax.dot_general(a, b, (dims, ((), ())), preferred_element_type=jnp.float32)


def places_of(routes_by_core, own_core, experts, cap):
    places = []
    for routes, core in zip(routes_by_core, (own_core, 1 - own_core)):
        rows = routes.shape[1]
        ids = lax.broadcasted_iota(jnp.int32, (experts, rows), 0)
        hits = (routes[0:1, :] == ids).astype(jnp.float32)
        for k in range(1, routes.shape[0]):
            hits = hits + (routes[k : k + 1, :] == ids).astype(jnp.float32)
        before = (
            lax.broadcasted_iota(jnp.int32, (rows, rows), 0)
            < lax.broadcasted_iota(jnp.int32, (rows, rows), 1)
        ).astype(jnp.bfloat16)
        slot = dot32(hits.astype(jnp.bfloat16), before).astype(jnp.int32)
        places.append(jnp.where(hits > 0.5, slot + core * cap + 1, 0))
    return jnp.concatenate(places, axis=1)


def at_rows(value, expert):
    mine = lax.broadcasted_iota(jnp.int32, value.shape, 0) == expert
    return jnp.sum(jnp.where(mine, value, jnp.zeros_like(value)), axis=0, keepdims=True)


def normed_of(tokens, gain):
    stream = tokens.astype(jnp.float32)
    mean_square = jnp.mean(stream * stream, axis=-1, keepdims=True)
    return (stream * lax.rsqrt(mean_square + 1e-05) * gain).astype(jnp.bfloat16)


def block_rows(rows, tokens):
    return lax.broadcasted_iota(jnp.int32, (rows, tokens), 0) + 1


def select_far(ids, own, other, routes_own, routes_other, gain, normed, *blocks, experts, cap):
    rows = own.shape[0]
    scale = gain[...].astype(jnp.float32)
    normed[0:rows, :] = normed_of(own[...], scale)
    normed[rows:, :] = normed_of(other[...], scale)
    place = places_of((routes_own[...], routes_other[...]), ids[NEAR + len(blocks)], experts, cap)
    values = normed[...]
    slots = block_rows(CORES * cap, CORES * rows)
    for m, block in enumerate(blocks):
        pick = (slots == at_rows(place, ids[NEAR + m])).astype(jnp.bfloat16)
        block[...] = dot32(pick, values).astype(jnp.bfloat16)


def both_places(ids_core, routes, routes_side, experts, cap):
    top = routes.shape[0] // CORES
    place = places_of((routes[:top, :], routes[top:, :]), ids_core, experts, cap)
    side = places_of((routes_side[:top, :], routes_side[top:, :]), ids_core, experts, cap)
    side = jnp.where(side > 0, side + CORES * cap, 0)
    return place, side


def select_near(ids, normed, side, side_other, routes, routes_side, gain, *refs, experts, cap):
    all_normed, blocks = refs[0], refs[1:]
    rows = side.shape[0]
    scale = gain[...].astype(jnp.float32)
    all_normed[0 : 2 * rows, :] = normed[...]
    all_normed[2 * rows : 3 * rows, :] = normed_of(side[...], scale)
    all_normed[3 * rows :, :] = normed_of(side_other[...], scale)
    core = ids[ids.shape[0] - 1]
    place = jnp.concatenate(both_places(core, routes[...], routes_side[...], experts, cap), axis=1)
    values = all_normed[...]
    slots = block_rows(2 * CORES * cap, 2 * CORES * rows)
    for m, block in enumerate(blocks):
        pick = (slots == at_rows(place, ids[m])).astype(jnp.bfloat16)
        block[...] = dot32(pick, values).astype(jnp.bfloat16)


def store_weight(high, low, at, weight):
    first = weight.astype(jnp.bfloat16)
    high[at, :] = first
    low[at, :] = (weight - first.astype(jnp.float32)).astype(jnp.bfloat16)


def weight_kernel(ids, normed, router, routes, routes_side, *refs, experts, cap):
    near_high, near_low, far_high, far_low = refs
    pair = CORES * cap
    core = ids[ids.shape[0] - 1]
    tokens = far_high.shape[1]
    logits = dot32(router[...], normed[...], ((1,), (1,)))
    own_place, side_place = both_places(core, routes[...], routes_side[...], experts, cap)
    place = jnp.concatenate([own_place, side_place], axis=1)
    expo = jnp.where(place > 0, jnp.exp(logits), 0.0)
    prob = expo / jnp.sum(expo, axis=0, keepdims=True)
    slots = block_rows(2 * pair, 2 * tokens)
    for m in range(NEAR):
        here = slots == at_rows(place, ids[m])
        weight = jnp.where(here, at_rows(prob, ids[m]), 0.0)
        store_weight(near_high, near_low, slice(m * 2 * pair, (m + 1) * 2 * pair), weight)
    slots = block_rows(pair, tokens)
    for m in range(far_high.shape[0] // pair):
        here = slots == at_rows(own_place, ids[NEAR + m])
        weight = jnp.where(here, at_rows(prob[:, :tokens], ids[NEAR + m]), 0.0)
        store_weight(far_high, far_low, slice(m * pair, (m + 1) * pair), weight)


def expert_kernel(*refs, ff, blocks):
    gate_up, down = refs[blocks], refs[blocks + 1]
    mine, send = refs[blocks + 2 : -1], refs[-1]
    values = jnp.concatenate([r[...] for r in refs[:blocks]], axis=0)
    hidden = dot32(values, gate_up[...], ((1,), (1,)))
    gate = hidden[:, :ff]
    up = hidden[:, ff:]
    activated = ((up + 1.0) * gate * jax.nn.sigmoid(1.702 * gate)).astype(jnp.bfloat16)
    partial_value = dot32(activated, down[...]).astype(jnp.bfloat16)
    at = 0
    for r in (*mine, send):
        r[...] = partial_value[at : at + r.shape[0]]
        at = at + r.shape[0]


def weighted(high, low, values):
    values = jnp.concatenate([r[...] for r in values], axis=0)
    dims = ((0,), (0,))
    return dot32(high[...], values, dims) + dot32(low[...], values, dims)


def combine_near(high, low, *refs):
    mixture = weighted(high, low, refs[:NEAR])
    at = 0
    for r in refs[NEAR:]:
        r[...] = mixture[at : at + r.shape[0]].astype(r.dtype)
        at = at + r.shape[0]


def combine_far(high, low, near_own, near_other, *refs):
    mixed_own, mixed_other = refs[-2], refs[-1]
    mixture = weighted(high, low, refs[:-2])
    rows = mixed_own.shape[0]
    mixed_own[...] = mixture[:rows] + near_own[...]
    mixed_other[...] = (mixture[rows:] + near_other[...]).astype(jnp.bfloat16)


def vmem_call(kernel, out_shape, scalars=0, count=0):
    specs = [pl.BlockSpec(memory_space=pltpu.SMEM)] * scalars
    specs = specs + [pl.BlockSpec(memory_space=pltpu.VMEM)] * (count - scalars)
    return pl.pallas_call(
        kernel,
        out_shape=out_shape,
        in_specs=specs,
        out_specs=jax.tree.map(lambda _: pl.BlockSpec(memory_space=pltpu.VMEM), out_shape),
        compiler_params=pltpu.CompilerParams(vmem_limit_bytes=VMEM_BYTES),
    )


def shards(tokens, routes, norm_gain, router_weight, gate_up_weight, down_weight):
    rows, width = tokens.shape
    top = routes.shape[1]
    experts = router_weight.shape[1]
    devices = lax.axis_size("ep")
    shard_count = devices // experts
    if shard_count != SHARDS or experts % CORES:
        raise ValueError("unsupported mesh")
    ff = down_weight.shape[1]
    cap = min(rows, shard_count * (17 * rows * top // (16 * experts * shard_count) + 1))
    chunks = experts // CORES
    pair = CORES * cap

    index = lax.axis_index("ep")
    core = index % CORES
    expert_high = index // (CORES * shard_count)
    ids = jnp.stack(
        [(expert_high ^ m) * CORES + core for m in range(chunks)] + [core]
    ).astype(jnp.int32)

    def split(i):
        e, s = divmod(i, shard_count)
        return e // CORES, e % CORES, s // CORES, s % CORES

    def join(high, e_low, x, c):
        return ((high * CORES + e_low) * 2 + x) * CORES + c

    far = []
    for m in range(chunks):
        pairs = []
        for i in range(devices):
            high, e_low, x, c = split(i)
            pairs.append((i, join(high ^ m, c, x, e_low)))
        far.append(pairs)
    to_core = [(i, i ^ 1) for i in range(devices)]
    to_x = [(i, i ^ CORES) for i in range(devices)]

    def move(value, perm):
        return lax.ppermute(value, "ep", perm)

    other = move(tokens, to_core)
    routes = routes.T
    routes_other = move(routes, to_core)
    side = move(tokens, to_x)
    both_routes = jnp.concatenate([routes, routes_other], axis=0)
    side_routes = move(both_routes, to_x)
    bf16 = functools.partial(jax.ShapeDtypeStruct, dtype=jnp.bfloat16)
    f32 = functools.partial(jax.ShapeDtypeStruct, dtype=jnp.float32)
    block, double = bf16((pair, width)), bf16((2 * pair, width))
    gain = norm_gain.reshape(1, width)
    sizes = dict(experts=experts, cap=cap)
    normed, *blocks = vmem_call(
        functools.partial(select_far, **sizes),
        [bf16((CORES * rows, width))] + [block] * (chunks - NEAR),
        1,
        6,
    )(ids, tokens, other, routes, routes_other, gain)
    sent = [None] * NEAR + [move(blocks[m - NEAR], far[m]) for m in range(NEAR, chunks)]
    all_normed, *blocks = vmem_call(
        functools.partial(select_near, **sizes),
        [bf16((2 * CORES * rows, width))] + [double] * NEAR,
        1,
        7,
    )(ids, normed, side, move(side, to_core), both_routes, side_routes, gain)
    for m in range(NEAR):
        sent[m] = move(blocks[m], far[m])
    near_weights = bf16((NEAR * 2 * pair, 2 * CORES * rows))
    far_weights = bf16(((chunks - NEAR) * pair, CORES * rows))
    near_high, near_low, far_high, far_low = vmem_call(
        functools.partial(weight_kernel, **sizes),
        [near_weights, near_weights, far_weights, far_weights],
        1,
        5,
    )(ids, all_normed, router_weight.T, both_routes, side_routes)

    gate_up = gate_up_weight[0].T
    down = down_weight[0]
    wide = jnp.float32
    back = []
    for m in range(chunks):
        if m < NEAR:
            mine, send = vmem_call(
                functools.partial(expert_kernel, ff=ff, blocks=2), [double, double], 0, 4
            )(sent[m], move(sent[m], to_core), gate_up, down)
            got = move(send, to_core)
            total = (mine.astype(wide) + got.astype(wide)).astype(jnp.bfloat16)
        else:
            across = move(sent[m], to_x)
            sent_other = move(sent[m], to_core)
            across_other = move(across, to_core)
            mine, mine_side, send = vmem_call(
                functools.partial(expert_kernel, ff=ff, blocks=4), [block, block, double], 0, 6
            )(sent[m], across, sent_other, across_other, gate_up, down)
            got = move(send, to_core)
            got_mine, got_side = got[:pair], got[pair:]
            out_side = (mine_side.astype(wide) + got_side.astype(wide)).astype(jnp.bfloat16)
            in_side = move(out_side, to_x)
            total = (mine.astype(wide) + got_mine.astype(wide) + in_side.astype(wide)).astype(
                jnp.bfloat16
            )
        back.append(move(total, far[m]))

    part = f32((rows, width))
    near_own, near_other, near_side, near_side_other = vmem_call(
        combine_near, [part, part, part, bf16((rows, width))], 0, 2 + NEAR
    )(near_high, near_low, *back[:NEAR])
    got = move(near_side_other, to_core)
    from_side = move((near_side + got.astype(wide)).astype(jnp.bfloat16), to_x)
    mixed_own, mixed_other = vmem_call(
        combine_far, [part, bf16((rows, width))], 0, 4 + chunks - NEAR
    )(far_high, far_low, near_own, near_other, *back[NEAR:])
    from_other = move(mixed_other, to_core)
    mixed = mixed_own + from_side.astype(wide) + from_other.astype(wide)
    return (tokens.astype(wide) + mixed).astype(jnp.bfloat16)


def solution(mesh):
    in_specs = (
        P(("groups", "ep"), None),
        P(("groups", "ep"), None),
        P(),
        P(),
        P("ep", None, None),
        P("ep", None, None),
    )
    out_specs = P(("groups", "ep"), None)
    return jax.shard_map(shards, mesh=mesh, in_specs=in_specs, out_specs=out_specs, check_vma=False)
```

time: 158 us -> 151 us (0.956); the launches traced: 158 us -> 149 us
  starting transfers between devices: 66 us -> 38.2 us
  waiting for transfers between devices: 59.2 us -> 75.9 us
  Pallas kernels: 26.5 us -> 29.2 us
  local copies, waits for them, and re-layouts: 4.08 us -> 2.47 us
    ppermute x31 -> x30, starting transfers between devices: 66 us -> 38.2 us  [move(): return lax.ppermute(value, 'ep', perm)]
    ppermute x31 -> x30, waiting for transfers between devices: 59.2 us -> 75.9 us  [move(): return lax.ppermute(value, 'ep', perm)]
    pallas_call x7 -> x9, Pallas kernels: 26.5 us -> 29.2 us  [the longest x2 11.4 us: shards(): vmem_call(functools.partial(expert_kernel, ff=ff, blocks=4), [block, bloc...]
    unnamed x14, local copies, waits for them, and re-layouts: 3.29 us -> 1.69 us
  transfers between devices with their start and end apart: 31 -> 30, of which waited for: 8 -> 15; matrix products, arithmetic and copies ran while one was open for 1% -> 2% of each run, Pallas kernels for 15% -> 20%
where the time goes in v3:
time: 151 us; the launch traced here: 149 us
  waiting for transfers between devices  75.9 us (50%)
  starting transfers between devices  38.2 us (25%)
  Pallas kernels  29.2 us (19%)
  other arithmetic  3.16 us (2%)
  local copies, waits for them, and re-layouts  2.47 us (2%)
    ppermute x30, waiting for transfers between devices, move(): return lax.ppermute(value, 'ep', perm)  75.9 us
    ppermute x30, starting transfers between devices, move(): return lax.ppermute(value, 'ep', perm)  38.2 us
    pallas_call x2, Pallas kernels, shards(): vmem_call(functools.partial(expert_kernel, ff=ff, blocks=4), [block, bloc...  11.4 us
    pallas_call x2, Pallas kernels, shards(): vmem_call(functools.partial(expert_kernel, ff=ff, blocks=2), [double, dou...  11.4 us
  transfers between devices with their start and end apart: 30, of which 15 were waited for; matrix products, arithmetic and copies ran while one was open for 2% of the time, Pallas kernels for 20%

profile of v3, /device:TPU:13, one launch (start us, length us, event | category | flops | bytes accessed | tf_op | source)
XLA Modules:
  0.0 149.0 jit_solution(7062756263862526020)
XLA Ops:
  0.0 0.7 collective-permute-start
  0.7 1.2 collective-permute-start.2
  1.9 0.3 collective-permute-start.1
  2.2 0.7 reshape.3.gain
  2.9 0.1 stack.23.ids
  3.0 0.2 collective-permute-done.1.routes_other
  3.3 1.0 copy-done.1
  4.3 0.7 copy-done.4
  4.9 1.2 shard_map.64
  6.1 2.4 %collective-permute-start.13 = (bf16[72,2880]{1,0:T(8,128)(2,1)S(1)}, bf16[72,2880]{1,0:T(8,128)(2,1)S(1)}, u32[]{:S(2)}, u32[]{:S(2)}) collective-permute-start(bf16[72,2880]{1,0:T(8,128)(2,1)S(1)} %get-tuple-element.45), channel_id=1, source_target_pairs={{0,16},{1,20},{2,18},{3,22},{4,17},{5,21},{6,19},{7,23},{8,24},{9,... | collective-permute-start | bytes 1244168 | tf_op jit(solution)/shard_map/ppermute | solution.py:205
  8.5 2.6 %collective-permute-done.2.side = bf16[64,2880]{1,0:T(8,128)(2,1)S(1)} collective-permute-done((bf16[64,2880]{1,0:T(8,128)(2,1)}, bf16[64,2880]{1,0:T(8,128)(2,1)S(1)}, u32[]{:S(2)}, u32[]{:S(2)}) %collective-permute-start.2) | collective-permute-done | bytes 368672 | tf_op jit(solution)/shard_map/ppermute | solution.py:205
  11.1 0.9 collective-permute-start.3
  12.1 1.2 collective-permute-start.4
  13.3 1.5 %collective-permute-done.4.routes_side = s32[8,64]{1,0:T(8,128)S(1)} collective-permute-done((s32[8,64]{1,0:T(8,128)S(1)}, s32[8,64]{1,0:T(8,128)S(1)}, u32[]{:S(2)}, u32[]{:S(2)}) %collective-permute-start.4) | collective-permute-done | bytes 2080 | tf_op jit(solution)/shard_map/ppermute | solution.py:205
  14.8 1.5 shard_map.65
  16.3 0.9 collective-permute-start.5
  17.2 0.2 collective-permute-start.9
  17.4 9.6 %collective-permute-done.13.refs_0_ = bf16[72,2880]{1,0:T(8,128)(2,1)S(1)} collective-permute-done((bf16[72,2880]{1,0:T(8,128)(2,1)S(1)}, bf16[72,2880]{1,0:T(8,128)(2,1)S(1)}, u32[]{:S(2)}, u32[]{:S(2)}) %collective-permute-start.13) | collective-permute-done | bytes 414752 | tf_op jit(solution)/shard_map/ppermute | solution.py:205
  27.1 0.3 collective-permute-start.14
  27.3 0.7 collective-permute-start.15
  28.1 9.9 %collective-permute-done.14.refs_1_ = bf16[72,2880]{1,0:T(8,128)(2,1)S(1)} collective-permute-done((bf16[72,2880]{1,0:T(8,128)(2,1)S(1)}, bf16[72,2880]{1,0:T(8,128)(2,1)S(1)}, u32[]{:S(2)}, u32[]{:S(2)}) %collective-permute-start.14) | collective-permute-done | bytes 414752 | tf_op jit(solution)/shard_map/ppermute | solution.py:205
  38.0 1.3 collective-permute-start.16
  39.3 0.8 collective-permute-done.20.refs_0_
  40.0 1.2 collective-permute-start.21
  41.3 3.5 %collective-permute-start.6 = (bf16[144,2880]{1,0:T(8,128)(2,1)S(1)}, bf16[144,2880]{1,0:T(8,128)(2,1)S(1)}, u32[]{:S(2)}, u32[]{:S(2)}) collective-permute-start(bf16[144,2880]{1,0:T(8,128)(2,1)S(1)} %collective-permute-done.5.refs_0_), channel_id=1, source_target_pairs={{0,1},{1,0},{2,3},{3,2},{4,5},{5,4},{6,7},{7,6},{8,9},{9,8},{10,11... | collective-permute-start | bytes 2488328 | tf_op jit(solution)/shard_map/ppermute | solution.py:205
  44.8 8.2 %collective-permute-done.9.refs_0_ = bf16[144,2880]{1,0:T(8,128)(2,1)S(1)} collective-permute-done((bf16[144,2880]{1,0:T(8,128)(2,1)S(1)}, bf16[144,2880]{1,0:T(8,128)(2,1)S(1)}, u32[]{:S(2)}, u32[]{:S(2)}) %collective-permute-start.9) | collective-permute-done | bytes 829472 | tf_op jit(solution)/shard_map/ppermute | solution.py:205
  53.0 0.5 collective-permute-start.10
  53.6 5.7 %shard_map.70 = (bf16[72,2880]{1,0:T(8,128)(2,1)S(1)}, bf16[72,2880]{1,0:T(8,128)(2,1)S(1)}, bf16[144,2880]{1,0:T(8,128)(2,1)S(1)}) custom-call(bf16[72,2880]{1,0:T(8,128)(2,1)S(1)} %collective-permute-done.13.refs_0_, bf16[72,2880]{1,0:T(8,128)(2,1)S(1)} %collective-permute-done.14.refs_1_, bf16[72,2880]{1,0:T(8,128)(2,1)S(1)} %collective-permute-done.15.refs_2_, ...), custom_call_target="tpu_custom_call" | custom-call | tf_op jit(solution)/shard_map/pallas_call | solution.py:257
  59.4 0.5 collective-permute-start.22
  59.9 0.1 collective-permute-start.23
  60.0 2.4 %collective-permute-done.22.refs_2_ = bf16[72,2880]{1,0:T(8,128)(2,1)S(1)} collective-permute-done((bf16[72,2880]{1,0:T(8,128)(2,1)S(1)}, bf16[72,2880]{1,0:T(8,128)(2,1)S(1)}, u32[]{:S(2)}, u32[]{:S(2)}) %collective-permute-start.22) | collective-permute-done | bytes 414752 | tf_op jit(solution)/shard_map/ppermute | solution.py:205
  62.4 0.6 collective-permute-done.23.refs_3_
  63.0 5.7 %shard_map.71 = (bf16[72,2880]{1,0:T(8,128)(2,1)S(1)}, bf16[72,2880]{1,0:T(8,128)(2,1)S(1)}, bf16[144,2880]{1,0:T(8,128)(2,1)S(1)}) custom-call(bf16[72,2880]{1,0:T(8,128)(2,1)S(1)} %collective-permute-done.20.refs_0_, bf16[72,2880]{1,0:T(8,128)(2,1)S(1)} %collective-permute-done.21.refs_1_, bf16[72,2880]{1,0:T(8,128)(2,1)S(1)} %collective-permute-done.22.refs_2_, ...), custom_call_target="tpu_custom_call" | custom-call | tf_op jit(solution)/shard_map/pallas_call | solution.py:257
  68.7 0.2 collective-permute-start.24
  68.9 5.7 %shard_map.67 = (bf16[144,2880]{1,0:T(8,128)(2,1)S(1)}, bf16[144,2880]{1,0:T(8,128)(2,1)S(1)}) custom-call(bf16[144,2880]{1,0:T(8,128)(2,1)S(1)} %collective-permute-done.5.refs_0_, bf16[144,2880]{1,0:T(8,128)(2,1)S(1)} %collective-permute-done.6.refs_1_, bf16[720,2880]{1,0:T(8,128)(2,1)} %bitcast.21, bf16[360,2880]{1,0:T(8,128)(2,1)S(1)} %bitcast.13), custom_call_target="tpu_custom_call" | custom-call | tf_op jit(solution)/shard_map/pallas_call | solution.py:248
  74.6 0.4 collective-permute-start.7
  75.0 5.7 %shard_map.68 = (bf16[144,2880]{1,0:T(8,128)(2,1)S(1)}, bf16[144,2880]{1,0:T(8,128)(2,1)S(1)}) custom-call(bf16[144,2880]{1,0:T(8,128)(2,1)S(1)} %collective-permute-done.9.refs_0_, bf16[144,2880]{1,0:T(8,128)(2,1)S(1)} %collective-permute-done.10.refs_1_, bf16[720,2880]{1,0:T(8,128)(2,1)} %bitcast.22, bf16[360,2880]{1,0:T(8,128)(2,1)S(1)} %bitcast.14), custom_call_target="tpu_custom_call" | custom-call | tf_op jit(solution)/shard_map/pallas_call | solution.py:248
  80.8 0.2 collective-permute-start.11
  81.0 0.1 add_convert_fusion.5
  81.1 0.4 collective-permute-start.18
  81.4 0.1 add_convert_fusion.3
  81.6 1.2 collective-permute-start.25
  82.8 1.4 add_convert_fusion.1
  84.2 1.1 collective-permute-start.8
  85.3 0.2 add_convert_fusion
  85.5 3.0 %collective-permute-start.12 = (bf16[144,2880]{1,0:T(8,128)(2,1)S(1)}, bf16[144,2880]{1,0:T(8,128)(2,1)S(1)}, u32[]{:S(2)}, u32[]{:S(2)}) collective-permute-start(bf16[144,2880]{1,0:T(8,128)(2,1)S(1)} %add_convert_fusion), channel_id=1, source_target_pairs={{0,8},{1,12},{2,10},{3,14},{4,9},{5,13},{6,11},{7,15},{8,0},{9,4},... | collective-permute-start | bytes 2488328 | tf_op jit(solution)/shard_map/ppermute | solution.py:205
  88.6 3.6 %collective-permute-done.18 = bf16[72,2880]{1,0:T(8,128)(2,1)S(1)} collective-permute-done((bf16[72,2880]{1,0:T(8,128)(2,1)S(1)}, bf16[72,2880]{1,0:T(8,128)(2,1)S(1)}, u32[]{:S(2)}, u32[]{:S(2)}) %collective-permute-start.18) | collective-permute-done | bytes 414752 | tf_op jit(solution)/shard_map/ppermute | solution.py:205
  92.1 0.2 add_convert_fusion.4
  92.3 5.1 %collective-permute-start.19 = (bf16[72,2880]{1,0:T(8,128)(2,1)S(1)}, bf16[72,2880]{1,0:T(8,128)(2,1)S(1)}, u32[]{:S(2)}, u32[]{:S(2)}) collective-permute-start(bf16[72,2880]{1,0:T(8,128)(2,1)S(1)} %add_convert_fusion.4), channel_id=1, source_target_pairs={{0,16},{1,20},{2,18},{3,22},{4,17},{5,21},{6,19},{7,23},{8,24},{9,... | collective-permute-start | bytes 1244168 | tf_op jit(solution)/shard_map/ppermute | solution.py:205
  97.4 3.8 %collective-permute-done.25 = bf16[72,2880]{1,0:T(8,128)(2,1)S(1)} collective-permute-done((bf16[72,2880]{1,0:T(8,128)(2,1)S(1)}, bf16[72,2880]{1,0:T(8,128)(2,1)S(1)}, u32[]{:S(2)}, u32[]{:S(2)}) %collective-permute-start.25) | collective-permute-done | bytes 414752 | tf_op jit(solution)/shard_map/ppermute | solution.py:205
  101.2 0.2 add_convert_fusion.2
  101.4 2.4 %collective-permute-start.26 = (bf16[72,2880]{1,0:T(8,128)(2,1)S(1)}, bf16[72,2880]{1,0:T(8,128)(2,1)S(1)}, u32[]{:S(2)}, u32[]{:S(2)}) collective-permute-start(bf16[72,2880]{1,0:T(8,128)(2,1)S(1)} %add_convert_fusion.2), channel_id=1, source_target_pairs={{0,24},{1,28},{2,26},{3,30},{4,25},{5,29},{6,27},{7,31},{8,16},{9,... | collective-permute-start | bytes 1244168 | tf_op jit(solution)/shard_map/ppermute | solution.py:205
  103.8 1.2 shard_map.66
  105.0 7.5 %collective-permute-done.12.refs_1_ = bf16[144,2880]{1,0:T(8,128)(2,1)S(1)} collective-permute-done((bf16[144,2880]{1,0:T(8,128)(2,1)S(1)}, bf16[144,2880]{1,0:T(8,128)(2,1)S(1)}, u32[]{:S(2)}, u32[]{:S(2)}) %collective-permute-start.12) | collective-permute-done | bytes 829472 | tf_op jit(solution)/shard_map/ppermute | solution.py:205
  112.5 1.8 %shard_map.69 = (f32[64,2880]{1,0:T(8,128)S(1)}, f32[64,2880]{1,0:T(8,128)S(1)}, f32[64,2880]{1,0:T(8,128)S(1)}, bf16[64,2880]{1,0:T(8,128)(2,1)S(1)}) custom-call(bf16[288,256]{1,0:T(8,128)(2,1)S(1)} %get-tuple-element.35.high, bf16[288,256]{1,0:T(8,128)(2,1)S(1)} %get-tuple-element.36.low, bf16[144,2880]{1,0:T(8,128)(2,1)S(1)} %collective-permute-done.8.refs_0_, ...), custom_call_target="tpu_custom_call" | custom-call | tf_op jit(solution)/shard_map/pallas_call | solution.py:270
  114.4 4.6 %collective-permute-start.27 = (bf16[64,2880]{1,0:T(8,128)(2,1)S(1)}, bf16[64,2880]{1,0:T(8,128)(2,1)S(1)}, u32[]{:S(2)}, u32[]{:S(2)}) collective-permute-start(bf16[64,2880]{1,0:T(8,128)(2,1)S(1)} %get-tuple-element.55), channel_id=1, source_target_pairs={{0,1},{1,0},{2,3},{3,2},{4,5},{5,4},{6,7},{7,6},{8,9},{9,8},{10,11... | collective-permute-start | bytes 1105928 | tf_op jit(solution)/shard_map/ppermute | solution.py:205
  118.9 14.9 %collective-permute-done.26.refs_1_ = bf16[72,2880]{1,0:T(8,128)(2,1)S(1)} collective-permute-done((bf16[72,2880]{1,0:T(8,128)(2,1)S(1)}, bf16[72,2880]{1,0:T(8,128)(2,1)S(1)}, u32[]{:S(2)}, u32[]{:S(2)}) %collective-permute-start.26) | collective-permute-done | bytes 414752 | tf_op jit(solution)/shard_map/ppermute | solution.py:205
  133.8 0.6 shard_map.72
  134.4 3.2 %collective-permute-start.29 = (bf16[64,2880]{1,0:T(8,128)(2,1)S(1)}, bf16[64,2880]{1,0:T(8,128)(2,1)S(1)}, u32[]{:S(2)}, u32[]{:S(2)}) collective-permute-start(bf16[64,2880]{1,0:T(8,128)(2,1)S(1)} %get-tuple-element.56), channel_id=1, source_target_pairs={{0,1},{1,0},{2,3},{3,2},{4,5},{5,4},{6,7},{7,6},{8,9},{9,8},{10,11... | collective-permute-start | bytes 1105928 | tf_op jit(solution)/shard_map/ppermute | solution.py:205
  137.6 0.1 add_convert_fusion.7
  137.7 0.3 collective-permute-start.28
  138.0 1.0 collective-permute-done.29
  139.0 9.1 %collective-permute-done.28 = bf16[64,2880]{1,0:T(8,128)(2,1)S(1)} collective-permute-done((bf16[64,2880]{1,0:T(8,128)(2,1)S(1)}, bf16[64,2880]{1,0:T(8,128)(2,1)S(1)}, u32[]{:S(2)}, u32[]{:S(2)}) %collective-permute-start.28) | collective-permute-done | bytes 368672 | tf_op jit(solution)/shard_map/ppermute | solution.py:205
  148.1 0.9 add_convert_fusion.6
  (30 shorter events, 0.1 us)
Async XLA Ops:
  0.0 53.6 %copy-start = (bf16[1,360,2880]{2,1,0:T(8,128)(2,1)S(1)}, bf16[1,360,2880]{2,1,0:T(8,128)(2,1)}, u32[]{:S(2)}) copy-start(bf16[1,360,2880]{2,1,0:T(8,128)(2,1)} %param.11) | copy-start | bytes 6220804
  0.0 3.3 %collective-permute-start = (bf16[64,2880]{1,0:T(8,128)(2,1)}, bf16[64,2880]{1,0:T(8,128)(2,1)S(1)}, u32[]{:S(2)}, u32[]{:S(2)}) collective-permute-start(bf16[64,2880]{1,0:T(8,128)(2,1)} %own.1), channel_id=1, source_target_pairs={{0,1},{1,0},{2,3},{3,2},{4,5},{5,4},{6,7},{7,6},{8,9},{9,8},{10,11... | collective-permute-start | bytes 1105928 | tf_op jit(solution)/shard_map/ppermute | solution.py:205
  0.7 10.5 %collective-permute-start.2 = (bf16[64,2880]{1,0:T(8,128)(2,1)}, bf16[64,2880]{1,0:T(8,128)(2,1)S(1)}, u32[]{:S(2)}, u32[]{:S(2)}) collective-permute-start(bf16[64,2880]{1,0:T(8,128)(2,1)} %own.1), channel_id=1, source_target_pairs={{0,2},{1,3},{2,0},{3,1},{4,6},{5,7},{6,4},{7,5},{8,10},{9,11},{10,... | collective-permute-start | bytes 1105928 | tf_op jit(solution)/shard_map/ppermute | solution.py:205
  1.9 1.4 collective-permute-start.1
  3.3 1.0 copy-start.1
  4.3 0.7 copy-start.4
  6.1 20.9 %collective-permute-start.13 = (bf16[72,2880]{1,0:T(8,128)(2,1)S(1)}, bf16[72,2880]{1,0:T(8,128)(2,1)S(1)}, u32[]{:S(2)}, u32[]{:S(2)}) collective-permute-start(bf16[72,2880]{1,0:T(8,128)(2,1)S(1)} %get-tuple-element.45), channel_id=1, source_target_pairs={{0,16},{1,20},{2,18},{3,22},{4,17},{5,21},{6,19},{7,23},{8,24},{9,... | collective-permute-start | bytes 1244168 | tf_op jit(solution)/shard_map/ppermute | solution.py:205
  11.1 3.7 %collective-permute-start.3 = (bf16[64,2880]{1,0:T(8,128)(2,1)S(1)}, bf16[64,2880]{1,0:T(8,128)(2,1)S(1)}, u32[]{:S(2)}, u32[]{:S(2)}) collective-permute-start(bf16[64,2880]{1,0:T(8,128)(2,1)S(1)} %collective-permute-done.2.side), channel_id=1, source_target_pairs={{0,1},{1,0},{2,3},{3,2},{4,5},{5,4},{6,7},{7,6},{8,9},{9,8},{10,11... | collective-permute-start | bytes 1105928 | tf_op jit(solution)/shard_map/ppermute | solution.py:205
  12.1 2.8 %collective-permute-start.4 = (s32[8,64]{1,0:T(8,128)S(1)}, s32[8,64]{1,0:T(8,128)S(1)}, u32[]{:S(2)}, u32[]{:S(2)}) collective-permute-start(s32[8,64]{1,0:T(8,128)S(1)} %pad_add_fusion.routes), channel_id=1, source_target_pairs={{0,2},{1,3},{2,0},{3,1},{4,6},{5,7},{6,4},{7,5},{8,10},{9,11},{10,... | collective-permute-start | bytes 6152 | tf_op jit(solution)/shard_map/ppermute | solution.py:205
  16.3 25.0 %collective-permute-start.5 = (bf16[144,2880]{1,0:T(8,128)(2,1)S(1)}, bf16[144,2880]{1,0:T(8,128)(2,1)S(1)}, u32[]{:S(2)}, u32[]{:S(2)}) collective-permute-start(bf16[144,2880]{1,0:T(8,128)(2,1)S(1)} %get-tuple-element.37), channel_id=1, source_target_pairs={{0,0},{1,4},{2,2},{3,6},{4,1},{5,5},{6,3},{7,7},{8,8},{9,12},{10,1... | collective-permute-start | bytes 2488328 | tf_op jit(solution)/shard_map/ppermute | solution.py:205
  17.2 35.8 %collective-permute-start.9 = (bf16[144,2880]{1,0:T(8,128)(2,1)S(1)}, bf16[144,2880]{1,0:T(8,128)(2,1)S(1)}, u32[]{:S(2)}, u32[]{:S(2)}) collective-permute-start(bf16[144,2880]{1,0:T(8,128)(2,1)S(1)} %get-tuple-element.40), channel_id=1, source_target_pairs={{0,8},{1,12},{2,10},{3,14},{4,9},{5,13},{6,11},{7,15},{8,0},{9,4},... | collective-permute-start | bytes 2488328 | tf_op jit(solution)/shard_map/ppermute | solution.py:205
  27.1 10.9 %collective-permute-start.14 = (bf16[72,2880]{1,0:T(8,128)(2,1)S(1)}, bf16[72,2880]{1,0:T(8,128)(2,1)S(1)}, u32[]{:S(2)}, u32[]{:S(2)}) collective-permute-start(bf16[72,2880]{1,0:T(8,128)(2,1)S(1)} %collective-permute-done.13.refs_0_), channel_id=1, source_target_pairs={{0,2},{1,3},{2,0},{3,1},{4,6},{5,7},{6,4},{7,5},{8,10},{9,11},{10,... | collective-permute-start | bytes 1244168 | tf_op jit(solution)/shard_map/ppermute | solution.py:205
  27.3 12.7 %collective-permute-start.20 = (bf16[72,2880]{1,0:T(8,128)(2,1)S(1)}, bf16[72,2880]{1,0:T(8,128)(2,1)S(1)}, u32[]{:S(2)}, u32[]{:S(2)}) collective-permute-start(bf16[72,2880]{1,0:T(8,128)(2,1)S(1)} %get-tuple-element.49), channel_id=1, source_target_pairs={{0,24},{1,28},{2,26},{3,30},{4,25},{5,29},{6,27},{7,31},{8,16},{9,... | collective-permute-start | bytes 1244168 | tf_op jit(solution)/shard_map/ppermute | solution.py:205
  27.3 26.2 %collective-permute-start.15 = (bf16[72,2880]{1,0:T(8,128)(2,1)S(1)}, bf16[72,2880]{1,0:T(8,128)(2,1)S(1)}, u32[]{:S(2)}, u32[]{:S(2)}) collective-permute-start(bf16[72,2880]{1,0:T(8,128)(2,1)S(1)} %collective-permute-done.13.refs_0_), channel_id=1, source_target_pairs={{0,1},{1,0},{2,3},{3,2},{4,5},{5,4},{6,7},{7,6},{8,9},{9,8},{10,11... | collective-permute-start | bytes 1244168 | tf_op jit(solution)/shard_map/ppermute | solution.py:205
  38.0 15.6 %collective-permute-start.16 = (bf16[72,2880]{1,0:T(8,128)(2,1)S(1)}, bf16[72,2880]{1,0:T(8,128)(2,1)S(1)}, u32[]{:S(2)}, u32[]{:S(2)}) collective-permute-start(bf16[72,2880]{1,0:T(8,128)(2,1)S(1)} %collective-permute-done.14.refs_1_), channel_id=1, source_target_pairs={{0,1},{1,0},{2,3},{3,2},{4,5},{5,4},{6,7},{7,6},{8,9},{9,8},{10,11... | collective-permute-start | bytes 1244168 | tf_op jit(solution)/shard_map/ppermute | solution.py:205
  40.0 19.8 %collective-permute-start.21 = (bf16[72,2880]{1,0:T(8,128)(2,1)S(1)}, bf16[72,2880]{1,0:T(8,128)(2,1)S(1)}, u32[]{:S(2)}, u32[]{:S(2)}) collective-permute-start(bf16[72,2880]{1,0:T(8,128)(2,1)S(1)} %collective-permute-done.20.refs_0_), channel_id=1, source_target_pairs={{0,2},{1,3},{2,0},{3,1},{4,6},{5,7},{6,4},{7,5},{8,10},{9,11},{10,... | collective-permute-start | bytes 1244168 | tf_op jit(solution)/shard_map/ppermute | solution.py:205
  41.3 27.6 %collective-permute-start.6 = (bf16[144,2880]{1,0:T(8,128)(2,1)S(1)}, bf16[144,2880]{1,0:T(8,128)(2,1)S(1)}, u32[]{:S(2)}, u32[]{:S(2)}) collective-permute-start(bf16[144,2880]{1,0:T(8,128)(2,1)S(1)} %collective-permute-done.5.refs_0_), channel_id=1, source_target_pairs={{0,1},{1,0},{2,3},{3,2},{4,5},{5,4},{6,7},{7,6},{8,9},{9,8},{10,11... | collective-permute-start | bytes 2488328 | tf_op jit(solution)/shard_map/ppermute | solution.py:205
  53.0 22.0 %collective-permute-start.10 = (bf16[144,2880]{1,0:T(8,128)(2,1)S(1)}, bf16[144,2880]{1,0:T(8,128)(2,1)S(1)}, u32[]{:S(2)}, u32[]{:S(2)}) collective-permute-start(bf16[144,2880]{1,0:T(8,128)(2,1)S(1)} %collective-permute-done.9.refs_0_), channel_id=1, source_target_pairs={{0,1},{1,0},{2,3},{3,2},{4,5},{5,4},{6,7},{7,6},{8,9},{9,8},{10,11... | collective-permute-start | bytes 2488328 | tf_op jit(solution)/shard_map/ppermute | solution.py:205
  59.3 21.7 %collective-permute-start.17 = (bf16[144,2880]{1,0:T(8,128)(2,1)S(1)}, bf16[144,2880]{1,0:T(8,128)(2,1)S(1)}, u32[]{:S(2)}, u32[]{:S(2)}) collective-permute-start(bf16[144,2880]{1,0:T(8,128)(2,1)S(1)} %get-tuple-element.47), channel_id=1, source_target_pairs={{0,1},{1,0},{2,3},{3,2},{4,5},{5,4},{6,7},{7,6},{8,9},{9,8},{10,11... | collective-permute-start | bytes 2488328 | tf_op jit(solution)/shard_map/ppermute | solution.py:205
  59.4 3.0 %collective-permute-start.22 = (bf16[72,2880]{1,0:T(8,128)(2,1)S(1)}, bf16[72,2880]{1,0:T(8,128)(2,1)S(1)}, u32[]{:S(2)}, u32[]{:S(2)}) collective-permute-start(bf16[72,2880]{1,0:T(8,128)(2,1)S(1)} %collective-permute-done.20.refs_0_), channel_id=1, source_target_pairs={{0,1},{1,0},{2,3},{3,2},{4,5},{5,4},{6,7},{7,6},{8,9},{9,8},{10,11... | collective-permute-start | bytes 1244168 | tf_op jit(solution)/shard_map/ppermute | solution.py:205
  59.9 3.1 %collective-permute-start.23 = (bf16[72,2880]{1,0:T(8,128)(2,1)S(1)}, bf16[72,2880]{1,0:T(8,128)(2,1)S(1)}, u32[]{:S(2)}, u32[]{:S(2)}) collective-permute-start(bf16[72,2880]{1,0:T(8,128)(2,1)S(1)} %collective-permute-done.21.refs_1_), channel_id=1, source_target_pairs={{0,1},{1,0},{2,3},{3,2},{4,5},{5,4},{6,7},{7,6},{8,9},{9,8},{10,11... | collective-permute-start | bytes 1244168 | tf_op jit(solution)/shard_map/ppermute | solution.py:205
  68.7 12.8 %collective-permute-start.24 = (bf16[144,2880]{1,0:T(8,128)(2,1)S(1)}, bf16[144,2880]{1,0:T(8,128)(2,1)S(1)}, u32[]{:S(2)}, u32[]{:S(2)}) collective-permute-start(bf16[144,2880]{1,0:T(8,128)(2,1)S(1)} %get-tuple-element.51), channel_id=1, source_target_pairs={{0,1},{1,0},{2,3},{3,2},{4,5},{5,4},{6,7},{7,6},{8,9},{9,8},{10,11... | collective-permute-start | bytes 2488328 | tf_op jit(solution)/shard_map/ppermute | solution.py:205
  74.6 8.2 %collective-permute-start.7 = (bf16[144,2880]{1,0:T(8,128)(2,1)S(1)}, bf16[144,2880]{1,0:T(8,128)(2,1)}, u32[]{:S(2)}, u32[]{:S(2)}) collective-permute-start(bf16[144,2880]{1,0:T(8,128)(2,1)S(1)} %get-tuple-element.39), channel_id=1, source_target_pairs={{0,1},{1,0},{2,3},{3,2},{4,5},{5,4},{6,7},{7,6},{8,9},{9,8},{10,11... | collective-permute-start | bytes 2488328 | tf_op jit(solution)/shard_map/ppermute | solution.py:205
  80.8 4.5 %collective-permute-start.11 = (bf16[144,2880]{1,0:T(8,128)(2,1)S(1)}, bf16[144,2880]{1,0:T(8,128)(2,1)S(1)}, u32[]{:S(2)}, u32[]{:S(2)}) collective-permute-start(bf16[144,2880]{1,0:T(8,128)(2,1)S(1)} %get-tuple-element.42), channel_id=1, source_target_pairs={{0,1},{1,0},{2,3},{3,2},{4,5},{5,4},{6,7},{7,6},{8,9},{9,8},{10,11... | collective-permute-start | bytes 2488328 | tf_op jit(solution)/shard_map/ppermute | solution.py:205
  81.0 1.8 %copy-start.5 = (bf16[144,2880]{1,0:T(8,128)(2,1)}, bf16[144,2880]{1,0:T(8,128)(2,1)S(1)}, u32[]{:S(2)}) copy-start(bf16[144,2880]{1,0:T(8,128)(2,1)S(1)} %collective-permute-done.17) | copy-start | bytes 2488324
  81.1 11.0 %collective-permute-start.18 = (bf16[72,2880]{1,0:T(8,128)(2,1)S(1)}, bf16[72,2880]{1,0:T(8,128)(2,1)S(1)}, u32[]{:S(2)}, u32[]{:S(2)}) collective-permute-start(bf16[72,2880]{1,0:T(8,128)(2,1)S(1)} %add_convert_fusion.5), channel_id=1, source_target_pairs={{0,2},{1,3},{2,0},{3,1},{4,6},{5,7},{6,4},{7,5},{8,10},{9,11},{10,... | collective-permute-start | bytes 1244168 | tf_op jit(solution)/shard_map/ppermute | solution.py:205
  81.6 19.6 %collective-permute-start.25 = (bf16[72,2880]{1,0:T(8,128)(2,1)S(1)}, bf16[72,2880]{1,0:T(8,128)(2,1)S(1)}, u32[]{:S(2)}, u32[]{:S(2)}) collective-permute-start(bf16[72,2880]{1,0:T(8,128)(2,1)S(1)} %add_convert_fusion.3), channel_id=1, source_target_pairs={{0,2},{1,3},{2,0},{3,1},{4,6},{5,7},{6,4},{7,5},{8,10},{9,11},{10,... | collective-permute-start | bytes 1244168 | tf_op jit(solution)/shard_map/ppermute | solution.py:205
  84.2 7.9 %copy-start.6 = (bf16[144,2880]{1,0:T(8,128)(2,1)S(1)}, bf16[144,2880]{1,0:T(8,128)(2,1)}, u32[]{:S(2)}) copy-start(bf16[144,2880]{1,0:T(8,128)(2,1)} %copy-done.5) | copy-start | bytes 2488324
  84.2 20.8 %collective-permute-start.8 = (bf16[144,2880]{1,0:T(8,128)(2,1)S(1)}, bf16[144,2880]{1,0:T(8,128)(2,1)S(1)}, u32[]{:S(2)}, u32[]{:S(2)}) collective-permute-start(bf16[144,2880]{1,0:T(8,128)(2,1)S(1)} %add_convert_fusion.1), channel_id=1, source_target_pairs={{0,0},{1,4},{2,2},{3,6},{4,1},{5,5},{6,3},{7,7},{8,8},{9,12},{10,1... | collective-permute-start | bytes 2488328 | tf_op jit(solution)/shard_map/ppermute | solution.py:205
  85.5 27.0 %collective-permute-start.12 = (bf16[144,2880]{1,0:T(8,128)(2,1)S(1)}, bf16[144,2880]{1,0:T(8,128)(2,1)S(1)}, u32[]{:S(2)}, u32[]{:S(2)}) collective-permute-start(bf16[144,2880]{1,0:T(8,128)(2,1)S(1)} %add_convert_fusion), channel_id=1, source_target_pairs={{0,8},{1,12},{2,10},{3,14},{4,9},{5,13},{6,11},{7,15},{8,0},{9,4},... | collective-permute-start | bytes 2488328 | tf_op jit(solution)/shard_map/ppermute | solution.py:205
  92.1 11.7 %copy-start.3 = (bf16[2880,8]{0,1:T(8,128)(2,1)S(1)}, bf16[2880,8]{0,1:T(8,128)(2,1)}, u32[]{:S(2)}) copy-start(bf16[2880,8]{0,1:T(8,128)(2,1)} %param.9) | copy-start | bytes 138244
  92.3 26.6 %collective-permute-start.19 = (bf16[72,2880]{1,0:T(8,128)(2,1)S(1)}, bf16[72,2880]{1,0:T(8,128)(2,1)S(1)}, u32[]{:S(2)}, u32[]{:S(2)}) collective-permute-start(bf16[72,2880]{1,0:T(8,128)(2,1)S(1)} %add_convert_fusion.4), channel_id=1, source_target_pairs={{0,16},{1,20},{2,18},{3,22},{4,17},{5,21},{6,19},{7,23},{8,24},{9,... | collective-permute-start | bytes 1244168 | tf_op jit(solution)/shard_map/ppermute | solution.py:205
  101.4 32.4 %collective-permute-start.26 = (bf16[72,2880]{1,0:T(8,128)(2,1)S(1)}, bf16[72,2880]{1,0:T(8,128)(2,1)S(1)}, u32[]{:S(2)}, u32[]{:S(2)}) collective-permute-start(bf16[72,2880]{1,0:T(8,128)(2,1)S(1)} %add_convert_fusion.2), channel_id=1, source_target_pairs={{0,24},{1,28},{2,26},{3,30},{4,25},{5,29},{6,27},{7,31},{8,16},{9,... | collective-permute-start | bytes 1244168 | tf_op jit(solution)/shard_map/ppermute | solution.py:205
  114.4 23.3 %collective-permute-start.27 = (bf16[64,2880]{1,0:T(8,128)(2,1)S(1)}, bf16[64,2880]{1,0:T(8,128)(2,1)S(1)}, u32[]{:S(2)}, u32[]{:S(2)}) collective-permute-start(bf16[64,2880]{1,0:T(8,128)(2,1)S(1)} %get-tuple-element.55), channel_id=1, source_target_pairs={{0,1},{1,0},{2,3},{3,2},{4,5},{5,4},{6,7},{7,6},{8,9},{9,8},{10,11... | collective-permute-start | bytes 1105928 | tf_op jit(solution)/shard_map/ppermute | solution.py:205
  133.8 14.3 %copy-start.2 = (bf16[64,2880]{1,0:T(8,128)(2,1)S(1)}, bf16[64,2880]{1,0:T(8,128)(2,1)}, u32[]{:S(2)}) copy-start(bf16[64,2880]{1,0:T(8,128)(2,1)} %own.1) | copy-start | bytes 1105924
  134.4 4.5 %collective-permute-start.29 = (bf16[64,2880]{1,0:T(8,128)(2,1)S(1)}, bf16[64,2880]{1,0:T(8,128)(2,1)S(1)}, u32[]{:S(2)}, u32[]{:S(2)}) collective-permute-start(bf16[64,2880]{1,0:T(8,128)(2,1)S(1)} %get-tuple-element.56), channel_id=1, source_target_pairs={{0,1},{1,0},{2,3},{3,2},{4,5},{5,4},{6,7},{7,6},{8,9},{9,8},{10,11... | collective-permute-start | bytes 1105928 | tf_op jit(solution)/shard_map/ppermute | solution.py:205
  137.7 10.4 %collective-permute-start.28 = (bf16[64,2880]{1,0:T(8,128)(2,1)S(1)}, bf16[64,2880]{1,0:T(8,128)(2,1)S(1)}, u32[]{:S(2)}, u32[]{:S(2)}) collective-permute-start(bf16[64,2880]{1,0:T(8,128)(2,1)S(1)} %add_convert_fusion.7), channel_id=1, source_target_pairs={{0,2},{1,3},{2,0},{3,1},{4,6},{5,7},{6,4},{7,5},{8,10},{9,11},{10,... | collective-permute-start | bytes 1105928 | tf_op jit(solution)/shard_map/ppermute | solution.py:205

commit v4 on v2

--- a/solution.py
+++ b/solution.py
@@ -10,6 +10,7 @@
 
 CORES = 2
 SHARDS = 4
+NEAR = 2
 VMEM_BYTES = 48 * 1024 * 1024
 
 
@@ -46,13 +47,14 @@
     return (stream * lax.rsqrt(mean_square + 1e-05) * gain).astype(jnp.bfloat16)
 
 
-def select_kernel(ids, own, other, routes_own, routes_other, gain, normed, *blocks, experts, cap):
+def select_kernel(ids, own, other, routes, gain, normed, *blocks, experts, cap):
     rows = own.shape[0]
+    top = routes.shape[0] // CORES
     scale = gain[...].astype(jnp.float32)
-    own_core = ids[len(blocks)]
+    own_core = ids[ids.shape[0] - 1]
     normed[0:rows, :] = normed_of(own[...], scale)
     normed[rows:, :] = normed_of(other[...], scale)
-    place, named = places_of(routes_own[...], routes_other[...], own_core, experts, cap)
+    place, named = places_of(routes[0:top, :], routes[top:, :], own_core, experts, cap)
     place = jnp.where(named, place + 1, 0)
     values = normed[...]
     slots = lax.broadcasted_iota(jnp.int32, (CORES * cap, CORES * rows), 0) + 1
@@ -61,11 +63,12 @@
         block[...] = dot32(pick, values).astype(jnp.bfloat16)
 
 
-def weight_kernel(ids, normed, router, routes_own, routes_other, high, low, *, experts, cap):
+def weight_kernel(ids, normed, router, routes, high, low, *, experts, cap):
     pair = CORES * cap
     count = high.shape[0] // pair
     logits = dot32(router[...], normed[...], ((1,), (1,)))
-    place, named = places_of(routes_own[...], routes_other[...], ids[count], experts, cap)
+    top = routes.shape[0] // CORES
+    place, named = places_of(routes[0:top, :], routes[top:, :], ids[count], experts, cap)
     expo = jnp.where(named, jnp.exp(logits), 0.0)
     prob = expo / jnp.sum(expo, axis=0, keepdims=True)
     place = jnp.where(named, place + 1, 0)
@@ -156,21 +159,34 @@
 
     other = move(tokens, to_core)
     routes = routes.T
-    routes_other = move(routes, to_core)
+    routes = jnp.concatenate([routes, move(routes, to_core)], axis=0)
     block = jax.ShapeDtypeStruct((pair, width), jnp.bfloat16)
     gain = norm_gain.reshape(1, width)
-    normed, *blocks = vmem_call(
-        functools.partial(select_kernel, experts=experts, cap=cap),
-        [jax.ShapeDtypeStruct((CORES * rows, width), jnp.bfloat16)] + [block] * chunks,
-        1,
-        6,
-    )(ids, tokens, other, routes, routes_other, gain)
-
-    near = [move(blocks[m], far[m]) for m in range(chunks)]
+
+    def select(own, other, routes):
+        return vmem_call(
+            functools.partial(select_kernel, experts=experts, cap=cap),
+            [jax.ShapeDtypeStruct((CORES * rows, width), jnp.bfloat16)] + [block] * NEAR,
+            1,
+            5,
+        )(ids, own, other, routes, gain)
+
+    lent = {}
+    for m in range(NEAR, chunks, NEAR):
+        pairs = []
+        for i in range(devices):
+            high, e_low, x, c = split(i)
+            pairs.append((i, join(high ^ m, e_low, x, c)))
+        lent[m] = (move(tokens, pairs), move(routes, pairs))
+    normed, *blocks = select(tokens, other, routes)
+    near = [move(blocks[n], far[n]) for n in range(NEAR)]
+    for (theirs, their_routes) in lent.values():
+        _, *blocks = select(theirs, move(theirs, to_core), their_routes)
+        near += [move(blocks[n], far[n]) for n in range(NEAR)]
     weights = jax.ShapeDtypeStruct((chunks * pair, CORES * rows), jnp.bfloat16)
     high, low = vmem_call(
-        functools.partial(weight_kernel, experts=experts, cap=cap), [weights, weights], 1, 5
-    )(ids, normed, router_weight.T, routes, routes_other)
+        functools.partial(weight_kernel, experts=experts, cap=cap), [weights, weights], 1, 4
+    )(ids, normed, router_weight.T, routes)
 
     gate_up = gate_up_weight[0].T
     down = down_weight[0]

time: 158 us -> 163 us (1.032)
  waiting for transfers between devices: 59.2 us -> 93.4 us
  starting transfers between devices: 66 us -> 35.3 us
    ppermute x31 -> x34, waiting for transfers between devices: 59.2 us -> 93.4 us  [move(): return lax.ppermute(value, 'ep', perm)]
    ppermute x31 -> x34, starting transfers between devices: 66 us -> 35.3 us  [move(): return lax.ppermute(value, 'ep', perm)]
    unnamed x14 -> x10, local copies, waits for them, and re-layouts: 3.29 us -> 2.6 us
  transfers between devices with their start and end apart: 31 -> 34, of which waited for: 8 -> 12; matrix products, arithmetic and copies ran while one was open for 1% -> 2% of each run, Pallas kernels for 15% -> 17%
where the time goes in v4:
time: 163 us
  waiting for transfers between devices  93.4 us (57%)
  starting transfers between devices  35.3 us (22%)
  Pallas kernels  28 us (17%)
  local copies, waits for them, and re-layouts  3.38 us (2%)
  other arithmetic  2.64 us (2%)
    ppermute x34, waiting for transfers between devices, move(): return lax.ppermute(value, 'ep', perm)  93.4 us
    ppermute x34, starting transfers between devices, move(): return lax.ppermute(value, 'ep', perm)  35.3 us
    pallas_call x4, Pallas kernels, shards(): vmem_call(functools.partial(expert_kernel, ff=ff), [block, block, jax.Sha...  23 us
  transfers between devices with their start and end apart: 34, of which 12 were waited for; matrix products, arithmetic and copies ran while one was open for 2% of the time, Pallas kernels for 17%

profile of v4, /device:TPU:13, one launch (start us, length us, event | category | flops | bytes accessed | tf_op | source)
XLA Modules:
  0.0 163.1 jit_solution(13876914893836374356)
XLA Ops:
  0.0 0.7 collective-permute-start
  0.7 2.3 %collective-permute-start.16 = (bf16[64,2880]{1,0:T(8,128)(2,1)}, bf16[64,2880]{1,0:T(8,128)(2,1)S(1)}, u32[]{:S(2)}, u32[]{:S(2)}) collective-permute-start(bf16[64,2880]{1,0:T(8,128)(2,1)} %own.1), channel_id=1, source_target_pairs={{0,16},{1,17},{2,18},{3,19},{4,20},{5,21},{6,22},{7,23},{8,24},{9,... | collective-permute-start | bytes 1105928 | tf_op jit(solution)/shard_map/ppermute | solution.py:158
  3.0 0.3 collective-permute-start.1
  3.3 0.7 reshape.3.gain
  4.0 0.1 stack.23.ids
  4.1 0.3 collective-permute-done.1
  4.4 0.7 pad_add_fusion.routes
  5.1 1.0 copy-done.2
  6.0 1.2 shard_map.64
  7.3 0.7 collective-permute-start.2
  8.0 11.8 %collective-permute-done.16.own = bf16[64,2880]{1,0:T(8,128)(2,1)S(1)} collective-permute-done((bf16[64,2880]{1,0:T(8,128)(2,1)}, bf16[64,2880]{1,0:T(8,128)(2,1)S(1)}, u32[]{:S(2)}, u32[]{:S(2)}) %collective-permute-start.16) | collective-permute-done | bytes 368672 | tf_op jit(solution)/shard_map/ppermute | solution.py:158
  19.8 0.4 collective-permute-start.17
  20.2 1.0 collective-permute-start.9
  21.2 1.2 collective-permute-start.3
  22.4 2.0 %collective-permute-start.18 = (s32[8,64]{1,0:T(8,128)S(1)}, s32[8,64]{1,0:T(8,128)S(1)}, u32[]{:S(2)}, u32[]{:S(2)}) collective-permute-start(s32[8,64]{1,0:T(8,128)S(1)} %pad_add_fusion.routes), channel_id=1, source_target_pairs={{0,16},{1,17},{2,18},{3,19},{4,20},{5,21},{6,22},{7,23},{8,24},{9,... | collective-permute-start | bytes 6152 | tf_op jit(solution)/shard_map/ppermute | solution.py:158
  24.5 8.7 %collective-permute-done.18.routes = s32[8,64]{1,0:T(8,128)S(1)} collective-permute-done((s32[8,64]{1,0:T(8,128)S(1)}, s32[8,64]{1,0:T(8,128)S(1)}, u32[]{:S(2)}, u32[]{:S(2)}) %collective-permute-start.18) | collective-permute-done | bytes 2080 | tf_op jit(solution)/shard_map/ppermute | solution.py:158
  33.1 1.8 %shard_map.68 = (bf16[128,2880]{1,0:T(8,128)(2,1)}, bf16[72,2880]{1,0:T(8,128)(2,1)S(1)}, bf16[72,2880]{1,0:T(8,128)(2,1)S(1)}) custom-call(s32[5]{0:T(128)S(1)} %stack.23.ids, bf16[64,2880]{1,0:T(8,128)(2,1)S(1)} %collective-permute-done.16.own, bf16[64,2880]{1,0:T(8,128)(2,1)S(1)} %collective-permute-done.17.other, ...), custom_call_target="tpu_custom_call" | custom-call | tf_op jit(solution)/shard_map/pallas_call | solution.py:167
  34.9 0.7 collective-permute-start.19
  35.7 2.2 %collective-permute-start.4 = (bf16[72,2880]{1,0:T(8,128)(2,1)S(1)}, bf16[72,2880]{1,0:T(8,128)(2,1)S(1)}, u32[]{:S(2)}, u32[]{:S(2)}) collective-permute-start(bf16[72,2880]{1,0:T(8,128)(2,1)S(1)} %collective-permute-done.2.a), channel_id=1, source_target_pairs={{0,1},{1,0},{2,3},{3,2},{4,5},{5,4},{6,7},{7,6},{8,9},{9,8},{10,11... | collective-permute-start | bytes 1244168 | tf_op jit(solution)/shard_map/ppermute | solution.py:158
  37.9 1.2 collective-permute-start.10
  39.2 0.4 collective-permute-start.5
  39.5 10.3 %collective-permute-start.11 = (bf16[72,2880]{1,0:T(8,128)(2,1)S(1)}, bf16[72,2880]{1,0:T(8,128)(2,1)S(1)}, u32[]{:S(2)}, u32[]{:S(2)}) collective-permute-start(bf16[72,2880]{1,0:T(8,128)(2,1)S(1)} %collective-permute-done.9.a), channel_id=1, source_target_pairs={{0,1},{1,0},{2,3},{3,2},{4,5},{5,4},{6,7},{7,6},{8,9},{9,8},{10,11... | collective-permute-start | bytes 1244168 | tf_op jit(solution)/shard_map/ppermute | solution.py:158
  49.8 1.2 collective-permute-start.20
  51.1 0.3 collective-permute-start.27
  51.3 0.6 collective-permute-start.12
  51.9 1.6 copy-done
  53.5 5.9 %shard_map.66 = (bf16[72,2880]{1,0:T(8,128)(2,1)S(1)}, bf16[72,2880]{1,0:T(8,128)(2,1)S(1)}, bf16[144,2880]{1,0:T(8,128)(2,1)S(1)}) custom-call(bf16[72,2880]{1,0:T(8,128)(2,1)S(1)} %collective-permute-done.2.a, bf16[72,2880]{1,0:T(8,128)(2,1)S(1)} %collective-permute-done.3.b, bf16[72,2880]{1,0:T(8,128)(2,1)S(1)} %collective-permute-done.4.c, ...), custom_call_target="tpu_custom_call" | custom-call | tf_op jit(solution)/shard_map/pallas_call | solution.py:198
  59.3 0.1 collective-permute-start.6
  59.4 0.5 collective-permute-start.21
  59.9 1.2 collective-permute-done.20.b
  61.2 1.3 collective-permute-start.22
  62.5 7.8 %collective-permute-done.27.b = bf16[72,2880]{1,0:T(8,128)(2,1)S(1)} collective-permute-done((bf16[72,2880]{1,0:T(8,128)(2,1)S(1)}, bf16[72,2880]{1,0:T(8,128)(2,1)S(1)}, u32[]{:S(2)}, u32[]{:S(2)}) %collective-permute-start.27) | collective-permute-done | bytes 414752 | tf_op jit(solution)/shard_map/ppermute | solution.py:158
  70.2 0.9 collective-permute-start.28
  71.1 5.7 %shard_map.67 = (bf16[72,2880]{1,0:T(8,128)(2,1)S(1)}, bf16[72,2880]{1,0:T(8,128)(2,1)S(1)}, bf16[144,2880]{1,0:T(8,128)(2,1)S(1)}) custom-call(bf16[72,2880]{1,0:T(8,128)(2,1)S(1)} %collective-permute-done.9.a, bf16[72,2880]{1,0:T(8,128)(2,1)S(1)} %collective-permute-done.10.b, bf16[72,2880]{1,0:T(8,128)(2,1)S(1)} %collective-permute-done.11.c, ...), custom_call_target="tpu_custom_call" | custom-call | tf_op jit(solution)/shard_map/pallas_call | solution.py:198
  76.9 0.6 collective-permute-start.13
  77.4 5.7 %shard_map.69 = (bf16[72,2880]{1,0:T(8,128)(2,1)S(1)}, bf16[72,2880]{1,0:T(8,128)(2,1)S(1)}, bf16[144,2880]{1,0:T(8,128)(2,1)S(1)}) custom-call(bf16[72,2880]{1,0:T(8,128)(2,1)S(1)} %collective-permute-done.19.a, bf16[72,2880]{1,0:T(8,128)(2,1)S(1)} %collective-permute-done.20.b, bf16[72,2880]{1,0:T(8,128)(2,1)S(1)} %collective-permute-done.21.c, ...), custom_call_target="tpu_custom_call" | custom-call | tf_op jit(solution)/shard_map/pallas_call | solution.py:198
  83.2 0.1 collective-permute-start.23
  83.3 5.7 %shard_map.70 = (bf16[72,2880]{1,0:T(8,128)(2,1)S(1)}, bf16[72,2880]{1,0:T(8,128)(2,1)S(1)}, bf16[144,2880]{1,0:T(8,128)(2,1)S(1)}) custom-call(bf16[72,2880]{1,0:T(8,128)(2,1)S(1)} %collective-permute-done.26.a, bf16[72,2880]{1,0:T(8,128)(2,1)S(1)} %collective-permute-done.27.b, bf16[72,2880]{1,0:T(8,128)(2,1)S(1)} %collective-permute-done.28.c, ...), custom_call_target="tpu_custom_call" | custom-call | tf_op jit(solution)/shard_map/pallas_call | solution.py:198
  89.0 0.5 collective-permute-start.30
  89.5 0.1 add_convert_fusion.7
  89.6 1.3 collective-permute-start.7
  90.9 0.1 add_convert_fusion.5
  91.0 0.3 collective-permute-start.14
  91.4 0.1 add_convert_fusion.3
  91.5 1.3 collective-permute-start.24
  92.8 0.1 add_convert_fusion.1
  92.9 0.3 collective-permute-start.31
  93.2 7.8 %collective-permute-done.7 = bf16[72,2880]{1,0:T(8,128)(2,1)S(1)} collective-permute-done((bf16[72,2880]{1,0:T(8,128)(2,1)S(1)}, bf16[72,2880]{1,0:T(8,128)(2,1)S(1)}, u32[]{:S(2)}, u32[]{:S(2)}) %collective-permute-start.7) | collective-permute-done | bytes 414752 | tf_op jit(solution)/shard_map/ppermute | solution.py:158
  101.0 0.2 add_convert_fusion.6
  101.2 0.8 collective-permute-start.8
  102.0 8.1 %collective-permute-done.14 = bf16[72,2880]{1,0:T(8,128)(2,1)S(1)} collective-permute-done((bf16[72,2880]{1,0:T(8,128)(2,1)S(1)}, bf16[72,2880]{1,0:T(8,128)(2,1)S(1)}, u32[]{:S(2)}, u32[]{:S(2)}) %collective-permute-start.14) | collective-permute-done | bytes 414752 | tf_op jit(solution)/shard_map/ppermute | solution.py:158
  110.1 0.2 add_convert_fusion.4
  110.3 0.1 collective-permute-start.15
  110.3 8.8 %collective-permute-done.24 = bf16[72,2880]{1,0:T(8,128)(2,1)S(1)} collective-permute-done((bf16[72,2880]{1,0:T(8,128)(2,1)S(1)}, bf16[72,2880]{1,0:T(8,128)(2,1)S(1)}, u32[]{:S(2)}, u32[]{:S(2)}) %collective-permute-start.24) | collective-permute-done | bytes 414752 | tf_op jit(solution)/shard_map/ppermute | solution.py:158
  119.2 0.2 add_convert_fusion.2
  119.4 8.8 %collective-permute-done.31 = bf16[72,2880]{1,0:T(8,128)(2,1)S(1)} collective-permute-done((bf16[72,2880]{1,0:T(8,128)(2,1)S(1)}, bf16[72,2880]{1,0:T(8,128)(2,1)S(1)}, u32[]{:S(2)}, u32[]{:S(2)}) %collective-permute-start.31) | collective-permute-done | bytes 414752 | tf_op jit(solution)/shard_map/ppermute | solution.py:158
  128.3 0.2 add_convert_fusion
  128.5 1.0 shard_map.65
  129.5 16.4 %collective-permute-done.25.refs_2_ = bf16[72,2880]{1,0:T(8,128)(2,1)S(1)} collective-permute-done((bf16[72,2880]{1,0:T(8,128)(2,1)S(1)}, bf16[72,2880]{1,0:T(8,128)(2,1)S(1)}, u32[]{:S(2)}, u32[]{:S(2)}) %collective-permute-start.25) | collective-permute-done | bytes 414752 | tf_op jit(solution)/shard_map/ppermute | solution.py:158
  145.9 12.3 %collective-permute-done.32.refs_3_ = bf16[72,2880]{1,0:T(8,128)(2,1)S(1)} collective-permute-done((bf16[72,2880]{1,0:T(8,128)(2,1)S(1)}, bf16[72,2880]{1,0:T(8,128)(2,1)S(1)}, u32[]{:S(2)}, u32[]{:S(2)}) %collective-permute-start.32) | collective-permute-done | bytes 414752 | tf_op jit(solution)/shard_map/ppermute | solution.py:158
  158.2 1.0 shard_map.71
  159.2 1.6 %collective-permute-start.33 = (bf16[64,2880]{1,0:T(8,128)(2,1)S(1)}, bf16[64,2880]{1,0:T(8,128)(2,1)S(1)}, u32[]{:S(2)}, u32[]{:S(2)}) collective-permute-start(bf16[64,2880]{1,0:T(8,128)(2,1)S(1)} %get-tuple-element.46), channel_id=1, source_target_pairs={{0,1},{1,0},{2,3},{3,2},{4,5},{5,4},{6,7},{7,6},{8,9},{9,8},{10,11... | collective-permute-start | bytes 1105928 | tf_op jit(solution)/shard_map/ppermute | solution.py:158
  160.9 1.3 collective-permute-done.33
  162.2 0.9 add_convert_fusion.8
  (34 shorter events, 0.3 us)
Async XLA Ops:
  0.0 5.1 %collective-permute-start = (bf16[64,2880]{1,0:T(8,128)(2,1)}, bf16[64,2880]{1,0:T(8,128)(2,1)S(1)}, u32[]{:S(2)}, u32[]{:S(2)}) collective-permute-start(bf16[64,2880]{1,0:T(8,128)(2,1)} %own.1), channel_id=1, source_target_pairs={{0,1},{1,0},{2,3},{3,2},{4,5},{5,4},{6,7},{7,6},{8,9},{9,8},{10,11... | collective-permute-start | bytes 1105928 | tf_op jit(solution)/shard_map/ppermute | solution.py:158
  0.7 19.1 %collective-permute-start.16 = (bf16[64,2880]{1,0:T(8,128)(2,1)}, bf16[64,2880]{1,0:T(8,128)(2,1)S(1)}, u32[]{:S(2)}, u32[]{:S(2)}) collective-permute-start(bf16[64,2880]{1,0:T(8,128)(2,1)} %own.1), channel_id=1, source_target_pairs={{0,16},{1,17},{2,18},{3,19},{4,20},{5,21},{6,22},{7,23},{8,24},{9,... | collective-permute-start | bytes 1105928 | tf_op jit(solution)/shard_map/ppermute | solution.py:158
  3.0 1.4 collective-permute-start.1
  5.1 1.0 copy-start.2
  7.3 13.9 %collective-permute-start.2 = (bf16[72,2880]{1,0:T(8,128)(2,1)S(1)}, bf16[72,2880]{1,0:T(8,128)(2,1)S(1)}, u32[]{:S(2)}, u32[]{:S(2)}) collective-permute-start(bf16[72,2880]{1,0:T(8,128)(2,1)S(1)} %get-tuple-element.29), channel_id=1, source_target_pairs={{0,0},{1,4},{2,2},{3,6},{4,1},{5,5},{6,3},{7,7},{8,8},{9,12},{10,1... | collective-permute-start | bytes 1244168 | tf_op jit(solution)/shard_map/ppermute | solution.py:158
  19.8 13.3 %collective-permute-start.17 = (bf16[64,2880]{1,0:T(8,128)(2,1)S(1)}, bf16[64,2880]{1,0:T(8,128)(2,1)S(1)}, u32[]{:S(2)}, u32[]{:S(2)}) collective-permute-start(bf16[64,2880]{1,0:T(8,128)(2,1)S(1)} %collective-permute-done.16.own), channel_id=1, source_target_pairs={{0,1},{1,0},{2,3},{3,2},{4,5},{5,4},{6,7},{7,6},{8,9},{9,8},{10,11... | collective-permute-start | bytes 1105928 | tf_op jit(solution)/shard_map/ppermute | solution.py:158
  20.2 17.7 %collective-permute-start.9 = (bf16[72,2880]{1,0:T(8,128)(2,1)S(1)}, bf16[72,2880]{1,0:T(8,128)(2,1)S(1)}, u32[]{:S(2)}, u32[]{:S(2)}) collective-permute-start(bf16[72,2880]{1,0:T(8,128)(2,1)S(1)} %get-tuple-element.33), channel_id=1, source_target_pairs={{0,8},{1,12},{2,10},{3,14},{4,9},{5,13},{6,11},{7,15},{8,0},{9,4},... | collective-permute-start | bytes 1244168 | tf_op jit(solution)/shard_map/ppermute | solution.py:158
  21.2 17.9 %collective-permute-start.3 = (bf16[72,2880]{1,0:T(8,128)(2,1)S(1)}, bf16[72,2880]{1,0:T(8,128)(2,1)S(1)}, u32[]{:S(2)}, u32[]{:S(2)}) collective-permute-start(bf16[72,2880]{1,0:T(8,128)(2,1)S(1)} %collective-permute-done.2.a), channel_id=1, source_target_pairs={{0,2},{1,3},{2,0},{3,1},{4,6},{5,7},{6,4},{7,5},{8,10},{9,11},{10,... | collective-permute-start | bytes 1244168 | tf_op jit(solution)/shard_map/ppermute | solution.py:158
  22.4 10.7 %collective-permute-start.18 = (s32[8,64]{1,0:T(8,128)S(1)}, s32[8,64]{1,0:T(8,128)S(1)}, u32[]{:S(2)}, u32[]{:S(2)}) collective-permute-start(s32[8,64]{1,0:T(8,128)S(1)} %pad_add_fusion.routes), channel_id=1, source_target_pairs={{0,16},{1,17},{2,18},{3,19},{4,20},{5,21},{6,22},{7,23},{8,24},{9,... | collective-permute-start | bytes 6152 | tf_op jit(solution)/shard_map/ppermute | solution.py:158
  34.9 4.6 %collective-permute-start.19 = (bf16[72,2880]{1,0:T(8,128)(2,1)S(1)}, bf16[72,2880]{1,0:T(8,128)(2,1)S(1)}, u32[]{:S(2)}, u32[]{:S(2)}) collective-permute-start(bf16[72,2880]{1,0:T(8,128)(2,1)S(1)} %get-tuple-element.37), channel_id=1, source_target_pairs={{0,0},{1,4},{2,2},{3,6},{4,1},{5,5},{6,3},{7,7},{8,8},{9,12},{10,1... | collective-permute-start | bytes 1244168 | tf_op jit(solution)/shard_map/ppermute | solution.py:158
  35.6 14.2 %collective-permute-start.26 = (bf16[72,2880]{1,0:T(8,128)(2,1)S(1)}, bf16[72,2880]{1,0:T(8,128)(2,1)S(1)}, u32[]{:S(2)}, u32[]{:S(2)}) collective-permute-start(bf16[72,2880]{1,0:T(8,128)(2,1)S(1)} %get-tuple-element.41), channel_id=1, source_target_pairs={{0,8},{1,12},{2,10},{3,14},{4,9},{5,13},{6,11},{7,15},{8,0},{9,4},... | collective-permute-start | bytes 1244168 | tf_op jit(solution)/shard_map/ppermute | solution.py:158
  35.7 15.4 %collective-permute-start.4 = (bf16[72,2880]{1,0:T(8,128)(2,1)S(1)}, bf16[72,2880]{1,0:T(8,128)(2,1)S(1)}, u32[]{:S(2)}, u32[]{:S(2)}) collective-permute-start(bf16[72,2880]{1,0:T(8,128)(2,1)S(1)} %collective-permute-done.2.a), channel_id=1, source_target_pairs={{0,1},{1,0},{2,3},{3,2},{4,5},{5,4},{6,7},{7,6},{8,9},{9,8},{10,11... | collective-permute-start | bytes 1244168 | tf_op jit(solution)/shard_map/ppermute | solution.py:158
  37.9 13.4 %collective-permute-start.10 = (bf16[72,2880]{1,0:T(8,128)(2,1)S(1)}, bf16[72,2880]{1,0:T(8,128)(2,1)S(1)}, u32[]{:S(2)}, u32[]{:S(2)}) collective-permute-start(bf16[72,2880]{1,0:T(8,128)(2,1)S(1)} %collective-permute-done.9.a), channel_id=1, source_target_pairs={{0,2},{1,3},{2,0},{3,1},{4,6},{5,7},{6,4},{7,5},{8,10},{9,11},{10,... | collective-permute-start | bytes 1244168 | tf_op jit(solution)/shard_map/ppermute | solution.py:158
  39.2 12.7 %collective-permute-start.5 = (bf16[72,2880]{1,0:T(8,128)(2,1)S(1)}, bf16[72,2880]{1,0:T(8,128)(2,1)S(1)}, u32[]{:S(2)}, u32[]{:S(2)}) collective-permute-start(bf16[72,2880]{1,0:T(8,128)(2,1)S(1)} %collective-permute-done.3.b), channel_id=1, source_target_pairs={{0,1},{1,0},{2,3},{3,2},{4,5},{5,4},{6,7},{7,6},{8,9},{9,8},{10,11... | collective-permute-start | bytes 1244168 | tf_op jit(solution)/shard_map/ppermute | solution.py:158
  39.5 19.9 %collective-permute-start.11 = (bf16[72,2880]{1,0:T(8,128)(2,1)S(1)}, bf16[72,2880]{1,0:T(8,128)(2,1)S(1)}, u32[]{:S(2)}, u32[]{:S(2)}) collective-permute-start(bf16[72,2880]{1,0:T(8,128)(2,1)S(1)} %collective-permute-done.9.a), channel_id=1, source_target_pairs={{0,1},{1,0},{2,3},{3,2},{4,5},{5,4},{6,7},{7,6},{8,9},{9,8},{10,11... | collective-permute-start | bytes 1244168 | tf_op jit(solution)/shard_map/ppermute | solution.py:158
  49.8 11.3 %collective-permute-start.20 = (bf16[72,2880]{1,0:T(8,128)(2,1)S(1)}, bf16[72,2880]{1,0:T(8,128)(2,1)S(1)}, u32[]{:S(2)}, u32[]{:S(2)}) collective-permute-start(bf16[72,2880]{1,0:T(8,128)(2,1)S(1)} %collective-permute-done.19.a), channel_id=1, source_target_pairs={{0,2},{1,3},{2,0},{3,1},{4,6},{5,7},{6,4},{7,5},{8,10},{9,11},{10,... | collective-permute-start | bytes 1244168 | tf_op jit(solution)/shard_map/ppermute | solution.py:158
  51.1 19.2 %collective-permute-start.27 = (bf16[72,2880]{1,0:T(8,128)(2,1)S(1)}, bf16[72,2880]{1,0:T(8,128)(2,1)S(1)}, u32[]{:S(2)}, u32[]{:S(2)}) collective-permute-start(bf16[72,2880]{1,0:T(8,128)(2,1)S(1)} %collective-permute-done.26.a), channel_id=1, source_target_pairs={{0,2},{1,3},{2,0},{3,1},{4,6},{5,7},{6,4},{7,5},{8,10},{9,11},{10,... | collective-permute-start | bytes 1244168 | tf_op jit(solution)/shard_map/ppermute | solution.py:158
  51.3 19.8 %collective-permute-start.12 = (bf16[72,2880]{1,0:T(8,128)(2,1)S(1)}, bf16[72,2880]{1,0:T(8,128)(2,1)S(1)}, u32[]{:S(2)}, u32[]{:S(2)}) collective-permute-start(bf16[72,2880]{1,0:T(8,128)(2,1)S(1)} %collective-permute-done.10.b), channel_id=1, source_target_pairs={{0,1},{1,0},{2,3},{3,2},{4,5},{5,4},{6,7},{7,6},{8,9},{9,8},{10,11... | collective-permute-start | bytes 1244168 | tf_op jit(solution)/shard_map/ppermute | solution.py:158
  51.9 1.6 copy-start
  53.5 17.6 %copy-start.1 = (bf16[1,360,2880]{2,1,0:T(8,128)(2,1)S(1)}, bf16[1,360,2880]{2,1,0:T(8,128)(2,1)}, u32[]{:S(2)}) copy-start(bf16[1,360,2880]{2,1,0:T(8,128)(2,1)} %param.11) | copy-start | bytes 6220804
  59.3 30.2 %collective-permute-start.6 = (bf16[144,2880]{1,0:T(8,128)(2,1)S(1)}, bf16[144,2880]{1,0:T(8,128)(2,1)S(1)}, u32[]{:S(2)}, u32[]{:S(2)}) collective-permute-start(bf16[144,2880]{1,0:T(8,128)(2,1)S(1)} %get-tuple-element.31), channel_id=1, source_target_pairs={{0,1},{1,0},{2,3},{3,2},{4,5},{5,4},{6,7},{7,6},{8,9},{9,8},{10,11... | collective-permute-start | bytes 2488328 | tf_op jit(solution)/shard_map/ppermute | solution.py:158
  59.4 17.4 %collective-permute-start.21 = (bf16[72,2880]{1,0:T(8,128)(2,1)S(1)}, bf16[72,2880]{1,0:T(8,128)(2,1)S(1)}, u32[]{:S(2)}, u32[]{:S(2)}) collective-permute-start(bf16[72,2880]{1,0:T(8,128)(2,1)S(1)} %collective-permute-done.19.a), channel_id=1, source_target_pairs={{0,1},{1,0},{2,3},{3,2},{4,5},{5,4},{6,7},{7,6},{8,9},{9,8},{10,11... | collective-permute-start | bytes 1244168 | tf_op jit(solution)/shard_map/ppermute | solution.py:158
  61.2 16.3 %collective-permute-start.22 = (bf16[72,2880]{1,0:T(8,128)(2,1)S(1)}, bf16[72,2880]{1,0:T(8,128)(2,1)S(1)}, u32[]{:S(2)}, u32[]{:S(2)}) collective-permute-start(bf16[72,2880]{1,0:T(8,128)(2,1)S(1)} %collective-permute-done.20.b), channel_id=1, source_target_pairs={{0,1},{1,0},{2,3},{3,2},{4,5},{5,4},{6,7},{7,6},{8,9},{9,8},{10,11... | collective-permute-start | bytes 1244168 | tf_op jit(solution)/shard_map/ppermute | solution.py:158
  70.2 13.0 %collective-permute-start.28 = (bf16[72,2880]{1,0:T(8,128)(2,1)S(1)}, bf16[72,2880]{1,0:T(8,128)(2,1)S(1)}, u32[]{:S(2)}, u32[]{:S(2)}) collective-permute-start(bf16[72,2880]{1,0:T(8,128)(2,1)S(1)} %collective-permute-done.26.a), channel_id=1, source_target_pairs={{0,1},{1,0},{2,3},{3,2},{4,5},{5,4},{6,7},{7,6},{8,9},{9,8},{10,11... | collective-permute-start | bytes 1244168 | tf_op jit(solution)/shard_map/ppermute | solution.py:158
  71.1 12.1 %collective-permute-start.29 = (bf16[72,2880]{1,0:T(8,128)(2,1)S(1)}, bf16[72,2880]{1,0:T(8,128)(2,1)S(1)}, u32[]{:S(2)}, u32[]{:S(2)}) collective-permute-start(bf16[72,2880]{1,0:T(8,128)(2,1)S(1)} %collective-permute-done.27.b), channel_id=1, source_target_pairs={{0,1},{1,0},{2,3},{3,2},{4,5},{5,4},{6,7},{7,6},{8,9},{9,8},{10,11... | collective-permute-start | bytes 1244168 | tf_op jit(solution)/shard_map/ppermute | solution.py:158
  76.9 14.1 %collective-permute-start.13 = (bf16[144,2880]{1,0:T(8,128)(2,1)S(1)}, bf16[144,2880]{1,0:T(8,128)(2,1)S(1)}, u32[]{:S(2)}, u32[]{:S(2)}) collective-permute-start(bf16[144,2880]{1,0:T(8,128)(2,1)S(1)} %get-tuple-element.35), channel_id=1, source_target_pairs={{0,1},{1,0},{2,3},{3,2},{4,5},{5,4},{6,7},{7,6},{8,9},{9,8},{10,11... | collective-permute-start | bytes 2488328 | tf_op jit(solution)/shard_map/ppermute | solution.py:158
  83.2 8.2 %collective-permute-start.23 = (bf16[144,2880]{1,0:T(8,128)(2,1)S(1)}, bf16[144,2880]{1,0:T(8,128)(2,1)S(1)}, u32[]{:S(2)}, u32[]{:S(2)}) collective-permute-start(bf16[144,2880]{1,0:T(8,128)(2,1)S(1)} %get-tuple-element.39), channel_id=1, source_target_pairs={{0,1},{1,0},{2,3},{3,2},{4,5},{5,4},{6,7},{7,6},{8,9},{9,8},{10,11... | collective-permute-start | bytes 2488328 | tf_op jit(solution)/shard_map/ppermute | solution.py:158
  89.0 3.8 %collective-permute-start.30 = (bf16[144,2880]{1,0:T(8,128)(2,1)S(1)}, bf16[144,2880]{1,0:T(8,128)(2,1)S(1)}, u32[]{:S(2)}, u32[]{:S(2)}) collective-permute-start(bf16[144,2880]{1,0:T(8,128)(2,1)S(1)} %get-tuple-element.43), channel_id=1, source_target_pairs={{0,1},{1,0},{2,3},{3,2},{4,5},{5,4},{6,7},{7,6},{8,9},{9,8},{10,11... | collective-permute-start | bytes 2488328 | tf_op jit(solution)/shard_map/ppermute | solution.py:158
  89.6 11.4 %collective-permute-start.7 = (bf16[72,2880]{1,0:T(8,128)(2,1)S(1)}, bf16[72,2880]{1,0:T(8,128)(2,1)S(1)}, u32[]{:S(2)}, u32[]{:S(2)}) collective-permute-start(bf16[72,2880]{1,0:T(8,128)(2,1)S(1)} %add_convert_fusion.7), channel_id=1, source_target_pairs={{0,2},{1,3},{2,0},{3,1},{4,6},{5,7},{6,4},{7,5},{8,10},{9,11},{10,... | collective-permute-start | bytes 1244168 | tf_op jit(solution)/shard_map/ppermute | solution.py:158
  91.0 19.1 %collective-permute-start.14 = (bf16[72,2880]{1,0:T(8,128)(2,1)S(1)}, bf16[72,2880]{1,0:T(8,128)(2,1)S(1)}, u32[]{:S(2)}, u32[]{:S(2)}) collective-permute-start(bf16[72,2880]{1,0:T(8,128)(2,1)S(1)} %add_convert_fusion.5), channel_id=1, source_target_pairs={{0,2},{1,3},{2,0},{3,1},{4,6},{5,7},{6,4},{7,5},{8,10},{9,11},{10,... | collective-permute-start | bytes 1244168 | tf_op jit(solution)/shard_map/ppermute | solution.py:158
  91.5 37.0 %copy-start.4 = (bf16[2880,8]{0,1:T(8,128)(2,1)S(1)}, bf16[2880,8]{0,1:T(8,128)(2,1)}, u32[]{:S(2)}) copy-start(bf16[2880,8]{0,1:T(8,128)(2,1)} %param.9) | copy-start | bytes 138244
  91.5 27.7 %collective-permute-start.24 = (bf16[72,2880]{1,0:T(8,128)(2,1)S(1)}, bf16[72,2880]{1,0:T(8,128)(2,1)S(1)}, u32[]{:S(2)}, u32[]{:S(2)}) collective-permute-start(bf16[72,2880]{1,0:T(8,128)(2,1)S(1)} %add_convert_fusion.3), channel_id=1, source_target_pairs={{0,2},{1,3},{2,0},{3,1},{4,6},{5,7},{6,4},{7,5},{8,10},{9,11},{10,... | collective-permute-start | bytes 1244168 | tf_op jit(solution)/shard_map/ppermute | solution.py:158
  92.9 35.4 %collective-permute-start.31 = (bf16[72,2880]{1,0:T(8,128)(2,1)S(1)}, bf16[72,2880]{1,0:T(8,128)(2,1)S(1)}, u32[]{:S(2)}, u32[]{:S(2)}) collective-permute-start(bf16[72,2880]{1,0:T(8,128)(2,1)S(1)} %add_convert_fusion.1), channel_id=1, source_target_pairs={{0,2},{1,3},{2,0},{3,1},{4,6},{5,7},{6,4},{7,5},{8,10},{9,11},{10,... | collective-permute-start | bytes 1244168 | tf_op jit(solution)/shard_map/ppermute | solution.py:158
  101.2 61.0 %copy-start.3 = (bf16[64,2880]{1,0:T(8,128)(2,1)S(1)}, bf16[64,2880]{1,0:T(8,128)(2,1)}, u32[]{:S(2)}) copy-start(bf16[64,2880]{1,0:T(8,128)(2,1)} %own.1) | copy-start | bytes 1105924
  101.2 28.3 %collective-permute-start.8 = (bf16[72,2880]{1,0:T(8,128)(2,1)S(1)}, bf16[72,2880]{1,0:T(8,128)(2,1)S(1)}, u32[]{:S(2)}, u32[]{:S(2)}) collective-permute-start(bf16[72,2880]{1,0:T(8,128)(2,1)S(1)} %add_convert_fusion.6), channel_id=1, source_target_pairs={{0,0},{1,4},{2,2},{3,6},{4,1},{5,5},{6,3},{7,7},{8,8},{9,12},{10,1... | collective-permute-start | bytes 1244168 | tf_op jit(solution)/shard_map/ppermute | solution.py:158
  110.3 19.3 %collective-permute-start.15 = (bf16[72,2880]{1,0:T(8,128)(2,1)S(1)}, bf16[72,2880]{1,0:T(8,128)(2,1)S(1)}, u32[]{:S(2)}, u32[]{:S(2)}) collective-permute-start(bf16[72,2880]{1,0:T(8,128)(2,1)S(1)} %add_convert_fusion.4), channel_id=1, source_target_pairs={{0,8},{1,12},{2,10},{3,14},{4,9},{5,13},{6,11},{7,15},{8,0},{9,4},... | collective-permute-start | bytes 1244168 | tf_op jit(solution)/shard_map/ppermute | solution.py:158
  119.4 26.6 %collective-permute-start.25 = (bf16[72,2880]{1,0:T(8,128)(2,1)S(1)}, bf16[72,2880]{1,0:T(8,128)(2,1)S(1)}, u32[]{:S(2)}, u32[]{:S(2)}) collective-permute-start(bf16[72,2880]{1,0:T(8,128)(2,1)S(1)} %add_convert_fusion.2), channel_id=1, source_target_pairs={{0,16},{1,20},{2,18},{3,22},{4,17},{5,21},{6,19},{7,23},{8,24},{9,... | collective-permute-start | bytes 1244168 | tf_op jit(solution)/shard_map/ppermute | solution.py:158
  128.4 29.8 %collective-permute-start.32 = (bf16[72,2880]{1,0:T(8,128)(2,1)S(1)}, bf16[72,2880]{1,0:T(8,128)(2,1)S(1)}, u32[]{:S(2)}, u32[]{:S(2)}) collective-permute-start(bf16[72,2880]{1,0:T(8,128)(2,1)S(1)} %add_convert_fusion), channel_id=1, source_target_pairs={{0,24},{1,28},{2,26},{3,30},{4,25},{5,29},{6,27},{7,31},{8,16},{9,... | collective-permute-start | bytes 1244168 | tf_op jit(solution)/shard_map/ppermute | solution.py:158
  159.2 3.0 %collective-permute-start.33 = (bf16[64,2880]{1,0:T(8,128)(2,1)S(1)}, bf16[64,2880]{1,0:T(8,128)(2,1)S(1)}, u32[]{:S(2)}, u32[]{:S(2)}) collective-permute-start(bf16[64,2880]{1,0:T(8,128)(2,1)S(1)} %get-tuple-element.46), channel_id=1, source_target_pairs={{0,1},{1,0},{2,3},{3,2},{4,5},{5,4},{6,7},{7,6},{8,9},{9,8},{10,11... | collective-permute-start | bytes 1105928 | tf_op jit(solution)/shard_map/ppermute | solution.py:158

commit v5 on v2

--- a/solution.py
+++ b/solution.py
@@ -10,7 +10,7 @@
 
 CORES = 2
 SHARDS = 4
-VMEM_BYTES = 48 * 1024 * 1024
+VMEM_BYTES = 16 * 1024 * 1024
 
 
 def dot32(a, b, dims=((1,), (0,))):
@@ -80,17 +80,20 @@
         )
 
 
-def expert_kernel(a, b, c, d, gate_up, down, mine_a, mine_b, send, *, ff):
-    rows = a.shape[0]
-    values = jnp.concatenate([a[...], b[...], c[...], d[...]], axis=0)
-    hidden = dot32(values, gate_up[...], ((1,), (1,)))
+def turn_kernel(stored, turned):
+    turned[...] = stored[...].T
+
+
+def expert_kernel(mine_in, other_in, gate_up, down, mine, send, *, ff):
+    rows = mine.shape[0]
+    values = jnp.concatenate([mine_in[...], other_in[...]], axis=0)
+    hidden = dot32(values, gate_up[...])
     gate = hidden[:, :ff]
     up = hidden[:, ff:]
     activated = ((up + 1.0) * gate * jax.nn.sigmoid(1.702 * gate)).astype(jnp.bfloat16)
     partial_value = dot32(activated, down[...]).astype(jnp.bfloat16)
-    mine_a[...] = partial_value[0:rows]
-    mine_b[...] = partial_value[rows : 2 * rows]
-    send[...] = partial_value[2 * rows :]
+    mine[...] = partial_value[:rows]
+    send[...] = partial_value[rows:]
 
 
 def combine_kernel(high, low, *refs):
@@ -172,29 +175,26 @@
         functools.partial(weight_kernel, experts=experts, cap=cap), [weights, weights], 1, 5
     )(ids, normed, router_weight.T, routes, routes_other)
 
-    gate_up = gate_up_weight[0].T
+    stored = gate_up_weight[0].T
+    gate_up = vmem_call(
+        turn_kernel, jax.ShapeDtypeStruct(stored.shape[::-1], stored.dtype), 0, 1
+    )(stored)
     down = down_weight[0]
+    wide = jnp.float32
+
+    def expert(mine, other):
+        mine, send = vmem_call(
+            functools.partial(expert_kernel, ff=ff), [block, block], 0, 4
+        )(mine, other, gate_up, down)
+        return mine.astype(wide) + move(send, to_core).astype(wide)
+
     back = []
     for m in range(chunks):
         side = move(near[m], to_x)
-        near_other = move(near[m], to_core)
-        side_other = move(side, to_core)
-        mine, mine_side, send = vmem_call(
-            functools.partial(expert_kernel, ff=ff),
-            [block, block, jax.ShapeDtypeStruct((2 * pair, width), jnp.bfloat16)],
-            0,
-            6,
-        )(near[m], side, near_other, side_other, gate_up, down)
-        got = move(send, to_core)
-        got_mine, got_side = got[:pair], got[pair:]
-        out_side = (mine_side.astype(jnp.float32) + got_side.astype(jnp.float32)).astype(
-            jnp.bfloat16
-        )
-        in_side = move(out_side, to_x)
-        total = (
-            mine.astype(jnp.float32) + got_mine.astype(jnp.float32) + in_side.astype(jnp.float32)
-        ).astype(jnp.bfloat16)
-        back.append(move(total, far[m]))
+        own_sum = expert(near[m], move(near[m], to_core))
+        side_sum = expert(side, move(side, to_core))
+        in_side = move(side_sum.astype(jnp.bfloat16), to_x)
+        back.append(move((own_sum + in_side.astype(wide)).astype(jnp.bfloat16), far[m]))
 
     mixed_own, mixed_other = vmem_call(
         combine_kernel,

time: 158 us -> 162 us (1.025); the launches traced: 158 us -> 160 us
  waiting for transfers between devices: 59.2 us -> 73.3 us
  starting transfers between devices: 66 us -> 58.9 us
  Pallas kernels: 26.5 us -> 20.8 us
    ppermute x31 -> x35, waiting for transfers between devices: 59.2 us -> 73.3 us  [move(): return lax.ppermute(value, 'ep', perm)]
    ppermute x31 -> x35, starting transfers between devices: 66 us -> 58.9 us  [move(): return lax.ppermute(value, 'ep', perm)]
    pallas_call x4 -> x9, Pallas kernels: 23 us -> 17.3 us  [the longest x8 16.1 us: expert(): vmem_call(functools.partial(expert_kernel, ff=ff), [block, block], 0, 4)]
  transfers between devices with their start and end apart: 31 -> 35, of which waited for: 8 -> 14; matrix products, arithmetic and copies ran while one was open for 1% -> 1% of each run, Pallas kernels for 15% -> 11%
where the time goes in v5:
time: 162 us; the launch traced here: 160 us
  waiting for transfers between devices  73.3 us (45%)
  starting transfers between devices  58.9 us (36%)
  Pallas kernels  20.8 us (13%)
  local copies, waits for them, and re-layouts  4.68 us (3%)
  other arithmetic  1.9 us (1%)
    ppermute x35, waiting for transfers between devices, move(): return lax.ppermute(value, 'ep', perm)  73.3 us
    ppermute x35, starting transfers between devices, move(): return lax.ppermute(value, 'ep', perm)  58.9 us
    pallas_call x8, Pallas kernels, expert(): vmem_call(functools.partial(expert_kernel, ff=ff), [block, block], 0, 4)  16.1 us
    unnamed x14, local copies, waits for them, and re-layouts  3.89 us
  transfers between devices with their start and end apart: 35, of which 14 were waited for; matrix products, arithmetic and copies ran while one was open for 1% of the time, Pallas kernels for 11%

profile of v5, /device:TPU:13, one launch (start us, length us, event | category | flops | bytes accessed | tf_op | source)
XLA Modules:
  0.0 159.8 jit_solution(4309855690019181199)
XLA Ops:
  0.0 0.7 collective-permute-start
  0.7 0.7 reshape.3.gain
  1.5 0.8 collective-permute-done.1.routes_other
  2.2 1.0 copy-done.2
  3.2 0.7 copy-done.5
  3.9 1.5 shard_map.64
  5.4 0.7 collective-permute-start.2
  6.1 0.2 collective-permute-start.10
  6.3 2.3 %collective-permute-start.18 = (bf16[72,2880]{1,0:T(8,128)(2,1)S(1)}, bf16[72,2880]{1,0:T(8,128)(2,1)S(1)}, u32[]{:S(2)}, u32[]{:S(2)}) collective-permute-start(bf16[72,2880]{1,0:T(8,128)(2,1)S(1)} %get-tuple-element.43), channel_id=1, source_target_pairs={{0,16},{1,20},{2,18},{3,22},{4,17},{5,21},{6,19},{7,23},{8,24},{9,... | collective-permute-start | bytes 1244168 | tf_op jit(solution)/shard_map/ppermute | solution.py:158
  8.6 0.2 collective-permute-start.26
  8.8 1.2 collective-permute-start.5
  10.0 10.0 %collective-permute-start.3 = (bf16[72,2880]{1,0:T(8,128)(2,1)S(1)}, bf16[72,2880]{1,0:T(8,128)(2,1)S(1)}, u32[]{:S(2)}, u32[]{:S(2)}) collective-permute-start(bf16[72,2880]{1,0:T(8,128)(2,1)S(1)} %collective-permute-done.2.mine_in), channel_id=1, source_target_pairs={{0,1},{1,0},{2,3},{3,2},{4,5},{5,4},{6,7},{7,6},{8,9},{9,8},{10,11... | collective-permute-start | bytes 1244168 | tf_op jit(solution)/shard_map/ppermute | solution.py:158
  19.9 0.7 collective-permute-done.10.mine_in
  20.7 1.2 collective-permute-start.13
  21.9 2.9 %collective-permute-done.18.mine_in = bf16[72,2880]{1,0:T(8,128)(2,1)S(1)} collective-permute-done((bf16[72,2880]{1,0:T(8,128)(2,1)S(1)}, bf16[72,2880]{1,0:T(8,128)(2,1)S(1)}, u32[]{:S(2)}, u32[]{:S(2)}) %collective-permute-start.18) | collective-permute-done | bytes 414752 | tf_op jit(solution)/shard_map/ppermute | solution.py:158
  24.8 15.1 %collective-permute-start.11 = (bf16[72,2880]{1,0:T(8,128)(2,1)S(1)}, bf16[72,2880]{1,0:T(8,128)(2,1)S(1)}, u32[]{:S(2)}, u32[]{:S(2)}) collective-permute-start(bf16[72,2880]{1,0:T(8,128)(2,1)S(1)} %collective-permute-done.10.mine_in), channel_id=1, source_target_pairs={{0,1},{1,0},{2,3},{3,2},{4,5},{5,4},{6,7},{7,6},{8,9},{9,8},{10,11... | collective-permute-start | bytes 1244168 | tf_op jit(solution)/shard_map/ppermute | solution.py:158
  40.0 3.3 %collective-permute-done.26.mine_in = bf16[72,2880]{1,0:T(8,128)(2,1)S(1)} collective-permute-done((bf16[72,2880]{1,0:T(8,128)(2,1)S(1)}, bf16[72,2880]{1,0:T(8,128)(2,1)S(1)}, u32[]{:S(2)}, u32[]{:S(2)}) %collective-permute-start.26) | collective-permute-done | bytes 414752 | tf_op jit(solution)/shard_map/ppermute | solution.py:158
  43.2 1.2 collective-permute-start.21
  44.5 0.3 collective-permute-start.29
  44.7 5.2 %collective-permute-start.6 = (bf16[72,2880]{1,0:T(8,128)(2,1)S(1)}, bf16[72,2880]{1,0:T(8,128)(2,1)S(1)}, u32[]{:S(2)}, u32[]{:S(2)}) collective-permute-start(bf16[72,2880]{1,0:T(8,128)(2,1)S(1)} %collective-permute-done.5.mine_in), channel_id=1, source_target_pairs={{0,1},{1,0},{2,3},{3,2},{4,5},{5,4},{6,7},{7,6},{8,9},{9,8},{10,11... | collective-permute-start | bytes 1244168 | tf_op jit(solution)/shard_map/ppermute | solution.py:158
  50.0 0.4 collective-permute-start.27
  50.4 9.6 %collective-permute-start.14 = (bf16[72,2880]{1,0:T(8,128)(2,1)S(1)}, bf16[72,2880]{1,0:T(8,128)(2,1)S(1)}, u32[]{:S(2)}, u32[]{:S(2)}) collective-permute-start(bf16[72,2880]{1,0:T(8,128)(2,1)S(1)} %collective-permute-done.13.mine_in), channel_id=1, source_target_pairs={{0,1},{1,0},{2,3},{3,2},{4,5},{5,4},{6,7},{7,6},{8,9},{9,8},{10,11... | collective-permute-start | bytes 1244168 | tf_op jit(solution)/shard_map/ppermute | solution.py:158
  60.0 2.2 %copy-done.1 = bf16[1,2880,720]{1,2,0:T(8,128)(2,1)S(1)} copy-done((bf16[1,2880,720]{1,2,0:T(8,128)(2,1)S(1)}, bf16[1,2880,720]{1,2,0:T(8,128)(2,1)}, u32[]{:S(2)}) %copy-start.1) | copy-done | bytes 4147224
  62.2 1.2 shard_map.66.gate_up
  63.4 1.1 collective-permute-start.22
  64.5 2.0 %shard_map.68 = (bf16[72,2880]{1,0:T(8,128)(2,1)S(1)}, bf16[72,2880]{1,0:T(8,128)(2,1)S(1)}) custom-call(bf16[72,2880]{1,0:T(8,128)(2,1)S(1)} %collective-permute-done.5.mine_in, bf16[72,2880]{1,0:T(8,128)(2,1)S(1)} %collective-permute-done.6.other_in, bf16[2880,720]{1,0:T(8,128)(2,1)S(1)} %shard_map.66.gate_up, bf16[360,2880]{1,0:T(8,128)(2,1)S(1)} %bitcast.11), custom_call_target="tpu_custom_call" | custom-call | tf_op jit(solution)/shard_map/pallas_call | solution.py:186
  66.5 0.6 collective-permute-start.7
  67.1 2.0 %shard_map.67 = (bf16[72,2880]{1,0:T(8,128)(2,1)S(1)}, bf16[72,2880]{1,0:T(8,128)(2,1)S(1)}) custom-call(bf16[72,2880]{1,0:T(8,128)(2,1)S(1)} %collective-permute-done.2.mine_in, bf16[72,2880]{1,0:T(8,128)(2,1)S(1)} %collective-permute-done.3.other_in, bf16[2880,720]{1,0:T(8,128)(2,1)S(1)} %shard_map.66.gate_up, bf16[360,2880]{1,0:T(8,128)(2,1)S(1)} %bitcast.12), custom_call_target="tpu_custom_call" | custom-call | tf_op jit(solution)/shard_map/pallas_call | solution.py:186
  69.1 2.0 %shard_map.69 = (bf16[72,2880]{1,0:T(8,128)(2,1)S(1)}, bf16[72,2880]{1,0:T(8,128)(2,1)S(1)}) custom-call(bf16[72,2880]{1,0:T(8,128)(2,1)S(1)} %collective-permute-done.10.mine_in, bf16[72,2880]{1,0:T(8,128)(2,1)S(1)} %collective-permute-done.11.other_in, bf16[2880,720]{1,0:T(8,128)(2,1)S(1)} %shard_map.66.gate_up, bf16[360,2880]{1,0:T(8,128)(2,1)S(1)} %bitcast.13), custom_call_target="tpu_custom_call" | custom-call | tf_op jit(solution)/shard_map/pallas_call | solution.py:186
  71.1 2.0 %shard_map.71 = (bf16[72,2880]{1,0:T(8,128)(2,1)S(1)}, bf16[72,2880]{1,0:T(8,128)(2,1)S(1)}) custom-call(bf16[72,2880]{1,0:T(8,128)(2,1)S(1)} %collective-permute-done.18.mine_in, bf16[72,2880]{1,0:T(8,128)(2,1)S(1)} %collective-permute-done.19.other_in, bf16[2880,720]{1,0:T(8,128)(2,1)S(1)} %shard_map.66.gate_up, bf16[360,2880]{1,0:T(8,128)(2,1)S(1)} %bitcast.14), custom_call_target="tpu_custom_call" | custom-call | tf_op jit(solution)/shard_map/pallas_call | solution.py:186
  73.2 2.0 %shard_map.73 = (bf16[72,2880]{1,0:T(8,128)(2,1)S(1)}, bf16[72,2880]{1,0:T(8,128)(2,1)S(1)}) custom-call(bf16[72,2880]{1,0:T(8,128)(2,1)S(1)} %collective-permute-done.26.mine_in, bf16[72,2880]{1,0:T(8,128)(2,1)S(1)} %collective-permute-done.27.other_in, bf16[2880,720]{1,0:T(8,128)(2,1)S(1)} %shard_map.66.gate_up, bf16[360,2880]{1,0:T(8,128)(2,1)S(1)} %bitcast.15), custom_call_target="tpu_custom_call" | custom-call | tf_op jit(solution)/shard_map/pallas_call | solution.py:186
  75.2 0.6 collective-permute-start.12
  75.7 2.0 %shard_map.70 = (bf16[72,2880]{1,0:T(8,128)(2,1)S(1)}, bf16[72,2880]{1,0:T(8,128)(2,1)S(1)}) custom-call(bf16[72,2880]{1,0:T(8,128)(2,1)S(1)} %collective-permute-done.13.mine_in, bf16[72,2880]{1,0:T(8,128)(2,1)S(1)} %collective-permute-done.14.other_in, bf16[2880,720]{1,0:T(8,128)(2,1)S(1)} %shard_map.66.gate_up, bf16[360,2880]{1,0:T(8,128)(2,1)S(1)} %bitcast.16), custom_call_target="tpu_custom_call" | custom-call | tf_op jit(solution)/shard_map/pallas_call | solution.py:186
  77.8 2.2 %shard_map.72 = (bf16[72,2880]{1,0:T(8,128)(2,1)S(1)}, bf16[72,2880]{1,0:T(8,128)(2,1)S(1)}) custom-call(bf16[72,2880]{1,0:T(8,128)(2,1)S(1)} %collective-permute-done.21.mine_in, bf16[72,2880]{1,0:T(8,128)(2,1)S(1)} %collective-permute-done.22.other_in, bf16[2880,720]{1,0:T(8,128)(2,1)S(1)} %shard_map.66.gate_up, bf16[360,2880]{1,0:T(8,128)(2,1)S(1)} %bitcast.17), custom_call_target="tpu_custom_call" | custom-call | tf_op jit(solution)/shard_map/pallas_call | solution.py:186
  80.0 0.6 collective-permute-start.28
  80.6 2.0 %shard_map.74 = (bf16[72,2880]{1,0:T(8,128)(2,1)S(1)}, bf16[72,2880]{1,0:T(8,128)(2,1)S(1)}) custom-call(bf16[72,2880]{1,0:T(8,128)(2,1)S(1)} %collective-permute-done.29.mine_in, bf16[72,2880]{1,0:T(8,128)(2,1)S(1)} %collective-permute-done.30.other_in, bf16[2880,720]{1,0:T(8,128)(2,1)S(1)} %shard_map.66.gate_up, bf16[360,2880]{1,0:T(8,128)(2,1)S(1)} %bitcast.18), custom_call_target="tpu_custom_call" | custom-call | tf_op jit(solution)/shard_map/pallas_call | solution.py:186
  82.8 1.6 %collective-permute-done.15 = bf16[72,2880]{1,0:T(8,128)(2,1)S(1)} collective-permute-done((bf16[72,2880]{1,0:T(8,128)(2,1)S(1)}, bf16[72,2880]{1,0:T(8,128)(2,1)S(1)}, u32[]{:S(2)}, u32[]{:S(2)}) %collective-permute-start.15) | collective-permute-done | bytes 414752 | tf_op jit(solution)/shard_map/ppermute | solution.py:158
  84.4 0.1 collective-permute-start.23
  84.7 1.5 collective-permute-done.23
  86.2 0.1 collective-permute-start.31
  86.4 1.5 collective-permute-done.31
  88.0 1.2 collective-permute-start.8
  89.2 0.1 add_convert_fusion.1
  89.3 0.3 collective-permute-start.16
  89.6 9.5 %collective-permute-done.8 = bf16[72,2880]{1,0:T(8,128)(2,1)S(1)} collective-permute-done((bf16[72,2880]{1,0:T(8,128)(2,1)S(1)}, bf16[72,2880]{1,0:T(8,128)(2,1)S(1)}, u32[]{:S(2)}, u32[]{:S(2)}) %collective-permute-start.8) | collective-permute-done | bytes 414752 | tf_op jit(solution)/shard_map/ppermute | solution.py:158
  99.1 1.2 collective-permute-start.24
  100.4 0.2 add_convert_fusion.6
  100.5 0.3 collective-permute-start.32
  100.9 7.4 %collective-permute-done.16 = bf16[72,2880]{1,0:T(8,128)(2,1)S(1)} collective-permute-done((bf16[72,2880]{1,0:T(8,128)(2,1)S(1)}, bf16[72,2880]{1,0:T(8,128)(2,1)S(1)}, u32[]{:S(2)}, u32[]{:S(2)}) %collective-permute-start.16) | collective-permute-done | bytes 414752 | tf_op jit(solution)/shard_map/ppermute | solution.py:158
  108.2 0.7 collective-permute-start.9
  108.9 0.2 add_convert_fusion.4
  109.2 8.1 %collective-permute-done.24 = bf16[72,2880]{1,0:T(8,128)(2,1)S(1)} collective-permute-done((bf16[72,2880]{1,0:T(8,128)(2,1)S(1)}, bf16[72,2880]{1,0:T(8,128)(2,1)S(1)}, u32[]{:S(2)}, u32[]{:S(2)}) %collective-permute-start.24) | collective-permute-done | bytes 414752 | tf_op jit(solution)/shard_map/ppermute | solution.py:158
  117.3 0.2 add_convert_fusion.2
  117.5 0.5 collective-permute-start.25
  118.0 8.4 %collective-permute-done.32 = bf16[72,2880]{1,0:T(8,128)(2,1)S(1)} collective-permute-done((bf16[72,2880]{1,0:T(8,128)(2,1)S(1)}, bf16[72,2880]{1,0:T(8,128)(2,1)S(1)}, u32[]{:S(2)}, u32[]{:S(2)}) %collective-permute-start.32) | collective-permute-done | bytes 414752 | tf_op jit(solution)/shard_map/ppermute | solution.py:158
  126.4 0.2 add_convert_fusion
  126.6 1.4 collective-permute-start.33
  127.9 1.0 shard_map.65
  128.9 15.6 %collective-permute-done.25.refs_2_ = bf16[72,2880]{1,0:T(8,128)(2,1)S(1)} collective-permute-done((bf16[72,2880]{1,0:T(8,128)(2,1)S(1)}, bf16[72,2880]{1,0:T(8,128)(2,1)S(1)}, u32[]{:S(2)}, u32[]{:S(2)}) %collective-permute-start.25) | collective-permute-done | bytes 414752 | tf_op jit(solution)/shard_map/ppermute | solution.py:158
  144.5 10.5 %collective-permute-done.33.refs_3_ = bf16[72,2880]{1,0:T(8,128)(2,1)S(1)} collective-permute-done((bf16[72,2880]{1,0:T(8,128)(2,1)S(1)}, bf16[72,2880]{1,0:T(8,128)(2,1)S(1)}, u32[]{:S(2)}, u32[]{:S(2)}) %collective-permute-start.33) | collective-permute-done | bytes 414752 | tf_op jit(solution)/shard_map/ppermute | solution.py:158
  155.0 1.0 shard_map.75
  156.0 1.6 collective-permute-start.34
  157.6 1.3 collective-permute-done.34
  158.9 0.9 add_convert_fusion.8
  (43 shorter events, 0.9 us)
Async XLA Ops:
  0.0 2.2 %collective-permute-start = (bf16[64,2880]{1,0:T(8,128)(2,1)}, bf16[64,2880]{1,0:T(8,128)(2,1)S(1)}, u32[]{:S(2)}, u32[]{:S(2)}) collective-permute-start(bf16[64,2880]{1,0:T(8,128)(2,1)} %own.1), channel_id=1, source_target_pairs={{0,1},{1,0},{2,3},{3,2},{4,5},{5,4},{6,7},{7,6},{8,9},{9,8},{10,11... | collective-permute-start | bytes 1105928 | tf_op jit(solution)/shard_map/ppermute | solution.py:158
  0.7 1.5 collective-permute-start.1
  2.2 1.0 copy-start.2
  3.2 0.7 copy-start.5
  5.4 3.4 %collective-permute-start.2 = (bf16[72,2880]{1,0:T(8,128)(2,1)S(1)}, bf16[72,2880]{1,0:T(8,128)(2,1)S(1)}, u32[]{:S(2)}, u32[]{:S(2)}) collective-permute-start(bf16[72,2880]{1,0:T(8,128)(2,1)S(1)} %get-tuple-element.33), channel_id=1, source_target_pairs={{0,0},{1,4},{2,2},{3,6},{4,1},{5,5},{6,3},{7,7},{8,8},{9,12},{10,1... | collective-permute-start | bytes 1244168 | tf_op jit(solution)/shard_map/ppermute | solution.py:158
  6.1 14.6 %collective-permute-start.10 = (bf16[72,2880]{1,0:T(8,128)(2,1)S(1)}, bf16[72,2880]{1,0:T(8,128)(2,1)S(1)}, u32[]{:S(2)}, u32[]{:S(2)}) collective-permute-start(bf16[72,2880]{1,0:T(8,128)(2,1)S(1)} %get-tuple-element.38), channel_id=1, source_target_pairs={{0,8},{1,12},{2,10},{3,14},{4,9},{5,13},{6,11},{7,15},{8,0},{9,4},... | collective-permute-start | bytes 1244168 | tf_op jit(solution)/shard_map/ppermute | solution.py:158
  6.3 18.5 %collective-permute-start.18 = (bf16[72,2880]{1,0:T(8,128)(2,1)S(1)}, bf16[72,2880]{1,0:T(8,128)(2,1)S(1)}, u32[]{:S(2)}, u32[]{:S(2)}) collective-permute-start(bf16[72,2880]{1,0:T(8,128)(2,1)S(1)} %get-tuple-element.43), channel_id=1, source_target_pairs={{0,16},{1,20},{2,18},{3,22},{4,17},{5,21},{6,19},{7,23},{8,24},{9,... | collective-permute-start | bytes 1244168 | tf_op jit(solution)/shard_map/ppermute | solution.py:158
  8.6 34.6 %collective-permute-start.26 = (bf16[72,2880]{1,0:T(8,128)(2,1)S(1)}, bf16[72,2880]{1,0:T(8,128)(2,1)S(1)}, u32[]{:S(2)}, u32[]{:S(2)}) collective-permute-start(bf16[72,2880]{1,0:T(8,128)(2,1)S(1)} %get-tuple-element.48), channel_id=1, source_target_pairs={{0,24},{1,28},{2,26},{3,30},{4,25},{5,29},{6,27},{7,31},{8,16},{9,... | collective-permute-start | bytes 1244168 | tf_op jit(solution)/shard_map/ppermute | solution.py:158
  8.8 35.7 %collective-permute-start.5 = (bf16[72,2880]{1,0:T(8,128)(2,1)S(1)}, bf16[72,2880]{1,0:T(8,128)(2,1)S(1)}, u32[]{:S(2)}, u32[]{:S(2)}) collective-permute-start(bf16[72,2880]{1,0:T(8,128)(2,1)S(1)} %collective-permute-done.2.mine_in), channel_id=1, source_target_pairs={{0,2},{1,3},{2,0},{3,1},{4,6},{5,7},{6,4},{7,5},{8,10},{9,11},{10,... | collective-permute-start | bytes 1244168 | tf_op jit(solution)/shard_map/ppermute | solution.py:158
  10.0 34.7 %collective-permute-start.3 = (bf16[72,2880]{1,0:T(8,128)(2,1)S(1)}, bf16[72,2880]{1,0:T(8,128)(2,1)S(1)}, u32[]{:S(2)}, u32[]{:S(2)}) collective-permute-start(bf16[72,2880]{1,0:T(8,128)(2,1)S(1)} %collective-permute-done.2.mine_in), channel_id=1, source_target_pairs={{0,1},{1,0},{2,3},{3,2},{4,5},{5,4},{6,7},{7,6},{8,9},{9,8},{10,11... | collective-permute-start | bytes 1244168 | tf_op jit(solution)/shard_map/ppermute | solution.py:158
  20.7 29.2 %collective-permute-start.13 = (bf16[72,2880]{1,0:T(8,128)(2,1)S(1)}, bf16[72,2880]{1,0:T(8,128)(2,1)S(1)}, u32[]{:S(2)}, u32[]{:S(2)}) collective-permute-start(bf16[72,2880]{1,0:T(8,128)(2,1)S(1)} %collective-permute-done.10.mine_in), channel_id=1, source_target_pairs={{0,2},{1,3},{2,0},{3,1},{4,6},{5,7},{6,4},{7,5},{8,10},{9,11},{10,... | collective-permute-start | bytes 1244168 | tf_op jit(solution)/shard_map/ppermute | solution.py:158
  24.8 25.1 %collective-permute-start.11 = (bf16[72,2880]{1,0:T(8,128)(2,1)S(1)}, bf16[72,2880]{1,0:T(8,128)(2,1)S(1)}, u32[]{:S(2)}, u32[]{:S(2)}) collective-permute-start(bf16[72,2880]{1,0:T(8,128)(2,1)S(1)} %collective-permute-done.10.mine_in), channel_id=1, source_target_pairs={{0,1},{1,0},{2,3},{3,2},{4,5},{5,4},{6,7},{7,6},{8,9},{9,8},{10,11... | collective-permute-start | bytes 1244168 | tf_op jit(solution)/shard_map/ppermute | solution.py:158
  43.2 7.2 %collective-permute-start.21 = (bf16[72,2880]{1,0:T(8,128)(2,1)S(1)}, bf16[72,2880]{1,0:T(8,128)(2,1)S(1)}, u32[]{:S(2)}, u32[]{:S(2)}) collective-permute-start(bf16[72,2880]{1,0:T(8,128)(2,1)S(1)} %collective-permute-done.18.mine_in), channel_id=1, source_target_pairs={{0,2},{1,3},{2,0},{3,1},{4,6},{5,7},{6,4},{7,5},{8,10},{9,11},{10,... | collective-permute-start | bytes 1244168 | tf_op jit(solution)/shard_map/ppermute | solution.py:158
  44.5 19.0 %collective-permute-start.29 = (bf16[72,2880]{1,0:T(8,128)(2,1)S(1)}, bf16[72,2880]{1,0:T(8,128)(2,1)S(1)}, u32[]{:S(2)}, u32[]{:S(2)}) collective-permute-start(bf16[72,2880]{1,0:T(8,128)(2,1)S(1)} %collective-permute-done.26.mine_in), channel_id=1, source_target_pairs={{0,2},{1,3},{2,0},{3,1},{4,6},{5,7},{6,4},{7,5},{8,10},{9,11},{10,... | collective-permute-start | bytes 1244168 | tf_op jit(solution)/shard_map/ppermute | solution.py:158
  44.7 19.8 %collective-permute-start.6 = (bf16[72,2880]{1,0:T(8,128)(2,1)S(1)}, bf16[72,2880]{1,0:T(8,128)(2,1)S(1)}, u32[]{:S(2)}, u32[]{:S(2)}) collective-permute-start(bf16[72,2880]{1,0:T(8,128)(2,1)S(1)} %collective-permute-done.5.mine_in), channel_id=1, source_target_pairs={{0,1},{1,0},{2,3},{3,2},{4,5},{5,4},{6,7},{7,6},{8,9},{9,8},{10,11... | collective-permute-start | bytes 1244168 | tf_op jit(solution)/shard_map/ppermute | solution.py:158
  49.9 16.6 %collective-permute-start.19 = (bf16[72,2880]{1,0:T(8,128)(2,1)S(1)}, bf16[72,2880]{1,0:T(8,128)(2,1)S(1)}, u32[]{:S(2)}, u32[]{:S(2)}) collective-permute-start(bf16[72,2880]{1,0:T(8,128)(2,1)S(1)} %collective-permute-done.18.mine_in), channel_id=1, source_target_pairs={{0,1},{1,0},{2,3},{3,2},{4,5},{5,4},{6,7},{7,6},{8,9},{9,8},{10,11... | collective-permute-start | bytes 1244168 | tf_op jit(solution)/shard_map/ppermute | solution.py:158
  50.0 23.1 %collective-permute-start.27 = (bf16[72,2880]{1,0:T(8,128)(2,1)S(1)}, bf16[72,2880]{1,0:T(8,128)(2,1)S(1)}, u32[]{:S(2)}, u32[]{:S(2)}) collective-permute-start(bf16[72,2880]{1,0:T(8,128)(2,1)S(1)} %collective-permute-done.26.mine_in), channel_id=1, source_target_pairs={{0,1},{1,0},{2,3},{3,2},{4,5},{5,4},{6,7},{7,6},{8,9},{9,8},{10,11... | collective-permute-start | bytes 1244168 | tf_op jit(solution)/shard_map/ppermute | solution.py:158
  50.4 24.8 %collective-permute-start.14 = (bf16[72,2880]{1,0:T(8,128)(2,1)S(1)}, bf16[72,2880]{1,0:T(8,128)(2,1)S(1)}, u32[]{:S(2)}, u32[]{:S(2)}) collective-permute-start(bf16[72,2880]{1,0:T(8,128)(2,1)S(1)} %collective-permute-done.13.mine_in), channel_id=1, source_target_pairs={{0,1},{1,0},{2,3},{3,2},{4,5},{5,4},{6,7},{7,6},{8,9},{9,8},{10,11... | collective-permute-start | bytes 1244168 | tf_op jit(solution)/shard_map/ppermute | solution.py:158
  60.0 2.2 %copy-start.1 = (bf16[1,2880,720]{1,2,0:T(8,128)(2,1)S(1)}, bf16[1,2880,720]{1,2,0:T(8,128)(2,1)}, u32[]{:S(2)}) copy-start(bf16[1,2880,720]{1,2,0:T(8,128)(2,1)} %param.10) | copy-start | bytes 12441604
  62.2 2.4 %copy-start = (bf16[1,360,2880]{2,1,0:T(8,128)(2,1)S(1)}, bf16[1,360,2880]{2,1,0:T(8,128)(2,1)}, u32[]{:S(2)}) copy-start(bf16[1,360,2880]{2,1,0:T(8,128)(2,1)} %param.11) | copy-start | bytes 6220804
  63.4 14.3 %collective-permute-start.22 = (bf16[72,2880]{1,0:T(8,128)(2,1)S(1)}, bf16[72,2880]{1,0:T(8,128)(2,1)S(1)}, u32[]{:S(2)}, u32[]{:S(2)}) collective-permute-start(bf16[72,2880]{1,0:T(8,128)(2,1)S(1)} %collective-permute-done.21.mine_in), channel_id=1, source_target_pairs={{0,1},{1,0},{2,3},{3,2},{4,5},{5,4},{6,7},{7,6},{8,9},{9,8},{10,11... | collective-permute-start | bytes 1244168 | tf_op jit(solution)/shard_map/ppermute | solution.py:158
  64.5 15.5 %collective-permute-start.30 = (bf16[72,2880]{1,0:T(8,128)(2,1)S(1)}, bf16[72,2880]{1,0:T(8,128)(2,1)S(1)}, u32[]{:S(2)}, u32[]{:S(2)}) collective-permute-start(bf16[72,2880]{1,0:T(8,128)(2,1)S(1)} %collective-permute-done.29.mine_in), channel_id=1, source_target_pairs={{0,1},{1,0},{2,3},{3,2},{4,5},{5,4},{6,7},{7,6},{8,9},{9,8},{10,11... | collective-permute-start | bytes 1244168 | tf_op jit(solution)/shard_map/ppermute | solution.py:158
  66.5 16.1 %collective-permute-start.7 = (bf16[72,2880]{1,0:T(8,128)(2,1)S(1)}, bf16[72,2880]{1,0:T(8,128)(2,1)S(1)}, u32[]{:S(2)}, u32[]{:S(2)}) collective-permute-start(bf16[72,2880]{1,0:T(8,128)(2,1)S(1)} %get-tuple-element.37), channel_id=1, source_target_pairs={{0,1},{1,0},{2,3},{3,2},{4,5},{5,4},{6,7},{7,6},{8,9},{9,8},{10,11... | collective-permute-start | bytes 1244168 | tf_op jit(solution)/shard_map/ppermute | solution.py:158
  73.1 16.2 %collective-permute-start.4 = (bf16[72,2880]{1,0:T(8,128)(2,1)S(1)}, bf16[72,2880]{1,0:T(8,128)(2,1)S(1)}, u32[]{:S(2)}, u32[]{:S(2)}) collective-permute-start(bf16[72,2880]{1,0:T(8,128)(2,1)S(1)} %get-tuple-element.35), channel_id=1, source_target_pairs={{0,1},{1,0},{2,3},{3,2},{4,5},{5,4},{6,7},{7,6},{8,9},{9,8},{10,11... | collective-permute-start | bytes 1244168 | tf_op jit(solution)/shard_map/ppermute | solution.py:158
  75.2 25.4 %collective-permute-start.12 = (bf16[72,2880]{1,0:T(8,128)(2,1)S(1)}, bf16[72,2880]{1,0:T(8,128)(2,1)S(1)}, u32[]{:S(2)}, u32[]{:S(2)}) collective-permute-start(bf16[72,2880]{1,0:T(8,128)(2,1)S(1)} %get-tuple-element.40), channel_id=1, source_target_pairs={{0,1},{1,0},{2,3},{3,2},{4,5},{5,4},{6,7},{7,6},{8,9},{9,8},{10,11... | collective-permute-start | bytes 1244168 | tf_op jit(solution)/shard_map/ppermute | solution.py:158
  77.7 31.4 %collective-permute-start.20 = (bf16[72,2880]{1,0:T(8,128)(2,1)S(1)}, bf16[72,2880]{1,0:T(8,128)(2,1)S(1)}, u32[]{:S(2)}, u32[]{:S(2)}) collective-permute-start(bf16[72,2880]{1,0:T(8,128)(2,1)S(1)} %get-tuple-element.45), channel_id=1, source_target_pairs={{0,1},{1,0},{2,3},{3,2},{4,5},{5,4},{6,7},{7,6},{8,9},{9,8},{10,11... | collective-permute-start | bytes 1244168 | tf_op jit(solution)/shard_map/ppermute | solution.py:158
  80.0 38.0 %collective-permute-start.28 = (bf16[72,2880]{1,0:T(8,128)(2,1)S(1)}, bf16[72,2880]{1,0:T(8,128)(2,1)S(1)}, u32[]{:S(2)}, u32[]{:S(2)}) collective-permute-start(bf16[72,2880]{1,0:T(8,128)(2,1)S(1)} %get-tuple-element.50), channel_id=1, source_target_pairs={{0,1},{1,0},{2,3},{3,2},{4,5},{5,4},{6,7},{7,6},{8,9},{9,8},{10,11... | collective-permute-start | bytes 1244168 | tf_op jit(solution)/shard_map/ppermute | solution.py:158
  82.6 1.8 %collective-permute-start.15 = (bf16[72,2880]{1,0:T(8,128)(2,1)S(1)}, bf16[72,2880]{1,0:T(8,128)(2,1)S(1)}, u32[]{:S(2)}, u32[]{:S(2)}) collective-permute-start(bf16[72,2880]{1,0:T(8,128)(2,1)S(1)} %get-tuple-element.42), channel_id=1, source_target_pairs={{0,1},{1,0},{2,3},{3,2},{4,5},{5,4},{6,7},{7,6},{8,9},{9,8},{10,11... | collective-permute-start | bytes 1244168 | tf_op jit(solution)/shard_map/ppermute | solution.py:158
  84.4 1.8 %collective-permute-start.23 = (bf16[72,2880]{1,0:T(8,128)(2,1)S(1)}, bf16[72,2880]{1,0:T(8,128)(2,1)S(1)}, u32[]{:S(2)}, u32[]{:S(2)}) collective-permute-start(bf16[72,2880]{1,0:T(8,128)(2,1)S(1)} %get-tuple-element.47), channel_id=1, source_target_pairs={{0,1},{1,0},{2,3},{3,2},{4,5},{5,4},{6,7},{7,6},{8,9},{9,8},{10,11... | collective-permute-start | bytes 1244168 | tf_op jit(solution)/shard_map/ppermute | solution.py:158
  86.2 1.8 %collective-permute-start.31 = (bf16[72,2880]{1,0:T(8,128)(2,1)S(1)}, bf16[72,2880]{1,0:T(8,128)(2,1)S(1)}, u32[]{:S(2)}, u32[]{:S(2)}) collective-permute-start(bf16[72,2880]{1,0:T(8,128)(2,1)S(1)} %get-tuple-element.52), channel_id=1, source_target_pairs={{0,1},{1,0},{2,3},{3,2},{4,5},{5,4},{6,7},{7,6},{8,9},{9,8},{10,11... | collective-permute-start | bytes 1244168 | tf_op jit(solution)/shard_map/ppermute | solution.py:158
  86.4 41.5 %copy-start.4 = (bf16[2880,8]{0,1:T(8,128)(2,1)S(1)}, bf16[2880,8]{0,1:T(8,128)(2,1)}, u32[]{:S(2)}) copy-start(bf16[2880,8]{0,1:T(8,128)(2,1)} %param.9) | copy-start | bytes 138244
  86.4 41.5 %copy-start.6 = (s32[64,4]{0,1:T(4,128)S(1)}, s32[64,4]{0,1:T(4,128)}, u32[]{:S(2)}) copy-start(s32[64,4]{0,1:T(4,128)} %param.7) | copy-start | bytes 3076
  88.0 11.2 %collective-permute-start.8 = (bf16[72,2880]{1,0:T(8,128)(2,1)S(1)}, bf16[72,2880]{1,0:T(8,128)(2,1)S(1)}, u32[]{:S(2)}, u32[]{:S(2)}) collective-permute-start(bf16[72,2880]{1,0:T(8,128)(2,1)S(1)} %add_convert_fusion.7), channel_id=1, source_target_pairs={{0,2},{1,3},{2,0},{3,1},{4,6},{5,7},{6,4},{7,5},{8,10},{9,11},{10,... | collective-permute-start | bytes 1244168 | tf_op jit(solution)/shard_map/ppermute | solution.py:158
  89.3 19.0 %collective-permute-start.16 = (bf16[72,2880]{1,0:T(8,128)(2,1)S(1)}, bf16[72,2880]{1,0:T(8,128)(2,1)S(1)}, u32[]{:S(2)}, u32[]{:S(2)}) collective-permute-start(bf16[72,2880]{1,0:T(8,128)(2,1)S(1)} %add_convert_fusion.5), channel_id=1, source_target_pairs={{0,2},{1,3},{2,0},{3,1},{4,6},{5,7},{6,4},{7,5},{8,10},{9,11},{10,... | collective-permute-start | bytes 1244168 | tf_op jit(solution)/shard_map/ppermute | solution.py:158
  99.1 18.2 %collective-permute-start.24 = (bf16[72,2880]{1,0:T(8,128)(2,1)S(1)}, bf16[72,2880]{1,0:T(8,128)(2,1)S(1)}, u32[]{:S(2)}, u32[]{:S(2)}) collective-permute-start(bf16[72,2880]{1,0:T(8,128)(2,1)S(1)} %add_convert_fusion.3), channel_id=1, source_target_pairs={{0,2},{1,3},{2,0},{3,1},{4,6},{5,7},{6,4},{7,5},{8,10},{9,11},{10,... | collective-permute-start | bytes 1244168 | tf_op jit(solution)/shard_map/ppermute | solution.py:158
  100.5 58.4 %copy-start.3 = (bf16[64,2880]{1,0:T(8,128)(2,1)S(1)}, bf16[64,2880]{1,0:T(8,128)(2,1)}, u32[]{:S(2)}) copy-start(bf16[64,2880]{1,0:T(8,128)(2,1)} %own.1) | copy-start | bytes 1105924
  100.5 25.9 %collective-permute-start.32 = (bf16[72,2880]{1,0:T(8,128)(2,1)S(1)}, bf16[72,2880]{1,0:T(8,128)(2,1)S(1)}, u32[]{:S(2)}, u32[]{:S(2)}) collective-permute-start(bf16[72,2880]{1,0:T(8,128)(2,1)S(1)} %add_convert_fusion.1), channel_id=1, source_target_pairs={{0,2},{1,3},{2,0},{3,1},{4,6},{5,7},{6,4},{7,5},{8,10},{9,11},{10,... | collective-permute-start | bytes 1244168 | tf_op jit(solution)/shard_map/ppermute | solution.py:158
  108.2 20.7 %collective-permute-start.9 = (bf16[72,2880]{1,0:T(8,128)(2,1)S(1)}, bf16[72,2880]{1,0:T(8,128)(2,1)S(1)}, u32[]{:S(2)}, u32[]{:S(2)}) collective-permute-start(bf16[72,2880]{1,0:T(8,128)(2,1)S(1)} %add_convert_fusion.6), channel_id=1, source_target_pairs={{0,0},{1,4},{2,2},{3,6},{4,1},{5,5},{6,3},{7,7},{8,8},{9,12},{10,1... | collective-permute-start | bytes 1244168 | tf_op jit(solution)/shard_map/ppermute | solution.py:158
  109.1 19.8 %collective-permute-start.17 = (bf16[72,2880]{1,0:T(8,128)(2,1)S(1)}, bf16[72,2880]{1,0:T(8,128)(2,1)S(1)}, u32[]{:S(2)}, u32[]{:S(2)}) collective-permute-start(bf16[72,2880]{1,0:T(8,128)(2,1)S(1)} %add_convert_fusion.4), channel_id=1, source_target_pairs={{0,8},{1,12},{2,10},{3,14},{4,9},{5,13},{6,11},{7,15},{8,0},{9,4},... | collective-permute-start | bytes 1244168 | tf_op jit(solution)/shard_map/ppermute | solution.py:158
  117.5 27.0 %collective-permute-start.25 = (bf16[72,2880]{1,0:T(8,128)(2,1)S(1)}, bf16[72,2880]{1,0:T(8,128)(2,1)S(1)}, u32[]{:S(2)}, u32[]{:S(2)}) collective-permute-start(bf16[72,2880]{1,0:T(8,128)(2,1)S(1)} %add_convert_fusion.2), channel_id=1, source_target_pairs={{0,16},{1,20},{2,18},{3,22},{4,17},{5,21},{6,19},{7,23},{8,24},{9,... | collective-permute-start | bytes 1244168 | tf_op jit(solution)/shard_map/ppermute | solution.py:158
  126.6 28.4 %collective-permute-start.33 = (bf16[72,2880]{1,0:T(8,128)(2,1)S(1)}, bf16[72,2880]{1,0:T(8,128)(2,1)S(1)}, u32[]{:S(2)}, u32[]{:S(2)}) collective-permute-start(bf16[72,2880]{1,0:T(8,128)(2,1)S(1)} %add_convert_fusion), channel_id=1, source_target_pairs={{0,24},{1,28},{2,26},{3,30},{4,25},{5,29},{6,27},{7,31},{8,16},{9,... | collective-permute-start | bytes 1244168 | tf_op jit(solution)/shard_map/ppermute | solution.py:158
  156.0 2.9 %collective-permute-start.34 = (bf16[64,2880]{1,0:T(8,128)(2,1)S(1)}, bf16[64,2880]{1,0:T(8,128)(2,1)S(1)}, u32[]{:S(2)}, u32[]{:S(2)}) collective-permute-start(bf16[64,2880]{1,0:T(8,128)(2,1)S(1)} %get-tuple-element.54), channel_id=1, source_target_pairs={{0,1},{1,0},{2,3},{3,2},{4,5},{5,4},{6,7},{7,6},{8,9},{9,8},{10,11... | collective-permute-start | bytes 1105928 | tf_op jit(solution)/shard_map/ppermute | solution.py:158

commit v6 on v5

--- a/solution.py
+++ b/solution.py
@@ -11,6 +11,10 @@
 CORES = 2
 SHARDS = 4
 VMEM_BYTES = 16 * 1024 * 1024
+
+
+def turn(m):
+    return m % CORES
 
 
 def dot32(a, b, dims=((1,), (0,))):
@@ -134,7 +138,7 @@
     core = index % CORES
     expert_high = index // (CORES * shard_count)
     ids = jnp.stack(
-        [(expert_high ^ m) * CORES + core for m in range(chunks)] + [core]
+        [(expert_high ^ m) * CORES + (core ^ turn(m)) for m in range(chunks)] + [core]
     ).astype(jnp.int32)
 
     def split(i):
@@ -149,7 +153,7 @@
         pairs = []
         for i in range(devices):
             high, e_low, x, c = split(i)
-            pairs.append((i, join(high ^ m, c, x, e_low)))
+            pairs.append((i, join(high ^ m, c ^ turn(m), x, e_low ^ turn(m))))
         far.append(pairs)
     to_core = [(i, i ^ 1) for i in range(devices)]
     to_x = [(i, i ^ CORES) for i in range(devices)]

time: 162 us -> 164 us (1.012); the launches traced: 160 us -> 164 us
  waiting for transfers between devices: 73.3 us -> 89.1 us
  starting transfers between devices: 58.9 us -> 46.8 us
    ppermute x35, waiting for transfers between devices: 73.3 us -> 89.1 us  [move(): return lax.ppermute(value, 'ep', perm)]
    ppermute x35, starting transfers between devices: 58.9 us -> 46.8 us  [move(): return lax.ppermute(value, 'ep', perm)]
  transfers between devices with their start and end apart: 35 -> 35, of which waited for: 14 -> 15; matrix products, arithmetic and copies ran while one was open for 1% -> 1% of each run, Pallas kernels for 11% -> 11%
where the time goes in v6:
time: 164 us
  waiting for transfers between devices  89.1 us (54%)
  starting transfers between devices  46.8 us (29%)
  Pallas kernels  20.7 us (13%)
  local copies, waits for them, and re-layouts  4.68 us (3%)
  other arithmetic  1.9 us (1%)
    ppermute x35, waiting for transfers between devices, move(): return lax.ppermute(value, 'ep', perm)  89.1 us
    ppermute x35, starting transfers between devices, move(): return lax.ppermute(value, 'ep', perm)  46.8 us
    pallas_call x8, Pallas kernels, expert(): vmem_call(functools.partial(expert_kernel, ff=ff), [block, block], 0, 4)  16.1 us
    unnamed x14, local copies, waits for them, and re-layouts  3.89 us
  transfers between devices with their start and end apart: 35, of which 15 were waited for; matrix products, arithmetic and copies ran while one was open for 1% of the time, Pallas kernels for 11%

profile of v6, /device:TPU:13, one launch (start us, length us, event | category | flops | bytes accessed | tf_op | source)
XLA Modules:
  0.0 163.6 jit_solution(14713069866624582602)
XLA Ops:
  0.0 0.7 collective-permute-start
  0.7 0.7 reshape.3.gain
  1.5 0.8 collective-permute-done.1.routes_other
  2.2 1.0 copy-done.2
  3.2 0.7 copy-done.5
  3.9 1.5 shard_map.64
  5.4 0.7 collective-permute-start.2
  6.1 2.7 %collective-permute-start.18 = (bf16[72,2880]{1,0:T(8,128)(2,1)S(1)}, bf16[72,2880]{1,0:T(8,128)(2,1)S(1)}, u32[]{:S(2)}, u32[]{:S(2)}) collective-permute-start(bf16[72,2880]{1,0:T(8,128)(2,1)S(1)} %get-tuple-element.43), channel_id=1, source_target_pairs={{0,16},{1,20},{2,18},{3,22},{4,17},{5,21},{6,19},{7,23},{8,24},{9,... | collective-permute-start | bytes 1244168 | tf_op jit(solution)/shard_map/ppermute | solution.py:162
  8.8 1.4 collective-permute-start.26
  10.2 1.2 collective-permute-start.5
  11.4 9.7 %collective-permute-start.3 = (bf16[72,2880]{1,0:T(8,128)(2,1)S(1)}, bf16[72,2880]{1,0:T(8,128)(2,1)S(1)}, u32[]{:S(2)}, u32[]{:S(2)}) collective-permute-start(bf16[72,2880]{1,0:T(8,128)(2,1)S(1)} %collective-permute-done.2.mine_in), channel_id=1, source_target_pairs={{0,1},{1,0},{2,3},{3,2},{4,5},{5,4},{6,7},{7,6},{8,9},{9,8},{10,11... | collective-permute-start | bytes 1244168 | tf_op jit(solution)/shard_map/ppermute | solution.py:162
  21.2 1.5 collective-permute-start.13
  22.7 3.4 %collective-permute-done.18.mine_in = bf16[72,2880]{1,0:T(8,128)(2,1)S(1)} collective-permute-done((bf16[72,2880]{1,0:T(8,128)(2,1)S(1)}, bf16[72,2880]{1,0:T(8,128)(2,1)S(1)}, u32[]{:S(2)}, u32[]{:S(2)}) %collective-permute-start.18) | collective-permute-done | bytes 414752 | tf_op jit(solution)/shard_map/ppermute | solution.py:162
  26.2 13.8 %collective-permute-start.11 = (bf16[72,2880]{1,0:T(8,128)(2,1)S(1)}, bf16[72,2880]{1,0:T(8,128)(2,1)S(1)}, u32[]{:S(2)}, u32[]{:S(2)}) collective-permute-start(bf16[72,2880]{1,0:T(8,128)(2,1)S(1)} %collective-permute-done.10.mine_in), channel_id=1, source_target_pairs={{0,1},{1,0},{2,3},{3,2},{4,5},{5,4},{6,7},{7,6},{8,9},{9,8},{10,11... | collective-permute-start | bytes 1244168 | tf_op jit(solution)/shard_map/ppermute | solution.py:162
  40.0 6.8 %collective-permute-done.26.mine_in = bf16[72,2880]{1,0:T(8,128)(2,1)S(1)} collective-permute-done((bf16[72,2880]{1,0:T(8,128)(2,1)S(1)}, bf16[72,2880]{1,0:T(8,128)(2,1)S(1)}, u32[]{:S(2)}, u32[]{:S(2)}) %collective-permute-start.26) | collective-permute-done | bytes 414752 | tf_op jit(solution)/shard_map/ppermute | solution.py:162
  46.8 1.2 collective-permute-start.21
  48.0 0.3 collective-permute-start.29
  48.2 0.8 collective-permute-start.6
  49.1 0.4 collective-permute-start.27
  49.6 8.3 %collective-permute-done.21.mine_in = bf16[72,2880]{1,0:T(8,128)(2,1)S(1)} collective-permute-done((bf16[72,2880]{1,0:T(8,128)(2,1)S(1)}, bf16[72,2880]{1,0:T(8,128)(2,1)S(1)}, u32[]{:S(2)}, u32[]{:S(2)}) %collective-permute-start.21) | collective-permute-done | bytes 414752 | tf_op jit(solution)/shard_map/ppermute | solution.py:162
  57.8 1.8 %collective-permute-start.14 = (bf16[72,2880]{1,0:T(8,128)(2,1)S(1)}, bf16[72,2880]{1,0:T(8,128)(2,1)S(1)}, u32[]{:S(2)}, u32[]{:S(2)}) collective-permute-start(bf16[72,2880]{1,0:T(8,128)(2,1)S(1)} %collective-permute-done.13.mine_in), channel_id=1, source_target_pairs={{0,1},{1,0},{2,3},{3,2},{4,5},{5,4},{6,7},{7,6},{8,9},{9,8},{10,11... | collective-permute-start | bytes 1244168 | tf_op jit(solution)/shard_map/ppermute | solution.py:162
  59.6 2.2 %copy-done.1 = bf16[1,2880,720]{1,2,0:T(8,128)(2,1)S(1)} copy-done((bf16[1,2880,720]{1,2,0:T(8,128)(2,1)S(1)}, bf16[1,2880,720]{1,2,0:T(8,128)(2,1)}, u32[]{:S(2)}) %copy-start.1) | copy-done | bytes 4147224
  61.9 1.2 shard_map.66.gate_up
  63.1 3.8 %collective-permute-done.29.mine_in = bf16[72,2880]{1,0:T(8,128)(2,1)S(1)} collective-permute-done((bf16[72,2880]{1,0:T(8,128)(2,1)S(1)}, bf16[72,2880]{1,0:T(8,128)(2,1)S(1)}, u32[]{:S(2)}, u32[]{:S(2)}) %collective-permute-start.29) | collective-permute-done | bytes 414752 | tf_op jit(solution)/shard_map/ppermute | solution.py:162
  66.9 1.1 collective-permute-start.22
  68.0 2.0 %shard_map.68 = (bf16[72,2880]{1,0:T(8,128)(2,1)S(1)}, bf16[72,2880]{1,0:T(8,128)(2,1)S(1)}) custom-call(bf16[72,2880]{1,0:T(8,128)(2,1)S(1)} %collective-permute-done.5.mine_in, bf16[72,2880]{1,0:T(8,128)(2,1)S(1)} %collective-permute-done.6.other_in, bf16[2880,720]{1,0:T(8,128)(2,1)S(1)} %shard_map.66.gate_up, bf16[360,2880]{1,0:T(8,128)(2,1)S(1)} %bitcast.11), custom_call_target="tpu_custom_call" | custom-call | tf_op jit(solution)/shard_map/pallas_call | solution.py:190
  70.0 0.6 collective-permute-start.7
  70.6 2.0 %shard_map.67 = (bf16[72,2880]{1,0:T(8,128)(2,1)S(1)}, bf16[72,2880]{1,0:T(8,128)(2,1)S(1)}) custom-call(bf16[72,2880]{1,0:T(8,128)(2,1)S(1)} %collective-permute-done.2.mine_in, bf16[72,2880]{1,0:T(8,128)(2,1)S(1)} %collective-permute-done.3.other_in, bf16[2880,720]{1,0:T(8,128)(2,1)S(1)} %shard_map.66.gate_up, bf16[360,2880]{1,0:T(8,128)(2,1)S(1)} %bitcast.12), custom_call_target="tpu_custom_call" | custom-call | tf_op jit(solution)/shard_map/pallas_call | solution.py:190
  72.6 2.0 %shard_map.69 = (bf16[72,2880]{1,0:T(8,128)(2,1)S(1)}, bf16[72,2880]{1,0:T(8,128)(2,1)S(1)}) custom-call(bf16[72,2880]{1,0:T(8,128)(2,1)S(1)} %collective-permute-done.10.mine_in, bf16[72,2880]{1,0:T(8,128)(2,1)S(1)} %collective-permute-done.11.other_in, bf16[2880,720]{1,0:T(8,128)(2,1)S(1)} %shard_map.66.gate_up, bf16[360,2880]{1,0:T(8,128)(2,1)S(1)} %bitcast.13), custom_call_target="tpu_custom_call" | custom-call | tf_op jit(solution)/shard_map/pallas_call | solution.py:190
  74.6 2.0 %shard_map.71 = (bf16[72,2880]{1,0:T(8,128)(2,1)S(1)}, bf16[72,2880]{1,0:T(8,128)(2,1)S(1)}) custom-call(bf16[72,2880]{1,0:T(8,128)(2,1)S(1)} %collective-permute-done.18.mine_in, bf16[72,2880]{1,0:T(8,128)(2,1)S(1)} %collective-permute-done.19.other_in, bf16[2880,720]{1,0:T(8,128)(2,1)S(1)} %shard_map.66.gate_up, bf16[360,2880]{1,0:T(8,128)(2,1)S(1)} %bitcast.14), custom_call_target="tpu_custom_call" | custom-call | tf_op jit(solution)/shard_map/pallas_call | solution.py:190
  76.7 2.0 %shard_map.73 = (bf16[72,2880]{1,0:T(8,128)(2,1)S(1)}, bf16[72,2880]{1,0:T(8,128)(2,1)S(1)}) custom-call(bf16[72,2880]{1,0:T(8,128)(2,1)S(1)} %collective-permute-done.26.mine_in, bf16[72,2880]{1,0:T(8,128)(2,1)S(1)} %collective-permute-done.27.other_in, bf16[2880,720]{1,0:T(8,128)(2,1)S(1)} %shard_map.66.gate_up, bf16[360,2880]{1,0:T(8,128)(2,1)S(1)} %bitcast.15), custom_call_target="tpu_custom_call" | custom-call | tf_op jit(solution)/shard_map/pallas_call | solution.py:190
  78.7 0.6 collective-permute-start.12
  79.2 2.0 %shard_map.70 = (bf16[72,2880]{1,0:T(8,128)(2,1)S(1)}, bf16[72,2880]{1,0:T(8,128)(2,1)S(1)}) custom-call(bf16[72,2880]{1,0:T(8,128)(2,1)S(1)} %collective-permute-done.13.mine_in, bf16[72,2880]{1,0:T(8,128)(2,1)S(1)} %collective-permute-done.14.other_in, bf16[2880,720]{1,0:T(8,128)(2,1)S(1)} %shard_map.66.gate_up, bf16[360,2880]{1,0:T(8,128)(2,1)S(1)} %bitcast.16), custom_call_target="tpu_custom_call" | custom-call | tf_op jit(solution)/shard_map/pallas_call | solution.py:190
  81.3 2.2 %shard_map.72 = (bf16[72,2880]{1,0:T(8,128)(2,1)S(1)}, bf16[72,2880]{1,0:T(8,128)(2,1)S(1)}) custom-call(bf16[72,2880]{1,0:T(8,128)(2,1)S(1)} %collective-permute-done.21.mine_in, bf16[72,2880]{1,0:T(8,128)(2,1)S(1)} %collective-permute-done.22.other_in, bf16[2880,720]{1,0:T(8,128)(2,1)S(1)} %shard_map.66.gate_up, bf16[360,2880]{1,0:T(8,128)(2,1)S(1)} %bitcast.17), custom_call_target="tpu_custom_call" | custom-call | tf_op jit(solution)/shard_map/pallas_call | solution.py:190
  83.5 0.6 collective-permute-start.28
  84.1 2.0 %shard_map.74 = (bf16[72,2880]{1,0:T(8,128)(2,1)S(1)}, bf16[72,2880]{1,0:T(8,128)(2,1)S(1)}) custom-call(bf16[72,2880]{1,0:T(8,128)(2,1)S(1)} %collective-permute-done.29.mine_in, bf16[72,2880]{1,0:T(8,128)(2,1)S(1)} %collective-permute-done.30.other_in, bf16[2880,720]{1,0:T(8,128)(2,1)S(1)} %shard_map.66.gate_up, bf16[360,2880]{1,0:T(8,128)(2,1)S(1)} %bitcast.18), custom_call_target="tpu_custom_call" | custom-call | tf_op jit(solution)/shard_map/pallas_call | solution.py:190
  86.3 1.6 %collective-permute-done.15 = bf16[72,2880]{1,0:T(8,128)(2,1)S(1)} collective-permute-done((bf16[72,2880]{1,0:T(8,128)(2,1)S(1)}, bf16[72,2880]{1,0:T(8,128)(2,1)S(1)}, u32[]{:S(2)}, u32[]{:S(2)}) %collective-permute-start.15) | collective-permute-done | bytes 414752 | tf_op jit(solution)/shard_map/ppermute | solution.py:162
  87.9 0.1 collective-permute-start.23
  88.1 0.1 add_convert_fusion.5
  88.2 1.5 collective-permute-done.23
  89.7 0.1 collective-permute-start.31
  90.0 1.5 collective-permute-done.31
  91.5 1.2 collective-permute-start.8
  92.7 0.1 add_convert_fusion.1
  92.8 0.3 collective-permute-start.16
  93.1 9.5 %collective-permute-done.8 = bf16[72,2880]{1,0:T(8,128)(2,1)S(1)} collective-permute-done((bf16[72,2880]{1,0:T(8,128)(2,1)S(1)}, bf16[72,2880]{1,0:T(8,128)(2,1)S(1)}, u32[]{:S(2)}, u32[]{:S(2)}) %collective-permute-start.8) | collective-permute-done | bytes 414752 | tf_op jit(solution)/shard_map/ppermute | solution.py:162
  102.7 1.2 collective-permute-start.24
  103.9 0.2 add_convert_fusion.6
  104.0 0.3 collective-permute-start.32
  104.4 7.4 %collective-permute-done.16 = bf16[72,2880]{1,0:T(8,128)(2,1)S(1)} collective-permute-done((bf16[72,2880]{1,0:T(8,128)(2,1)S(1)}, bf16[72,2880]{1,0:T(8,128)(2,1)S(1)}, u32[]{:S(2)}, u32[]{:S(2)}) %collective-permute-start.16) | collective-permute-done | bytes 414752 | tf_op jit(solution)/shard_map/ppermute | solution.py:162
  111.7 0.7 collective-permute-start.9
  112.4 0.2 add_convert_fusion.4
  112.7 8.1 %collective-permute-done.24 = bf16[72,2880]{1,0:T(8,128)(2,1)S(1)} collective-permute-done((bf16[72,2880]{1,0:T(8,128)(2,1)S(1)}, bf16[72,2880]{1,0:T(8,128)(2,1)S(1)}, u32[]{:S(2)}, u32[]{:S(2)}) %collective-permute-start.24) | collective-permute-done | bytes 414752 | tf_op jit(solution)/shard_map/ppermute | solution.py:162
  120.8 0.2 add_convert_fusion.2
  121.1 8.8 %collective-permute-done.32 = bf16[72,2880]{1,0:T(8,128)(2,1)S(1)} collective-permute-done((bf16[72,2880]{1,0:T(8,128)(2,1)S(1)}, bf16[72,2880]{1,0:T(8,128)(2,1)S(1)}, u32[]{:S(2)}, u32[]{:S(2)}) %collective-permute-start.32) | collective-permute-done | bytes 414752 | tf_op jit(solution)/shard_map/ppermute | solution.py:162
  129.9 0.2 add_convert_fusion
  130.1 0.8 collective-permute-start.33
  130.9 1.0 shard_map.65
  131.9 15.3 %collective-permute-done.25.refs_2_ = bf16[72,2880]{1,0:T(8,128)(2,1)S(1)} collective-permute-done((bf16[72,2880]{1,0:T(8,128)(2,1)S(1)}, bf16[72,2880]{1,0:T(8,128)(2,1)S(1)}, u32[]{:S(2)}, u32[]{:S(2)}) %collective-permute-start.25) | collective-permute-done | bytes 414752 | tf_op jit(solution)/shard_map/ppermute | solution.py:162
  147.1 10.9 %collective-permute-done.33.refs_3_ = bf16[72,2880]{1,0:T(8,128)(2,1)S(1)} collective-permute-done((bf16[72,2880]{1,0:T(8,128)(2,1)S(1)}, bf16[72,2880]{1,0:T(8,128)(2,1)S(1)}, u32[]{:S(2)}, u32[]{:S(2)}) %collective-permute-start.33) | collective-permute-done | bytes 414752 | tf_op jit(solution)/shard_map/ppermute | solution.py:162
  158.0 1.0 shard_map.75
  159.0 2.4 %collective-permute-start.34 = (bf16[64,2880]{1,0:T(8,128)(2,1)S(1)}, bf16[64,2880]{1,0:T(8,128)(2,1)S(1)}, u32[]{:S(2)}, u32[]{:S(2)}) collective-permute-start(bf16[64,2880]{1,0:T(8,128)(2,1)S(1)} %get-tuple-element.54), channel_id=1, source_target_pairs={{0,1},{1,0},{2,3},{3,2},{4,5},{5,4},{6,7},{7,6},{8,9},{9,8},{10,11... | collective-permute-start | bytes 1105928 | tf_op jit(solution)/shard_map/ppermute | solution.py:162
  161.4 1.3 collective-permute-done.34
  162.7 0.9 add_convert_fusion.8
  (43 shorter events, 0.9 us)
Async XLA Ops:
  0.0 2.2 %collective-permute-start = (bf16[64,2880]{1,0:T(8,128)(2,1)}, bf16[64,2880]{1,0:T(8,128)(2,1)S(1)}, u32[]{:S(2)}, u32[]{:S(2)}) collective-permute-start(bf16[64,2880]{1,0:T(8,128)(2,1)} %own.1), channel_id=1, source_target_pairs={{0,1},{1,0},{2,3},{3,2},{4,5},{5,4},{6,7},{7,6},{8,9},{9,8},{10,11... | collective-permute-start | bytes 1105928 | tf_op jit(solution)/shard_map/ppermute | solution.py:162
  0.7 1.5 collective-permute-start.1
  2.2 1.0 copy-start.2
  3.2 0.7 copy-start.5
  5.4 4.9 %collective-permute-start.2 = (bf16[72,2880]{1,0:T(8,128)(2,1)S(1)}, bf16[72,2880]{1,0:T(8,128)(2,1)S(1)}, u32[]{:S(2)}, u32[]{:S(2)}) collective-permute-start(bf16[72,2880]{1,0:T(8,128)(2,1)S(1)} %get-tuple-element.33), channel_id=1, source_target_pairs={{0,0},{1,4},{2,2},{3,6},{4,1},{5,5},{6,3},{7,7},{8,8},{9,12},{10,1... | collective-permute-start | bytes 1244168 | tf_op jit(solution)/shard_map/ppermute | solution.py:162
  6.1 15.1 %collective-permute-start.10 = (bf16[72,2880]{1,0:T(8,128)(2,1)S(1)}, bf16[72,2880]{1,0:T(8,128)(2,1)S(1)}, u32[]{:S(2)}, u32[]{:S(2)}) collective-permute-start(bf16[72,2880]{1,0:T(8,128)(2,1)S(1)} %get-tuple-element.38), channel_id=1, source_target_pairs={{0,13},{1,9},{2,15},{3,11},{4,12},{5,8},{6,14},{7,10},{8,5},{9,1},... | collective-permute-start | bytes 1244168 | tf_op jit(solution)/shard_map/ppermute | solution.py:162
  6.1 20.0 %collective-permute-start.18 = (bf16[72,2880]{1,0:T(8,128)(2,1)S(1)}, bf16[72,2880]{1,0:T(8,128)(2,1)S(1)}, u32[]{:S(2)}, u32[]{:S(2)}) collective-permute-start(bf16[72,2880]{1,0:T(8,128)(2,1)S(1)} %get-tuple-element.43), channel_id=1, source_target_pairs={{0,16},{1,20},{2,18},{3,22},{4,17},{5,21},{6,19},{7,23},{8,24},{9,... | collective-permute-start | bytes 1244168 | tf_op jit(solution)/shard_map/ppermute | solution.py:162
  8.8 37.9 %collective-permute-start.26 = (bf16[72,2880]{1,0:T(8,128)(2,1)S(1)}, bf16[72,2880]{1,0:T(8,128)(2,1)S(1)}, u32[]{:S(2)}, u32[]{:S(2)}) collective-permute-start(bf16[72,2880]{1,0:T(8,128)(2,1)S(1)} %get-tuple-element.48), channel_id=1, source_target_pairs={{0,29},{1,25},{2,31},{3,27},{4,28},{5,24},{6,30},{7,26},{8,21},{9,... | collective-permute-start | bytes 1244168 | tf_op jit(solution)/shard_map/ppermute | solution.py:162
  10.2 37.7 %collective-permute-start.5 = (bf16[72,2880]{1,0:T(8,128)(2,1)S(1)}, bf16[72,2880]{1,0:T(8,128)(2,1)S(1)}, u32[]{:S(2)}, u32[]{:S(2)}) collective-permute-start(bf16[72,2880]{1,0:T(8,128)(2,1)S(1)} %collective-permute-done.2.mine_in), channel_id=1, source_target_pairs={{0,2},{1,3},{2,0},{3,1},{4,6},{5,7},{6,4},{7,5},{8,10},{9,11},{10,... | collective-permute-start | bytes 1244168 | tf_op jit(solution)/shard_map/ppermute | solution.py:162
  11.4 36.8 %collective-permute-start.3 = (bf16[72,2880]{1,0:T(8,128)(2,1)S(1)}, bf16[72,2880]{1,0:T(8,128)(2,1)S(1)}, u32[]{:S(2)}, u32[]{:S(2)}) collective-permute-start(bf16[72,2880]{1,0:T(8,128)(2,1)S(1)} %collective-permute-done.2.mine_in), channel_id=1, source_target_pairs={{0,1},{1,0},{2,3},{3,2},{4,5},{5,4},{6,7},{7,6},{8,9},{9,8},{10,11... | collective-permute-start | bytes 1244168 | tf_op jit(solution)/shard_map/ppermute | solution.py:162
  21.2 27.8 %collective-permute-start.13 = (bf16[72,2880]{1,0:T(8,128)(2,1)S(1)}, bf16[72,2880]{1,0:T(8,128)(2,1)S(1)}, u32[]{:S(2)}, u32[]{:S(2)}) collective-permute-start(bf16[72,2880]{1,0:T(8,128)(2,1)S(1)} %collective-permute-done.10.mine_in), channel_id=1, source_target_pairs={{0,2},{1,3},{2,0},{3,1},{4,6},{5,7},{6,4},{7,5},{8,10},{9,11},{10,... | collective-permute-start | bytes 1244168 | tf_op jit(solution)/shard_map/ppermute | solution.py:162
  26.2 22.9 %collective-permute-start.11 = (bf16[72,2880]{1,0:T(8,128)(2,1)S(1)}, bf16[72,2880]{1,0:T(8,128)(2,1)S(1)}, u32[]{:S(2)}, u32[]{:S(2)}) collective-permute-start(bf16[72,2880]{1,0:T(8,128)(2,1)S(1)} %collective-permute-done.10.mine_in), channel_id=1, source_target_pairs={{0,1},{1,0},{2,3},{3,2},{4,5},{5,4},{6,7},{7,6},{8,9},{9,8},{10,11... | collective-permute-start | bytes 1244168 | tf_op jit(solution)/shard_map/ppermute | solution.py:162
  46.8 11.1 %collective-permute-start.21 = (bf16[72,2880]{1,0:T(8,128)(2,1)S(1)}, bf16[72,2880]{1,0:T(8,128)(2,1)S(1)}, u32[]{:S(2)}, u32[]{:S(2)}) collective-permute-start(bf16[72,2880]{1,0:T(8,128)(2,1)S(1)} %collective-permute-done.18.mine_in), channel_id=1, source_target_pairs={{0,2},{1,3},{2,0},{3,1},{4,6},{5,7},{6,4},{7,5},{8,10},{9,11},{10,... | collective-permute-start | bytes 1244168 | tf_op jit(solution)/shard_map/ppermute | solution.py:162
  48.0 18.9 %collective-permute-start.29 = (bf16[72,2880]{1,0:T(8,128)(2,1)S(1)}, bf16[72,2880]{1,0:T(8,128)(2,1)S(1)}, u32[]{:S(2)}, u32[]{:S(2)}) collective-permute-start(bf16[72,2880]{1,0:T(8,128)(2,1)S(1)} %collective-permute-done.26.mine_in), channel_id=1, source_target_pairs={{0,2},{1,3},{2,0},{3,1},{4,6},{5,7},{6,4},{7,5},{8,10},{9,11},{10,... | collective-permute-start | bytes 1244168 | tf_op jit(solution)/shard_map/ppermute | solution.py:162
  48.2 19.8 %collective-permute-start.6 = (bf16[72,2880]{1,0:T(8,128)(2,1)S(1)}, bf16[72,2880]{1,0:T(8,128)(2,1)S(1)}, u32[]{:S(2)}, u32[]{:S(2)}) collective-permute-start(bf16[72,2880]{1,0:T(8,128)(2,1)S(1)} %collective-permute-done.5.mine_in), channel_id=1, source_target_pairs={{0,1},{1,0},{2,3},{3,2},{4,5},{5,4},{6,7},{7,6},{8,9},{9,8},{10,11... | collective-permute-start | bytes 1244168 | tf_op jit(solution)/shard_map/ppermute | solution.py:162
  49.0 21.0 %collective-permute-start.19 = (bf16[72,2880]{1,0:T(8,128)(2,1)S(1)}, bf16[72,2880]{1,0:T(8,128)(2,1)S(1)}, u32[]{:S(2)}, u32[]{:S(2)}) collective-permute-start(bf16[72,2880]{1,0:T(8,128)(2,1)S(1)} %collective-permute-done.18.mine_in), channel_id=1, source_target_pairs={{0,1},{1,0},{2,3},{3,2},{4,5},{5,4},{6,7},{7,6},{8,9},{9,8},{10,11... | collective-permute-start | bytes 1244168 | tf_op jit(solution)/shard_map/ppermute | solution.py:162
  49.1 27.5 %collective-permute-start.27 = (bf16[72,2880]{1,0:T(8,128)(2,1)S(1)}, bf16[72,2880]{1,0:T(8,128)(2,1)S(1)}, u32[]{:S(2)}, u32[]{:S(2)}) collective-permute-start(bf16[72,2880]{1,0:T(8,128)(2,1)S(1)} %collective-permute-done.26.mine_in), channel_id=1, source_target_pairs={{0,1},{1,0},{2,3},{3,2},{4,5},{5,4},{6,7},{7,6},{8,9},{9,8},{10,11... | collective-permute-start | bytes 1244168 | tf_op jit(solution)/shard_map/ppermute | solution.py:162
  57.8 20.8 %collective-permute-start.14 = (bf16[72,2880]{1,0:T(8,128)(2,1)S(1)}, bf16[72,2880]{1,0:T(8,128)(2,1)S(1)}, u32[]{:S(2)}, u32[]{:S(2)}) collective-permute-start(bf16[72,2880]{1,0:T(8,128)(2,1)S(1)} %collective-permute-done.13.mine_in), channel_id=1, source_target_pairs={{0,1},{1,0},{2,3},{3,2},{4,5},{5,4},{6,7},{7,6},{8,9},{9,8},{10,11... | collective-permute-start | bytes 1244168 | tf_op jit(solution)/shard_map/ppermute | solution.py:162
  59.6 2.2 %copy-start.1 = (bf16[1,2880,720]{1,2,0:T(8,128)(2,1)S(1)}, bf16[1,2880,720]{1,2,0:T(8,128)(2,1)}, u32[]{:S(2)}) copy-start(bf16[1,2880,720]{1,2,0:T(8,128)(2,1)} %param.10) | copy-start | bytes 12441604
  61.8 6.2 %copy-start = (bf16[1,360,2880]{2,1,0:T(8,128)(2,1)S(1)}, bf16[1,360,2880]{2,1,0:T(8,128)(2,1)}, u32[]{:S(2)}) copy-start(bf16[1,360,2880]{2,1,0:T(8,128)(2,1)} %param.11) | copy-start | bytes 6220804
  66.9 14.3 %collective-permute-start.22 = (bf16[72,2880]{1,0:T(8,128)(2,1)S(1)}, bf16[72,2880]{1,0:T(8,128)(2,1)S(1)}, u32[]{:S(2)}, u32[]{:S(2)}) collective-permute-start(bf16[72,2880]{1,0:T(8,128)(2,1)S(1)} %collective-permute-done.21.mine_in), channel_id=1, source_target_pairs={{0,1},{1,0},{2,3},{3,2},{4,5},{5,4},{6,7},{7,6},{8,9},{9,8},{10,11... | collective-permute-start | bytes 1244168 | tf_op jit(solution)/shard_map/ppermute | solution.py:162
  68.0 15.5 %collective-permute-start.30 = (bf16[72,2880]{1,0:T(8,128)(2,1)S(1)}, bf16[72,2880]{1,0:T(8,128)(2,1)S(1)}, u32[]{:S(2)}, u32[]{:S(2)}) collective-permute-start(bf16[72,2880]{1,0:T(8,128)(2,1)S(1)} %collective-permute-done.29.mine_in), channel_id=1, source_target_pairs={{0,1},{1,0},{2,3},{3,2},{4,5},{5,4},{6,7},{7,6},{8,9},{9,8},{10,11... | collective-permute-start | bytes 1244168 | tf_op jit(solution)/shard_map/ppermute | solution.py:162
  70.0 16.1 %collective-permute-start.7 = (bf16[72,2880]{1,0:T(8,128)(2,1)S(1)}, bf16[72,2880]{1,0:T(8,128)(2,1)S(1)}, u32[]{:S(2)}, u32[]{:S(2)}) collective-permute-start(bf16[72,2880]{1,0:T(8,128)(2,1)S(1)} %get-tuple-element.37), channel_id=1, source_target_pairs={{0,1},{1,0},{2,3},{3,2},{4,5},{5,4},{6,7},{7,6},{8,9},{9,8},{10,11... | collective-permute-start | bytes 1244168 | tf_op jit(solution)/shard_map/ppermute | solution.py:162
  76.6 16.2 %collective-permute-start.4 = (bf16[72,2880]{1,0:T(8,128)(2,1)S(1)}, bf16[72,2880]{1,0:T(8,128)(2,1)S(1)}, u32[]{:S(2)}, u32[]{:S(2)}) collective-permute-start(bf16[72,2880]{1,0:T(8,128)(2,1)S(1)} %get-tuple-element.35), channel_id=1, source_target_pairs={{0,1},{1,0},{2,3},{3,2},{4,5},{5,4},{6,7},{7,6},{8,9},{9,8},{10,11... | collective-permute-start | bytes 1244168 | tf_op jit(solution)/shard_map/ppermute | solution.py:162
  78.7 25.4 %collective-permute-start.12 = (bf16[72,2880]{1,0:T(8,128)(2,1)S(1)}, bf16[72,2880]{1,0:T(8,128)(2,1)S(1)}, u32[]{:S(2)}, u32[]{:S(2)}) collective-permute-start(bf16[72,2880]{1,0:T(8,128)(2,1)S(1)} %get-tuple-element.40), channel_id=1, source_target_pairs={{0,1},{1,0},{2,3},{3,2},{4,5},{5,4},{6,7},{7,6},{8,9},{9,8},{10,11... | collective-permute-start | bytes 1244168 | tf_op jit(solution)/shard_map/ppermute | solution.py:162
  81.2 31.4 %collective-permute-start.20 = (bf16[72,2880]{1,0:T(8,128)(2,1)S(1)}, bf16[72,2880]{1,0:T(8,128)(2,1)S(1)}, u32[]{:S(2)}, u32[]{:S(2)}) collective-permute-start(bf16[72,2880]{1,0:T(8,128)(2,1)S(1)} %get-tuple-element.45), channel_id=1, source_target_pairs={{0,1},{1,0},{2,3},{3,2},{4,5},{5,4},{6,7},{7,6},{8,9},{9,8},{10,11... | collective-permute-start | bytes 1244168 | tf_op jit(solution)/shard_map/ppermute | solution.py:162
  83.5 37.5 %collective-permute-start.28 = (bf16[72,2880]{1,0:T(8,128)(2,1)S(1)}, bf16[72,2880]{1,0:T(8,128)(2,1)S(1)}, u32[]{:S(2)}, u32[]{:S(2)}) collective-permute-start(bf16[72,2880]{1,0:T(8,128)(2,1)S(1)} %get-tuple-element.50), channel_id=1, source_target_pairs={{0,1},{1,0},{2,3},{3,2},{4,5},{5,4},{6,7},{7,6},{8,9},{9,8},{10,11... | collective-permute-start | bytes 1244168 | tf_op jit(solution)/shard_map/ppermute | solution.py:162
  86.1 1.8 %collective-permute-start.15 = (bf16[72,2880]{1,0:T(8,128)(2,1)S(1)}, bf16[72,2880]{1,0:T(8,128)(2,1)S(1)}, u32[]{:S(2)}, u32[]{:S(2)}) collective-permute-start(bf16[72,2880]{1,0:T(8,128)(2,1)S(1)} %get-tuple-element.42), channel_id=1, source_target_pairs={{0,1},{1,0},{2,3},{3,2},{4,5},{5,4},{6,7},{7,6},{8,9},{9,8},{10,11... | collective-permute-start | bytes 1244168 | tf_op jit(solution)/shard_map/ppermute | solution.py:162
  87.9 1.8 %collective-permute-start.23 = (bf16[72,2880]{1,0:T(8,128)(2,1)S(1)}, bf16[72,2880]{1,0:T(8,128)(2,1)S(1)}, u32[]{:S(2)}, u32[]{:S(2)}) collective-permute-start(bf16[72,2880]{1,0:T(8,128)(2,1)S(1)} %get-tuple-element.47), channel_id=1, source_target_pairs={{0,1},{1,0},{2,3},{3,2},{4,5},{5,4},{6,7},{7,6},{8,9},{9,8},{10,11... | collective-permute-start | bytes 1244168 | tf_op jit(solution)/shard_map/ppermute | solution.py:162
  89.7 1.8 %collective-permute-start.31 = (bf16[72,2880]{1,0:T(8,128)(2,1)S(1)}, bf16[72,2880]{1,0:T(8,128)(2,1)S(1)}, u32[]{:S(2)}, u32[]{:S(2)}) collective-permute-start(bf16[72,2880]{1,0:T(8,128)(2,1)S(1)} %get-tuple-element.52), channel_id=1, source_target_pairs={{0,1},{1,0},{2,3},{3,2},{4,5},{5,4},{6,7},{7,6},{8,9},{9,8},{10,11... | collective-permute-start | bytes 1244168 | tf_op jit(solution)/shard_map/ppermute | solution.py:162
  89.9 40.9 %copy-start.4 = (bf16[2880,8]{0,1:T(8,128)(2,1)S(1)}, bf16[2880,8]{0,1:T(8,128)(2,1)}, u32[]{:S(2)}) copy-start(bf16[2880,8]{0,1:T(8,128)(2,1)} %param.9) | copy-start | bytes 138244
  89.9 40.9 %copy-start.6 = (s32[64,4]{0,1:T(4,128)S(1)}, s32[64,4]{0,1:T(4,128)}, u32[]{:S(2)}) copy-start(s32[64,4]{0,1:T(4,128)} %param.7) | copy-start | bytes 3076
  91.5 11.2 %collective-permute-start.8 = (bf16[72,2880]{1,0:T(8,128)(2,1)S(1)}, bf16[72,2880]{1,0:T(8,128)(2,1)S(1)}, u32[]{:S(2)}, u32[]{:S(2)}) collective-permute-start(bf16[72,2880]{1,0:T(8,128)(2,1)S(1)} %add_convert_fusion.7), channel_id=1, source_target_pairs={{0,2},{1,3},{2,0},{3,1},{4,6},{5,7},{6,4},{7,5},{8,10},{9,11},{10,... | collective-permute-start | bytes 1244168 | tf_op jit(solution)/shard_map/ppermute | solution.py:162
  92.8 19.0 %collective-permute-start.16 = (bf16[72,2880]{1,0:T(8,128)(2,1)S(1)}, bf16[72,2880]{1,0:T(8,128)(2,1)S(1)}, u32[]{:S(2)}, u32[]{:S(2)}) collective-permute-start(bf16[72,2880]{1,0:T(8,128)(2,1)S(1)} %add_convert_fusion.5), channel_id=1, source_target_pairs={{0,2},{1,3},{2,0},{3,1},{4,6},{5,7},{6,4},{7,5},{8,10},{9,11},{10,... | collective-permute-start | bytes 1244168 | tf_op jit(solution)/shard_map/ppermute | solution.py:162
  102.7 18.2 %collective-permute-start.24 = (bf16[72,2880]{1,0:T(8,128)(2,1)S(1)}, bf16[72,2880]{1,0:T(8,128)(2,1)S(1)}, u32[]{:S(2)}, u32[]{:S(2)}) collective-permute-start(bf16[72,2880]{1,0:T(8,128)(2,1)S(1)} %add_convert_fusion.3), channel_id=1, source_target_pairs={{0,2},{1,3},{2,0},{3,1},{4,6},{5,7},{6,4},{7,5},{8,10},{9,11},{10,... | collective-permute-start | bytes 1244168 | tf_op jit(solution)/shard_map/ppermute | solution.py:162
  104.0 58.7 %copy-start.3 = (bf16[64,2880]{1,0:T(8,128)(2,1)S(1)}, bf16[64,2880]{1,0:T(8,128)(2,1)}, u32[]{:S(2)}) copy-start(bf16[64,2880]{1,0:T(8,128)(2,1)} %own.1) | copy-start | bytes 1105924
  104.0 25.9 %collective-permute-start.32 = (bf16[72,2880]{1,0:T(8,128)(2,1)S(1)}, bf16[72,2880]{1,0:T(8,128)(2,1)S(1)}, u32[]{:S(2)}, u32[]{:S(2)}) collective-permute-start(bf16[72,2880]{1,0:T(8,128)(2,1)S(1)} %add_convert_fusion.1), channel_id=1, source_target_pairs={{0,2},{1,3},{2,0},{3,1},{4,6},{5,7},{6,4},{7,5},{8,10},{9,11},{10,... | collective-permute-start | bytes 1244168 | tf_op jit(solution)/shard_map/ppermute | solution.py:162
  111.7 20.1 %collective-permute-start.9 = (bf16[72,2880]{1,0:T(8,128)(2,1)S(1)}, bf16[72,2880]{1,0:T(8,128)(2,1)S(1)}, u32[]{:S(2)}, u32[]{:S(2)}) collective-permute-start(bf16[72,2880]{1,0:T(8,128)(2,1)S(1)} %add_convert_fusion.6), channel_id=1, source_target_pairs={{0,0},{1,4},{2,2},{3,6},{4,1},{5,5},{6,3},{7,7},{8,8},{9,12},{10,1... | collective-permute-start | bytes 1244168 | tf_op jit(solution)/shard_map/ppermute | solution.py:162
  112.6 19.3 %collective-permute-start.17 = (bf16[72,2880]{1,0:T(8,128)(2,1)S(1)}, bf16[72,2880]{1,0:T(8,128)(2,1)S(1)}, u32[]{:S(2)}, u32[]{:S(2)}) collective-permute-start(bf16[72,2880]{1,0:T(8,128)(2,1)S(1)} %add_convert_fusion.4), channel_id=1, source_target_pairs={{0,13},{1,9},{2,15},{3,11},{4,12},{5,8},{6,14},{7,10},{8,5},{9,1},... | collective-permute-start | bytes 1244168 | tf_op jit(solution)/shard_map/ppermute | solution.py:162
  121.0 26.2 %collective-permute-start.25 = (bf16[72,2880]{1,0:T(8,128)(2,1)S(1)}, bf16[72,2880]{1,0:T(8,128)(2,1)S(1)}, u32[]{:S(2)}, u32[]{:S(2)}) collective-permute-start(bf16[72,2880]{1,0:T(8,128)(2,1)S(1)} %add_convert_fusion.2), channel_id=1, source_target_pairs={{0,16},{1,20},{2,18},{3,22},{4,17},{5,21},{6,19},{7,23},{8,24},{9,... | collective-permute-start | bytes 1244168 | tf_op jit(solution)/shard_map/ppermute | solution.py:162
  130.1 27.9 %collective-permute-start.33 = (bf16[72,2880]{1,0:T(8,128)(2,1)S(1)}, bf16[72,2880]{1,0:T(8,128)(2,1)S(1)}, u32[]{:S(2)}, u32[]{:S(2)}) collective-permute-start(bf16[72,2880]{1,0:T(8,128)(2,1)S(1)} %add_convert_fusion), channel_id=1, source_target_pairs={{0,29},{1,25},{2,31},{3,27},{4,28},{5,24},{6,30},{7,26},{8,21},{9,... | collective-permute-start | bytes 1244168 | tf_op jit(solution)/shard_map/ppermute | solution.py:162
  159.0 3.7 %collective-permute-start.34 = (bf16[64,2880]{1,0:T(8,128)(2,1)S(1)}, bf16[64,2880]{1,0:T(8,128)(2,1)S(1)}, u32[]{:S(2)}, u32[]{:S(2)}) collective-permute-start(bf16[64,2880]{1,0:T(8,128)(2,1)S(1)} %get-tuple-element.54), channel_id=1, source_target_pairs={{0,1},{1,0},{2,3},{3,2},{4,5},{5,4},{6,7},{7,6},{8,9},{9,8},{10,11... | collective-permute-start | bytes 1105928 | tf_op jit(solution)/shard_map/ppermute | solution.py:162
